TPU v7x, 256 devices: a whole 4x4x8 slice. The times are simulated.
256 devices in a mesh: dp: 32 (over z, y_hi, core), tensor: 8 (over x, y_lo).
Axes of the slice: x: 4, y: 4 (y_hi: 2, y_lo: 2; y = y_hi * 2 + y_lo), z: 8, core: 2. Of those that a mesh axis runs over, the one named last changes fastest.
Arguments:
- tokens: bfloat16 [128, 576, 1024], P('dp', 'tensor'), may hold values from -150 to 150
- cotangent: bfloat16 [128, 576, 1024], P('dp', 'tensor'), may hold values from -6 to 6
- dispatch_weight: bfloat16 [1024, 64], replicated, may hold values from -3 to 3
- w_in: bfloat16 [64, 1024, 4096], P('dp', None, 'tensor'), may hold values from -0.1875 to 0.1875
- w_out: bfloat16 [64, 4096, 1024], P('dp', 'tensor'), may hold values from -0.09375 to 0.09375
Outputs:
- grad_tokens: bfloat16 [128, 576, 1024], P('dp', 'tensor')
- grad_router: float32 [1024, 64], replicated
- grad_w_in: bfloat16 [64, 1024, 4096], P('dp', None, 'tensor')
- grad_w_out: bfloat16 [64, 4096, 1024], P('dp', 'tensor')
All inputs are finite; a program needn't handle non-finite values.
Results may differ from a plain program's by a relative error of at most 0.0079.
Values may be sent and summed in bfloat16 or wider, within the bound.
No kernel may reach another device: no remote copies, remote signals or barrier semaphores. Data moves between devices by JAX's collectives and lax.ppermute only.
A program may use at most 64 MiB of HBM per device.

v0:
```python
import jax
import jax.numpy as jnp
from jax import lax
from jax.sharding import PartitionSpec as P


def split_up(x, dim, length):
    lengths = x.shape
    blocks = x.reshape(*lengths[:dim], length, lengths[dim] // length, *lengths[dim + 1 :])
    return jnp.moveaxis(blocks, dim, 0)


def summed_on_arrival(x, axis, dim):
    blocks = split_up(x, dim, lax.axis_size(axis))
    arrived = lax.all_to_all(blocks, axis, split_axis=0, concat_axis=0, tiled=True)
    return arrived.sum(axis=0)


def sent_to_all(x, axis):
    length = lax.axis_size(axis)
    return lax.all_to_all(jnp.broadcast_to(x[None], (length, *x.shape)), axis, 0, 0, tiled=True)


def laid_out(blocks, dim):
    lengths = list(blocks.shape[1:])
    lengths[dim] *= blocks.shape[0]
    return jnp.moveaxis(blocks, 0, dim).reshape(lengths)


def gathered_copies(x, axis, dim):
    blocks = sent_to_all(x, axis)
    return laid_out(blocks, dim)


def collected_together(x, axis):
    leaves = jax.tree.leaves(x)
    sequence = sorted(range(len(leaves)), key=lambda k: -leaves[k].size)
    width = (1, *leaves[sequence[0]].shape)[-1]
    lines = [
        jnp.pad(leaves[k].reshape(-1), (0, -leaves[k].size % width)).reshape(-1, width)
        for k in sequence
    ]
    both, at, found = (sent_to_all(jnp.concatenate(lines), axis), 0, {})
    for k, line in zip(sequence, lines):
        piece = both[:, at : at + len(line)].reshape(len(both), -1)
        found[k] = piece[:, : leaves[k].size].reshape(-1, *leaves[k].shape)
        at += len(line)
    numbers = iter(range(len(leaves)))
    return jax.tree.map(lambda _: found[next(numbers)], x)


def combined_pairwise(pieces, combine):
    while len(jax.tree.leaves(pieces)[0]) > 1:
        pieces = jax.vmap(combine)(
            *(jax.tree.map(lambda part: part[side::2], pieces) for side in (0, 1))
        )
    return jax.tree.map(lambda part: part[0], pieces)


def merged(x, axis, combine):
    pieces = collected_together(x, axis)
    return combined_pairwise(pieces, combine)


def over_copies(x, axis):
    return sent_to_all(x, axis).sum(axis=0)


def to_experts(partial_rows):
    shared_part = summed_on_arrival(partial_rows, "tensor", 2).astype(jnp.bfloat16)
    arrived = lax.all_to_all(shared_part, "dp", split_axis=1, concat_axis=0, tiled=True)
    result = gathered_copies(arrived, "tensor", 2)
    return result


def to_images(partial_rows):
    shared_part = summed_on_arrival(partial_rows, "tensor", 2).astype(jnp.bfloat16)
    arrived = lax.all_to_all(shared_part, "dp", split_axis=0, concat_axis=1, tiled=True)
    result = gathered_copies(arrived, "tensor", 2)
    return result


def join_stats(former, latter):
    biggest = jnp.maximum(former[0], latter[0])
    return (
        biggest,
        former[1] * jnp.exp(former[0] - biggest) + latter[1] * jnp.exp(latter[0] - biggest),
    )


def dispatch_softmax(logits):
    local_max = jnp.max(logits, axis=1)
    local_total = jnp.sum(jnp.exp(logits - local_max[:, None, :]), axis=1)
    global_max, totals = merged((local_max, local_total), "tensor", join_stats)
    exponent = jnp.exp(logits - global_max[:, None, :])
    return exponent / totals[:, None, :]


def on_device(tokens, cotangent, dispatch_weight, w_in, w_out):
    wide = jnp.float32
    logits = jnp.einsum("isd,de->ise", tokens, dispatch_weight, preferred_element_type=wide)
    dispatch = dispatch_softmax(logits)
    combine = jax.nn.softmax(logits, axis=2)
    dispatch_low = dispatch.astype(jnp.bfloat16)
    combine_low = combine.astype(jnp.bfloat16)
    slot_inputs = to_experts(
        jnp.einsum("ise,isd->ied", dispatch_low, tokens, preferred_element_type=wide)
    )
    pre_act = jnp.einsum("ied,edf->ief", slot_inputs, w_in, preferred_element_type=wide)
    hidden_act, gelu_back = jax.vjp(jax.nn.gelu, pre_act)
    hidden_low = hidden_act.astype(jnp.bfloat16)
    slot_outputs = to_images(
        jnp.einsum("ief,efd->ied", hidden_low, w_out, preferred_element_type=wide)
    )
    grad_combine = jnp.einsum("isd,ied->ise", cotangent, slot_outputs, preferred_element_type=wide)
    grad_slots_out = to_experts(
        jnp.einsum("ise,isd->ied", combine_low, cotangent, preferred_element_type=wide)
    )
    grad_hidden = jnp.einsum("ied,efd->ief", grad_slots_out, w_out, preferred_element_type=wide)
    grad_pre = gelu_back(grad_hidden)[0].astype(jnp.bfloat16)
    grad_w_out = jnp.einsum(
        "ief,ied->efd", hidden_low, grad_slots_out, preferred_element_type=wide
    ).astype(jnp.bfloat16)
    grad_w_in = jnp.einsum(
        "ied,ief->edf", slot_inputs, grad_pre, preferred_element_type=wide
    ).astype(jnp.bfloat16)
    grad_slots_in = to_images(
        jnp.einsum("ief,edf->ied", grad_pre, w_in, preferred_element_type=wide)
    )
    grad_dispatch = jnp.einsum("isd,ied->ise", tokens, grad_slots_in, preferred_element_type=wide)
    column_dot = over_copies(jnp.sum(grad_dispatch * dispatch, axis=1), "tensor")
    row_dot = jnp.sum(grad_combine * combine, axis=2, keepdims=True)
    grad_logits = (
        combine * (grad_combine - row_dot) + dispatch * (grad_dispatch - column_dot[:, None, :])
    ).astype(jnp.bfloat16)
    token_part = jnp.einsum(
        "ise,ied->isd", dispatch_low, grad_slots_in, preferred_element_type=wide
    )
    router_part = jnp.einsum(
        "ise,de->isd", grad_logits, dispatch_weight, preferred_element_type=wide
    )
    grad_tokens = (token_part + router_part).astype(jnp.bfloat16)
    local_router = jnp.einsum("isd,ise->de", tokens, grad_logits, preferred_element_type=wide)
    grad_router = lax.psum(local_router, ("dp", "tensor"))
    return (grad_tokens, grad_router, grad_w_in, grad_w_out)


def solution(mesh):
    return jax.shard_map(
        on_device,
        mesh=mesh,
        in_specs=(
            P("dp", "tensor", None),
            P("dp", "tensor", None),
            P(),
            P("dp", None, "tensor"),
            P("dp", "tensor", None),
        ),
        out_specs=(P("dp", "tensor", None), P(), P("dp", None, "tensor"), P("dp", "tensor", None)),
        check_vma=False,
    )
```

profile of v0, /device:TPU:1, one launch (start us, length us, event | category | flops | bytes accessed | tf_op | source)
XLA Modules:
  0.0 495.3 jit_solution(7292811887007530040)
XLA Ops:
  7.2 1.7 fusion.48
  9.2 10.7 %all_to_all.110 = f32[8,1,512]{2,1,0:T(1,128)S(1)} all-to-all(f32[8,1,512]{2,1,0:T(1,128)S(1)} %reshape.63), channel_id=1, replica_groups=mesh['dp'=32,'tensor'=8] {'tensor'}, dimensions={0} | all-to-all | bytes 32768 | tf_op jit(solution)/shard_map/all_to_all | solution.py:21
  21.2 1.4 convolution_bitcast_fusion.2
  23.7 4.2 all-to-all-start.4
  28.6 1.4 convolution_bitcast_fusion.3
  31.1 10.9 %all-to-all-done.4 = f32[8,4,64,128]{3,2,1,0:T(8,128)} async-done(((f32[8,4,64,128]{3,2,1,0:T(8,128)}), f32[8,4,64,128]{3,2,1,0:T(8,128)}, u32[]{:S(2)}, u32[]{:S(2)}) %all-to-all-start.4) | async-done | bytes 1048608 | tf_op jit(solution)/shard_map/all_to_all | solution.py:15
  42.0 3.9 all-to-all-start.1
  46.0 1.3 reduce_sum.84
  47.9 12.2 %all-to-all-done.1 = f32[8,4,64,128]{3,2,1,0:T(8,128)S(1)} async-done(((f32[8,4,64,128]{3,2,1,0:T(8,128)}), f32[8,4,64,128]{3,2,1,0:T(8,128)S(1)}, u32[]{:S(2)}, u32[]{:S(2)}) %all-to-all-start.1) | async-done | bytes 1048608 | tf_op jit(solution)/shard_map/all_to_all | solution.py:15
  60.1 13.4 %all-to-all-start.5 = ((bf16[4,64,128]{2,0,1:T(4,128)(2,1)}), bf16[4,64,128]{2,0,1:T(4,128)(2,1)S(1)}, u32[]{:S(2)}, u32[]{:S(2)}) async-start(bf16[4,64,128]{2,0,1:T(4,128)(2,1)} %copy.87), calls=%async_computation.5 | async-start | bytes 131072 | tf_op jit(solution)/shard_map/all_to_all | solution.py:71
  74.2 9.0 %all-to-all-done.5 = bf16[4,64,128]{2,0,1:T(4,128)(2,1)S(1)} async-done(((bf16[4,64,128]{2,0,1:T(4,128)(2,1)}), bf16[4,64,128]{2,0,1:T(4,128)(2,1)S(1)}, u32[]{:S(2)}, u32[]{:S(2)}) %all-to-all-start.5) | async-done | bytes 65568 | tf_op jit(solution)/shard_map/all_to_all | solution.py:71
  83.2 3.9 all-to-all-start.2
  87.2 9.8 %all-to-all-done.2 = bf16[4,64,128]{2,0,1:T(4,128)(2,1)S(1)} async-done(((bf16[4,64,128]{2,0,1:T(4,128)(2,1)}), bf16[4,64,128]{2,0,1:T(4,128)(2,1)S(1)}, u32[]{:S(2)}, u32[]{:S(2)}) %all-to-all-start.2) | async-done | bytes 65568 | tf_op jit(solution)/shard_map/all_to_all | solution.py:71
  98.0 3.5 all-to-all-start.6
  101.5 9.0 %all-to-all-done.6 = bf16[8,128,2,128]{3,1,2,0:T(8,128)(2,1)S(1)} async-done(((bf16[8,128,2,128]{3,1,2,0:T(8,128)(2,1)}), bf16[8,128,2,128]{3,1,2,0:T(8,128)(2,1)S(1)}, u32[]{:S(2)}, u32[]{:S(2)}) %all-to-all-start.6) | async-done | bytes 524320 | tf_op jit(solution)/shard_map/all_to_all | solution.py:21
  111.5 4.1 all-to-all-start.3
  116.1 8.2 %all-to-all-done.3 = bf16[8,128,2,128]{3,1,2,0:T(8,128)(2,1)} async-done(((bf16[8,128,2,128]{3,1,2,0:T(8,128)(2,1)}), bf16[8,128,2,128]{3,1,2,0:T(8,128)(2,1)}, u32[]{:S(2)}, u32[]{:S(2)}) %all-to-all-start.3) | async-done | bytes 524320 | tf_op jit(solution)/shard_map/all_to_all | solution.py:21
  124.2 2.8 fusion.15
  128.9 4.2 all-to-all-start.7
  133.1 2.2 convolution_bitcast_fusion
  136.4 11.1 %all-to-all-done.7 = f32[8,128,2,128]{3,1,2,0:T(8,128)} async-done(((f32[8,128,2,128]{3,1,2,0:T(8,128)}), f32[8,128,2,128]{3,1,2,0:T(8,128)}, u32[]{:S(2)}, u32[]{:S(2)}) %all-to-all-start.7) | async-done | bytes 1048608 | tf_op jit(solution)/shard_map/all_to_all | solution.py:15
  147.5 4.2 all-to-all-start.10
  151.8 1.9 reduce_sum.85
  153.7 1.5 copy.92
  155.2 10.5 %all-to-all-done.10 = f32[8,128,2,128]{3,1,2,0:T(8,128)} async-done(((f32[8,128,2,128]{3,1,2,0:T(8,128)}), f32[8,128,2,128]{3,1,2,0:T(8,128)}, u32[]{:S(2)}, u32[]{:S(2)}) %all-to-all-start.10) | async-done | bytes 1048608 | tf_op jit(solution)/shard_map/all_to_all | solution.py:15
  165.8 6.7 %all-to-all-start.8 = ((bf16[128,2,128]{2,1,0:T(2,128)(2,1)}), bf16[128,2,128]{2,1,0:T(2,128)(2,1)}, u32[]{:S(2)}, u32[]{:S(2)}) async-start(bf16[128,2,128]{2,1,0:T(2,128)(2,1)} %copy.92), calls=%async_computation.8 | async-start | bytes 131072 | tf_op jit(solution)/shard_map/all_to_all | solution.py:78
  172.4 1.9 reduce_sum.86
  174.4 1.5 copy.97
  175.9 6.5 %all-to-all-done.8 = bf16[128,2,128]{2,1,0:T(2,128)(2,1)} async-done(((bf16[128,2,128]{2,1,0:T(2,128)(2,1)}), bf16[128,2,128]{2,1,0:T(2,128)(2,1)}, u32[]{:S(2)}, u32[]{:S(2)}) %all-to-all-start.8) | async-done | bytes 65568 | tf_op jit(solution)/shard_map/all_to_all | solution.py:78
  182.4 4.5 all-to-all-start.11
  188.5 8.4 %all-to-all-done.11 = bf16[128,2,128]{2,1,0:T(2,128)(2,1)} async-done(((bf16[128,2,128]{2,1,0:T(2,128)(2,1)}), bf16[128,2,128]{2,1,0:T(2,128)(2,1)}, u32[]{:S(2)}, u32[]{:S(2)}) %all-to-all-start.11) | async-done | bytes 65568 | tf_op jit(solution)/shard_map/all_to_all | solution.py:78
  196.9 1.8 broadcast_in_dim.26
  198.7 4.1 all-to-all-start.9
  202.8 2.1 convolution_convert_fusion.1
  204.9 3.1 convolution_convert_fusion
  209.0 3.0 all-to-all-done.9
  212.9 4.1 all-to-all-start.12
  217.1 2.2 multiply_reduce_fusion.1
  219.9 1.5 fusion.19
  221.5 4.2 all-to-all-done.12
  225.7 3.7 all-to-all-start.13
  229.5 2.2 convolution_bitcast_fusion.8
  231.7 2.8 all-to-all-done.13
  234.5 1.2 reduce.1
  237.0 2.5 convolution_bitcast_fusion.6
  239.6 2.5 fusion.2
  242.1 244.7 %all-reduce.2.cloned.1.call-done = f32[1024,64]{0,1:T(8,128)} async-done(((f32[1024,64]{0,1:T(8,128)}), f32[1024,64]{0,1:T(8,128)}) %all-reduce.2.cloned.1.call-update) | async-done | bytes 262160 | tf_op jit(solution)/shard_map/psum | solution.py:144
  486.8 1.7 copy.154
  (48 shorter events, 16.7 us)
Async XLA Ops:
  7.2 108.4 %copy-start = (bf16[2,1024,512]{2,1,0:T(8,128)(2,1)S(1)}, bf16[2,1024,512]{2,1,0:T(8,128)(2,1)}, u32[]{:S(2)}) copy-start(bf16[2,1024,512]{2,1,0:T(8,128)(2,1)} %param.8) | copy-start | bytes 6291460
  21.2 198.8 %copy-start.2 = (f32[4,64]{1,0:T(4,128)}, f32[4,64]{1,0:T(4,128)S(1)}, u32[]{:S(2)}) copy-start(f32[4,64]{1,0:T(4,128)S(1)} %get-tuple-element.10) | copy-start | bytes 3076
  21.2 198.8 %copy-start.3 = (f32[4,64]{1,0:T(4,128)}, f32[4,64]{1,0:T(4,128)S(1)}, u32[]{:S(2)}) copy-start(f32[4,64]{1,0:T(4,128)S(1)} %get-tuple-element.11) | copy-start | bytes 3076
  23.7 18.3 %all-to-all-start.4 = ((f32[8,4,64,128]{3,2,1,0:T(8,128)}), f32[8,4,64,128]{3,2,1,0:T(8,128)}, u32[]{:S(2)}, u32[]{:S(2)}) async-start(f32[8,4,64,128]{3,2,1,0:T(8,128)} %bitcast.137), calls=%async_computation.4 | async-start | bytes 2097152 | tf_op jit(solution)/shard_map/all_to_all | solution.py:15
  28.6 13.4 %copy-start.4 = (f32[4,72]{1,0:T(4,128)}, f32[4,72]{1,0:T(4,128)S(1)}, u32[]{:S(2)}) copy-start(f32[4,72]{1,0:T(4,128)S(1)} %get-tuple-element.14) | copy-start | bytes 3460
  42.0 18.1 %all-to-all-start.1 = ((f32[8,4,64,128]{3,2,1,0:T(8,128)}), f32[8,4,64,128]{3,2,1,0:T(8,128)S(1)}, u32[]{:S(2)}, u32[]{:S(2)}) async-start(f32[8,4,64,128]{3,2,1,0:T(8,128)} %bitcast.140), calls=%async_computation.1 | async-start | bytes 2097152 | tf_op jit(solution)/shard_map/all_to_all | solution.py:15
  60.1 23.1 %all-to-all-start.5 = ((bf16[4,64,128]{2,0,1:T(4,128)(2,1)}), bf16[4,64,128]{2,0,1:T(4,128)(2,1)S(1)}, u32[]{:S(2)}, u32[]{:S(2)}) async-start(bf16[4,64,128]{2,0,1:T(4,128)(2,1)} %copy.87), calls=%async_computation.5 | async-start | bytes 131072 | tf_op jit(solution)/shard_map/all_to_all | solution.py:71
  83.2 13.8 %all-to-all-start.2 = ((bf16[4,64,128]{2,0,1:T(4,128)(2,1)}), bf16[4,64,128]{2,0,1:T(4,128)(2,1)S(1)}, u32[]{:S(2)}, u32[]{:S(2)}) async-start(bf16[4,64,128]{2,0,1:T(4,128)(2,1)} %copy.82), calls=%async_computation.2 | async-start | bytes 131072 | tf_op jit(solution)/shard_map/all_to_all | solution.py:71
  98.0 12.6 %all-to-all-start.6 = ((bf16[8,128,2,128]{3,1,2,0:T(8,128)(2,1)}), bf16[8,128,2,128]{3,1,2,0:T(8,128)(2,1)S(1)}, u32[]{:S(2)}, u32[]{:S(2)}) async-start(bf16[8,128,2,128]{3,1,2,0:T(8,128)(2,1)} %broadcast_in_dim.24), calls=%async_computation.6 | async-start | bytes 1048576 | tf_op jit(solution)/shard_map/all_to_all | solution.py:21
  111.5 12.8 %all-to-all-start.3 = ((bf16[8,128,2,128]{3,1,2,0:T(8,128)(2,1)}), bf16[8,128,2,128]{3,1,2,0:T(8,128)(2,1)}, u32[]{:S(2)}, u32[]{:S(2)}) async-start(bf16[8,128,2,128]{3,1,2,0:T(8,128)(2,1)} %broadcast_in_dim.22), calls=%async_computation.3 | async-start | bytes 1048576 | tf_op jit(solution)/shard_map/all_to_all | solution.py:21
  128.9 18.6 %all-to-all-start.7 = ((f32[8,128,2,128]{3,1,2,0:T(8,128)}), f32[8,128,2,128]{3,1,2,0:T(8,128)}, u32[]{:S(2)}, u32[]{:S(2)}) async-start(f32[8,128,2,128]{3,1,2,0:T(8,128)} %bitcast.142), calls=%async_computation.7 | async-start | bytes 2097152 | tf_op jit(solution)/shard_map/all_to_all | solution.py:15
  147.5 18.2 %all-to-all-start.10 = ((f32[8,128,2,128]{3,1,2,0:T(8,128)}), f32[8,128,2,128]{3,1,2,0:T(8,128)}, u32[]{:S(2)}, u32[]{:S(2)}) async-start(f32[8,128,2,128]{3,1,2,0:T(8,128)} %bitcast.141), calls=%async_computation.10 | async-start | bytes 2097152 | tf_op jit(solution)/shard_map/all_to_all | solution.py:15
  165.8 16.6 %all-to-all-start.8 = ((bf16[128,2,128]{2,1,0:T(2,128)(2,1)}), bf16[128,2,128]{2,1,0:T(2,128)(2,1)}, u32[]{:S(2)}, u32[]{:S(2)}) async-start(bf16[128,2,128]{2,1,0:T(2,128)(2,1)} %copy.92), calls=%async_computation.8 | async-start | bytes 131072 | tf_op jit(solution)/shard_map/all_to_all | solution.py:78
  182.4 14.5 %all-to-all-start.11 = ((bf16[128,2,128]{2,1,0:T(2,128)(2,1)}), bf16[128,2,128]{2,1,0:T(2,128)(2,1)}, u32[]{:S(2)}, u32[]{:S(2)}) async-start(bf16[128,2,128]{2,1,0:T(2,128)(2,1)} %copy.97), calls=%async_computation.11 | async-start | bytes 131072 | tf_op jit(solution)/shard_map/all_to_all | solution.py:78
  198.7 13.3 %all-to-all-start.9 = ((bf16[8,4,64,128]{3,2,1,0:T(8,128)(2,1)}), bf16[8,4,64,128]{3,2,1,0:T(8,128)(2,1)}, u32[]{:S(2)}, u32[]{:S(2)}) async-start(bf16[8,4,64,128]{3,2,1,0:T(8,128)(2,1)} %broadcast_in_dim.26), calls=%async_computation.9 | async-start | bytes 1048576 | tf_op jit(solution)/shard_map/all_to_all | solution.py:21
  212.9 12.8 %all-to-all-start.12 = ((bf16[8,4,64,128]{3,2,1,0:T(8,128)(2,1)}), bf16[8,4,64,128]{3,2,1,0:T(8,128)(2,1)}, u32[]{:S(2)}, u32[]{:S(2)}) async-start(bf16[8,4,64,128]{3,2,1,0:T(8,128)(2,1)} %broadcast_in_dim.28), calls=%async_computation.12 | async-start | bytes 1048576 | tf_op jit(solution)/shard_map/all_to_all | solution.py:21
  221.5 18.1 %copy-start.1 = (bf16[1024,64]{0,1:T(8,128)(2,1)S(1)}, bf16[1024,64]{0,1:T(8,128)(2,1)}, u32[]{:S(2)}) copy-start(bf16[1024,64]{0,1:T(8,128)(2,1)} %param.7) | copy-start | bytes 393220
  225.7 8.8 %all-to-all-start.13 = ((f32[8,1,256]{2,1,0:T(1,128)}), f32[8,1,256]{2,1,0:T(1,128)S(1)}, u32[]{:S(2)}, u32[]{:S(2)}) async-start(f32[8,1,256]{2,1,0:T(1,128)} %reshape.65), calls=%async_computation.13 | async-start | bytes 16384 | tf_op jit(solution)/shard_map/all_to_all | solution.py:21
  229.4 257.3 %all-reduce.2.cloned.1.call-start = ((), (), s32[]{:S(2)}) async-start(), calls=%async_computation.14 | async-start | bytes 524288 | tf_op jit(solution)/shard_map/psum | solution.py:144
Sparse Core Ops, SparseCore 0:
  239.7 247.0 all-reduce.1
where the time goes:
time: 498 us; the launch traced here: 495 us
  waiting for transfers between devices  350 us (70%)
  starting transfers between devices  64.8 us (13%)
  matrix products  26.7 us (5%)
  local copies, waits for them, and re-layouts  19.7 us (4%)
  between operations  14.3 us (3%)
  blocking collectives  10.7 us (2%)
  other arithmetic  8.52 us (2%)
    psum x1, waiting for transfers between devices, on_device(): grad_router = lax.psum(local_router, ('dp', 'tensor'))  245 us
    all_to_all x4, waiting for transfers between devices, summed_on_arrival(): lax.all_to_all(blocks, axis, split_axis=0, concat_axis=0, tiled=True)  44.7 us
    all_to_all x5, waiting for transfers between devices, sent_to_all(): lax.all_to_all(jnp.broadcast_to(x[None], (length, *x.shape)), axis, 0, 0,...  27.3 us
    all_to_all x5, starting transfers between devices, sent_to_all(): lax.all_to_all(jnp.broadcast_to(x[None], (length, *x.shape)), axis, 0, 0,...  19.7 us
    all_to_all x2, waiting for transfers between devices, to_experts(): lax.all_to_all(shared_part, 'dp', split_axis=1, concat_axis=0, tiled=True)  18.9 us
    all_to_all x2, starting transfers between devices, to_experts(): lax.all_to_all(shared_part, 'dp', split_axis=1, concat_axis=0, tiled=True)  17.3 us
    all_to_all x4, starting transfers between devices, summed_on_arrival(): lax.all_to_all(blocks, axis, split_axis=0, concat_axis=0, tiled=True)  16.6 us
    all_to_all x2, waiting for transfers between devices, to_images(): lax.all_to_all(shared_part, 'dp', split_axis=0, concat_axis=1, tiled=True)  14.9 us
  transfers between devices with their start and end apart: 14, of which 14 were waited for; matrix products, arithmetic and copies ran while one was open for 7% of the time, Pallas kernels for 0%

commit v1 on v0

v1 whole, which is shorter than its diff:
```python
import jax
import jax.numpy as jnp
from jax import lax
from jax.sharding import PartitionSpec as P

NARROW = jnp.bfloat16
WIDE = jnp.float32


def exchanged(blocks, axis):
    return lax.all_to_all(blocks, axis, split_axis=0, concat_axis=0, tiled=True)


def pieces(x, count):
    found = []
    for _ in range(count):
        piece = lax.reduce_precision(x, exponent_bits=8, mantissa_bits=7)
        found.append(piece.astype(NARROW))
        x = x - piece
    return found


def with_extra_rows(blocks, rows):
    extra = jnp.stack(rows + [jnp.zeros_like(rows[0])] * (8 - len(rows)))
    extra = jnp.broadcast_to(extra[None], (blocks.shape[0], *extra.shape))
    return jnp.concatenate([blocks, extra], axis=1)


def feature_blocks(x, count):
    rows, width = x.shape
    return jnp.moveaxis(x.reshape(rows, count, width // count), 1, 0)


def joined_features(blocks):
    count, rows, width = blocks.shape
    return jnp.moveaxis(blocks, 0, 1).reshape(rows, count * width)


def on_device(tokens, cotangent, dispatch_weight, w_in, w_out):
    images, seq, width = tokens.shape
    slots = dispatch_weight.shape[1]
    parts = lax.axis_size("tensor")
    groups = lax.axis_size("dp")
    own = slots // groups
    rows = slots * images
    block = width // parts

    logits = jnp.einsum("isd,de->eis", tokens, dispatch_weight, preferred_element_type=WIDE)
    high, low = pieces(jnp.max(logits, axis=2), 2)
    local_top = high.astype(WIDE) + low.astype(WIDE)
    weight = jnp.exp(logits - local_top[:, :, None])
    local_total = jnp.sum(weight, axis=2)
    combine = jax.nn.softmax(logits, axis=0)
    partial_in = jnp.einsum("eis,isd->eid", weight.astype(NARROW), tokens, preferred_element_type=WIDE)
    partial_back = jnp.einsum(
        "eis,isd->eid", combine.astype(NARROW), cotangent, preferred_element_type=WIDE
    )
    sent = jnp.concatenate(
        [
            feature_blocks(partial_in.reshape(rows, width), parts),
            feature_blocks(partial_back.reshape(rows, width), parts),
        ],
        axis=2,
    ).astype(NARROW)
    stats = [high.reshape(rows), low.reshape(rows), *pieces(local_total.reshape(rows), 2)]
    arrived = exchanged(with_extra_rows(sent, stats), "tensor")

    seen = arrived[:, rows : rows + 4, :].astype(WIDE)
    tops = seen[:, 0] + seen[:, 1]
    top = jnp.max(tops, axis=0)
    factor = jnp.exp(tops - top)
    total = jnp.sum(factor * (seen[:, 2] + seen[:, 3]), axis=0)
    factor = factor / total
    body = arrived[:, :rows].astype(WIDE)
    slot_part = jnp.sum(body[:, :, :block] * factor[:, :, None], axis=0)
    back_part = jnp.sum(body[:, :, block:], axis=0)
    both = jnp.concatenate([slot_part, back_part], axis=1).astype(NARROW)
    arrived = exchanged(both.reshape(groups, own * images, 2 * block), "dp")
    ordered = jnp.moveaxis(arrived.reshape(groups, own, images, 2 * block), 1, 0).reshape(
        rows, 2 * block
    )
    arrived = exchanged(jnp.broadcast_to(ordered[None], (parts, *ordered.shape)), "tensor")
    total_images = groups * images
    slot_inputs = joined_features(arrived[:, :, :block]).reshape(own, total_images, width)
    grad_slots_out = joined_features(arrived[:, :, block:]).reshape(own, total_images, width)

    pre_act = jnp.einsum("eid,edf->eif", slot_inputs, w_in, preferred_element_type=WIDE)
    hidden_act, gelu_back = jax.vjp(jax.nn.gelu, pre_act)
    hidden_low = hidden_act.astype(NARROW)
    slot_outputs = jnp.einsum("eif,efd->eid", hidden_low, w_out, preferred_element_type=WIDE)
    grad_hidden = jnp.einsum("eid,efd->eif", grad_slots_out, w_out, preferred_element_type=WIDE)
    grad_pre = gelu_back(grad_hidden)[0].astype(NARROW)
    grad_slots_in = jnp.einsum("eif,edf->eid", grad_pre, w_in, preferred_element_type=WIDE)
    sent = jnp.concatenate(
        [
            feature_blocks(slot_outputs.reshape(rows, width), parts),
            feature_blocks(grad_slots_in.reshape(rows, width), parts),
        ],
        axis=2,
    ).astype(NARROW)
    arrived = exchanged(sent, "tensor")
    both = jnp.sum(arrived.astype(WIDE), axis=0).astype(NARROW)
    both = jnp.moveaxis(both.reshape(own, groups, images, 2 * block), 0, 1)
    grad_w_out = jnp.einsum(
        "eif,eid->efd", hidden_low, grad_slots_out, preferred_element_type=WIDE
    ).astype(NARROW)
    grad_w_in = jnp.einsum(
        "eid,eif->edf", slot_inputs, grad_pre, preferred_element_type=WIDE
    ).astype(NARROW)
    arrived = exchanged(both.reshape(groups, own * images, 2 * block), "dp").reshape(rows, 2 * block)
    dot_part = jnp.sum(slot_part * arrived[:, block:].astype(WIDE), axis=1)
    sent = jnp.broadcast_to(arrived[None], (parts, *arrived.shape))
    arrived = exchanged(with_extra_rows(sent, pieces(dot_part, 3)), "tensor")
    column_dot = jnp.sum(arrived[:, rows : rows + 3].astype(WIDE), axis=(0, 1))
    slot_outputs = joined_features(arrived[:, :rows, :block]).reshape(slots, images, width)
    grad_slots_in = joined_features(arrived[:, :rows, block:]).reshape(slots, images, width)

    dispatch = jnp.exp(logits - top.reshape(slots, images, 1)) / total.reshape(slots, images, 1)
    grad_combine = jnp.einsum("isd,eid->eis", cotangent, slot_outputs, preferred_element_type=WIDE)
    grad_dispatch = jnp.einsum("isd,eid->eis", tokens, grad_slots_in, preferred_element_type=WIDE)
    row_dot = jnp.sum(grad_combine * combine, axis=0, keepdims=True)
    grad_logits = (
        combine * (grad_combine - row_dot)
        + dispatch * (grad_dispatch - column_dot.reshape(slots, images, 1))
    ).astype(NARROW)
    local_router = jnp.einsum("eis,isd->ed", grad_logits, tokens, preferred_element_type=WIDE)
    ranks = groups * parts
    piece = slots * width // ranks
    arrived = exchanged(local_router.reshape(ranks, piece // 128, 128), ("dp", "tensor"))
    owned = jnp.sum(arrived, axis=0)
    arrived = exchanged(jnp.broadcast_to(owned[None], (ranks, *owned.shape)), ("dp", "tensor"))
    grad_router = arrived.reshape(slots, width).T
    token_part = jnp.einsum(
        "eis,eid->isd", dispatch.astype(NARROW), grad_slots_in, preferred_element_type=WIDE
    )
    router_part = jnp.einsum(
        "eis,de->isd", grad_logits, dispatch_weight, preferred_element_type=WIDE
    )
    grad_tokens = (token_part + router_part).astype(NARROW)
    return (grad_tokens, grad_router, grad_w_in, grad_w_out)


def solution(mesh):
    return jax.shard_map(
        on_device,
        mesh=mesh,
        in_specs=(
            P("dp", "tensor", None),
            P("dp", "tensor", None),
            P(),
            P("dp", None, "tensor"),
            P("dp", "tensor", None),
        ),
        out_specs=(P("dp", "tensor", None), P(), P("dp", None, "tensor"), P("dp", "tensor", None)),
        check_vma=False,
    )
```

time: 498 us -> 206 us (0.41)
  waiting for transfers between devices: 350 us -> 38.7 us
  blocking collectives: 10.7 us -> 94.9 us
  starting transfers between devices: 64.8 us -> 17.1 us
  between operations: 14.3 us -> 1.05 us
    psum x1 -> x0, waiting for transfers between devices: 245 us -> none  [on_device(): grad_router = lax.psum(local_router, ('dp', 'tensor'))]
    all_to_all x1 -> x5, blocking collectives: 10.7 us -> 94.9 us  [exchanged(): return lax.all_to_all(blocks, axis, split_axis=0, concat_axis=0, tiled=True)]
    all_to_all x13 -> x3, waiting for transfers between devices: 106 us -> 38.7 us  [exchanged(): return lax.all_to_all(blocks, axis, split_axis=0, concat_axis=0, tiled=True)]
    all_to_all x13 -> x3, starting transfers between devices: 64.8 us -> 17.1 us  [exchanged(): return lax.all_to_all(blocks, axis, split_axis=0, concat_axis=0, tiled=True)]
    transpose x0 -> x10, local copies, waits for them, and re-layouts: none -> 9.14 us  [the longest x6 8.2 us: joined_features(): return jnp.moveaxis(blocks, 0, 1).reshape(rows, count * width)]
    another operation x0 -> x12, local copies, waits for them, and re-layouts: none -> 6.62 us  [the longest x1 2.03 us: on_device(): joined_features(arrived[:, :rows, :block]).reshape(slots, images, width)]
  transfers between devices with their start and end apart: 14 -> 3, of which waited for: 14 -> 3; matrix products, arithmetic and copies ran while one was open for 7% -> 5% of each run, Pallas kernels for 0% -> 0%
where the time goes in v1:
time: 206 us; the launch traced here: 205 us
  blocking collectives  94.9 us (46%)
  waiting for transfers between devices  38.7 us (19%)
  matrix products  24.8 us (12%)
  local copies, waits for them, and re-layouts  22.9 us (11%)
  starting transfers between devices  17.1 us (8%)
  other arithmetic  5.92 us (3%)
    all_to_all x5, blocking collectives, exchanged(): return lax.all_to_all(blocks, axis, split_axis=0, concat_axis=0, tiled=True)  94.9 us
    all_to_all x3, waiting for transfers between devices, exchanged(): return lax.all_to_all(blocks, axis, split_axis=0, concat_axis=0, tiled=True)  38.7 us
    all_to_all x3, starting transfers between devices, exchanged(): return lax.all_to_all(blocks, axis, split_axis=0, concat_axis=0, tiled=True)  17.1 us
    transpose x6, local copies, waits for them, and re-layouts, joined_features(): return jnp.moveaxis(blocks, 0, 1).reshape(rows, count * width)  8.2 us
  transfers between devices with their start and end apart: 3, of which 3 were waited for; matrix products, arithmetic and copies ran while one was open for 5% of the time, Pallas kernels for 0%

profile of v1, /device:TPU:1, one launch (start us, length us, event | category | flops | bytes accessed | tf_op | source)
XLA Modules:
  0.0 205.3 jit_solution(6385429041890323102)
XLA Ops:
  0.6 1.8 fusion.53
  2.9 1.4 fusion.3
  4.6 0.4 copy.40
  5.1 1.0 reshape_reshape.28
  6.0 1.4 fusion.4
  7.4 0.4 copy.41
  8.1 1.2 pad_maximum_fusion
  9.5 21.0 %all_to_all.40 = bf16[8,264,256]{2,1,0:T(8,128)(2,1)S(1)} all-to-all(bf16[8,264,256]{2,1,0:T(8,128)(2,1)S(1)} %copy.44), channel_id=1, replica_groups=mesh['dp'=32,'tensor'=8] {'tensor'}, dimensions={0} | all-to-all | bytes 2162688 | tf_op jit(solution)/shard_map/all_to_all | solution.py:11
  30.8 0.3 slice_reduce_fusion
  31.1 23.4 %all_to_all.41 = bf16[32,8,256]{2,1,0:T(8,128)(2,1)S(1)} all-to-all(bf16[32,8,256]{2,1,0:T(8,128)(2,1)S(1)} %pad_maximum_fusion.3), channel_id=1, replica_groups=mesh['dp'=32,'tensor'=8] {'dp'}, dimensions={0} | all-to-all | bytes 262144 | tf_op jit(solution)/shard_map/all_to_all | solution.py:11
  54.8 17.5 %all_to_all.42 = bf16[8,256,256]{2,1,0:T(8,128)(2,1)S(1)} all-to-all(bf16[8,256,256]{2,1,0:T(8,128)(2,1)S(1)} %broadcast_in_dim.16), channel_id=1, replica_groups=mesh['dp'=32,'tensor'=8] {'tensor'}, dimensions={0} | all-to-all | bytes 2097152 | tf_op jit(solution)/shard_map/all_to_all | solution.py:11
  72.4 1.1 slice_bitcast_fusion.2
  73.4 0.3 copy.53
  73.8 0.2 reshape_reshape.32
  74.0 1.4 copy.51
  75.4 1.0 reshape_reshape.30
  76.4 2.5 %fusion.55 = f32[2,128,512]{2,1,0:T(8,128)S(1)} fusion(bf16[2,128,1024]{2,1,0:T(8,128)(2,1)S(1)} %reshape_reshape.32, bf16[2,512,1024]{2,1,0:T(8,128)(2,1)} %param.9), kind=kOutput, calls=%fused_computation.102 | convolution fusion | flops 268435456 | bytes 3145728 | tf_op jit(solution)/shard_map/eid,efd->eif/dot_general | solution.py:91
  78.9 0.7 fusion.20
  79.7 0.8 convolution_convert_fusion.4
  80.7 0.9 copy-done.1
  81.6 0.6 convolution_convert_fusion.5
  82.5 17.1 %all_to_all.43 = bf16[8,256,256]{2,1,0:T(8,128)(2,1)} all-to-all(bf16[8,256,256]{2,1,0:T(8,128)(2,1)S(1)} %pad_maximum_fusion.2), channel_id=1, replica_groups=mesh['dp'=32,'tensor'=8] {'tensor'}, dimensions={0} | all-to-all | bytes 2097152 | tf_op jit(solution)/shard_map/all_to_all | solution.py:11
  99.6 1.4 reduce_sum.100
  101.1 15.9 %all_to_all.44 = bf16[32,8,256]{2,1,0:T(8,128)(2,1)S(1)} all-to-all(bf16[32,8,256]{2,1,0:T(8,128)(2,1)S(1)} %copy.56), channel_id=1, replica_groups=mesh['dp'=32,'tensor'=8] {'dp'}, dimensions={0} | all-to-all | bytes 262144 | tf_op jit(solution)/shard_map/all_to_all | solution.py:11
  117.3 1.1 pad_maximum_fusion.1
  118.3 4.4 %all-to-all-start.5 = ((bf16[8,264,256]{2,1,0:T(8,128)(2,1)}), bf16[8,264,256]{2,1,0:T(8,128)(2,1)}, u32[]{:S(2)}, u32[]{:S(2)}) async-start(bf16[8,264,256]{2,1,0:T(8,128)(2,1)} %pad_maximum_fusion.1), calls=%async_computation.5 | async-start | bytes 2162688 | tf_op jit(solution)/shard_map/all_to_all | solution.py:11
  123.1 17.0 %all-to-all-done.5 = bf16[8,264,256]{2,1,0:T(8,128)(2,1)} async-done(((bf16[8,264,256]{2,1,0:T(8,128)(2,1)}), bf16[8,264,256]{2,1,0:T(8,128)(2,1)}, u32[]{:S(2)}, u32[]{:S(2)}) %all-to-all-start.5) | async-done | bytes 1081376 | tf_op jit(solution)/shard_map/all_to_all | solution.py:11
  140.1 2.1 %slice_bitcast_fusion = (bf16[256,8,128]{2,0,1:T(8,128)(2,1)S(1)}, bf16[256,8,128]{2,0,1:T(8,128)(2,1)}) fusion(bf16[8,264,256]{2,1,0:T(8,128)(2,1)} %all-to-all-done.5), kind=kLoop, calls=%fused_computation.39 | loop fusion | bytes 2097152 | tf_op jit(solution)/shard_map/transpose | solution.py:36
  142.2 1.1 copy.59
  143.4 2.0 reshape_reshape.35
  145.4 2.2 %convolution_bitcast_fusion.2 = f32[64,4,72]{2,0,1:T(8,128)} fusion(bf16[4,72,1024]{2,1,0:T(8,128)(2,1)} %param.6, bf16[64,4,1024]{2,1,0:T(4,128)(2,1)} %reshape_reshape.35), kind=kOutput, calls=%fused_computation.15 | convolution fusion | flops 37748736 | bytes 1187840 | tf_op jit(solution)/shard_map/isd,eid->eis/dot_general | solution.py:119
  147.6 0.8 convert_reduce_fusion
  148.6 2.2 %copy.57 = bf16[256,8,128]{2,1,0:T(8,128)(2,1)} copy(bf16[256,8,128]{2,0,1:T(8,128)(2,1)} %get-tuple-element.7) | data formatting | bytes 1048576 | tf_op jit(solution)/shard_map/transpose | solution.py:36
  150.8 2.0 reshape_reshape.34
  152.7 2.0 fusion.11
  154.8 2.0 convolution_bitcast_fusion
  156.8 1.9 reshape.195
  158.7 5.9 %all-to-all-start.6 = ((f32[256,2,128]{2,1,0:T(2,128)}), f32[256,2,128]{2,1,0:T(2,128)S(1)}, u32[]{:S(2)}, u32[]{:S(2)}) async-start(f32[256,2,128]{2,1,0:T(2,128)} %reshape.195), calls=%async_computation.6 | async-start | bytes 524288 | tf_op jit(solution)/shard_map/all_to_all | solution.py:11
  164.7 3.2 %convolution_convert_fusion.1 = bf16[2,1024,512]{2,1,0:T(8,128)(2,1)} fusion(bf16[2,128,1024]{2,1,0:T(8,128)(2,1)} %reshape_reshape.30, bf16[2,128,512]{2,1,0:T(8,128)(2,1)} %copy-done.6), kind=kOutput, calls=%fused_computation.3 | convolution fusion | flops 269484032 | bytes 2883584 | tf_op jit(solution)/shard_map/eid,eif->edf/dot_general | solution.py:107
  167.9 2.1 %convolution_convert_fusion = bf16[2,512,1024]{2,1,0:T(8,128)(2,1)} fusion(bf16[2,128,1024]{2,1,0:T(8,128)(2,1)S(1)} %reshape_reshape.32, f32[2,128,512]{2,1,0:T(8,128)S(1)} %copy-done.5), kind=kOutput, calls=%fused_computation.2 | convolution fusion | flops 270663680 | bytes 3145728 | tf_op jit(solution)/shard_map/eif,eid->efd/dot_general | solution.py:104
  169.9 10.7 %all-to-all-done.6 = f32[256,2,128]{2,1,0:T(2,128)S(1)} async-done(((f32[256,2,128]{2,1,0:T(2,128)}), f32[256,2,128]{2,1,0:T(2,128)S(1)}, u32[]{:S(2)}, u32[]{:S(2)}) %all-to-all-start.6) | async-done | bytes 262176 | tf_op jit(solution)/shard_map/all_to_all | solution.py:11
  180.7 0.3 reduce_sum.105
  181.0 0.8 broadcast_in_dim.20
  181.7 6.8 %all-to-all-start.7 = ((f32[256,2,128]{2,1,0:T(2,128)}), f32[256,2,128]{2,1,0:T(2,128)}, u32[]{:S(2)}, u32[]{:S(2)}) async-start(f32[256,2,128]{2,1,0:T(2,128)} %broadcast_in_dim.20), calls=%async_computation.7 | async-start | bytes 524288 | tf_op jit(solution)/shard_map/all_to_all | solution.py:11
  188.5 1.6 fusion.23
  190.2 2.4 %fusion.2 = bf16[4,72,1024]{2,1,0:T(8,128)(2,1)} fusion(f32[4,72,1024]{2,1,0:T(8,128)S(1)} %fusion.23, f32[64,4,72]{2,0,1:T(8,128)} %fusion.11, f32[64,4,72]{2,0,1:T(8,128)} %convolution_bitcast_fusion.2, bf16[1024,64]{0,1:T(8,128)(2,1)} %param.7, f32[64,4,72]{2,0,1:T(8,128)} %copy-done.7, f32[4,72]{1,0:T(4,128)S(1)} %get-tuple-element.22), kind=kOutput, calls=%fused_computation.5 | convolution fusion | flops 38467936 | bytes 2122880 | tf_op jit(solution)/shard_map/eis,de->isd/dot_general | solution.py:136
  192.5 10.9 %all-to-all-done.7 = f32[256,2,128]{2,1,0:T(2,128)} async-done(((f32[256,2,128]{2,1,0:T(2,128)}), f32[256,2,128]{2,1,0:T(2,128)}, u32[]{:S(2)}, u32[]{:S(2)}) %all-to-all-start.7) | async-done | bytes 262176 | tf_op jit(solution)/shard_map/all_to_all | solution.py:11
  203.5 1.9 reshape.196
  (60 shorter events, 3.1 us)
Async XLA Ops:
  0.6 78.3 %copy-start = (bf16[2,1024,512]{2,1,0:T(8,128)(2,1)S(1)}, bf16[2,1024,512]{2,1,0:T(8,128)(2,1)}, u32[]{:S(2)}) copy-start(bf16[2,1024,512]{2,1,0:T(8,128)(2,1)} %param.8) | copy-start | bytes 6291460
  2.7 152.1 %copy-start.7 = (f32[64,4,72]{2,0,1:T(8,128)}, f32[64,4,72]{2,0,1:T(8,128)S(1)}, u32[]{:S(2)}) copy-start(f32[64,4,72]{2,0,1:T(8,128)S(1)} %get-tuple-element.23) | copy-start | bytes 221188
  76.4 2.5 %copy-start.3 = (bf16[2,128,1024]{2,1,0:T(8,128)(2,1)S(1)}, bf16[2,128,1024]{2,1,0:T(8,128)(2,1)}, u32[]{:S(2)}) copy-start(bf16[2,128,1024]{2,1,0:T(8,128)(2,1)} %reshape_reshape.30) | copy-start | bytes 1572868
  79.7 1.0 copy-start.6
  79.7 1.0 copy-start.4
  79.7 1.9 copy-start.1
  118.3 21.8 %all-to-all-start.5 = ((bf16[8,264,256]{2,1,0:T(8,128)(2,1)}), bf16[8,264,256]{2,1,0:T(8,128)(2,1)}, u32[]{:S(2)}, u32[]{:S(2)}) async-start(bf16[8,264,256]{2,1,0:T(8,128)(2,1)} %pad_maximum_fusion.1), calls=%async_computation.5 | async-start | bytes 2162688 | tf_op jit(solution)/shard_map/all_to_all | solution.py:11
  143.4 9.4 %copy-start.2 = (bf16[4,72,1024]{2,1,0:T(8,128)(2,1)S(1)}, bf16[4,72,1024]{2,1,0:T(8,128)(2,1)}, u32[]{:S(2)}) copy-start(bf16[4,72,1024]{2,1,0:T(8,128)(2,1)} %param.5) | copy-start | bytes 1769476
  156.8 11.0 %copy-start.5 = (f32[2,128,512]{2,1,0:T(8,128)S(1)}, f32[2,128,512]{2,1,0:T(8,128)}, u32[]{:S(2)}) copy-start(f32[2,128,512]{2,1,0:T(8,128)} %copy-done.4) | copy-start | bytes 1572868
  158.7 21.9 %all-to-all-start.6 = ((f32[256,2,128]{2,1,0:T(2,128)}), f32[256,2,128]{2,1,0:T(2,128)S(1)}, u32[]{:S(2)}, u32[]{:S(2)}) async-start(f32[256,2,128]{2,1,0:T(2,128)} %reshape.195), calls=%async_computation.6 | async-start | bytes 524288 | tf_op jit(solution)/shard_map/all_to_all | solution.py:11
  181.7 21.7 %all-to-all-start.7 = ((f32[256,2,128]{2,1,0:T(2,128)}), f32[256,2,128]{2,1,0:T(2,128)}, u32[]{:S(2)}, u32[]{:S(2)}) async-start(f32[256,2,128]{2,1,0:T(2,128)} %broadcast_in_dim.20), calls=%async_computation.7 | async-start | bytes 524288 | tf_op jit(solution)/shard_map/all_to_all | solution.py:11

commit v2 on v1

v2 whole, which is shorter than its diff:
```python
import functools

import jax
import jax.numpy as jnp
from jax import lax
from jax.experimental import pallas as pl
from jax.experimental.pallas import tpu as pltpu
from jax.sharding import Mesh
from jax.sharding import PartitionSpec as P

NARROW = jnp.bfloat16
WIDE = jnp.float32
LANES = 128
EXTRA = 8
FAR = -1e30
MIDDLE = NARROW
DP = ("z", "y_hi", "core")
PLANE = ("y_hi", "tensor")
COLUMN = ("z", "core")


def dot(a, b, over_a=1, over_b=0):
    return lax.dot_general(a, b, (((over_a,), (over_b,)), ((), ())), preferred_element_type=WIDE)


def iota(shape, dim):
    return lax.broadcasted_iota(jnp.int32, shape, dim)


def pieces(x, count):
    found = []
    for _ in range(count):
        piece = x.astype(NARROW).astype(WIDE)
        found.append(piece)
        x = x - piece
    return found


def as_lanes(columns, rows):
    lane = iota((rows, LANES), 1)
    found = jnp.zeros((rows, LANES), WIDE)
    for k, column in enumerate(columns):
        found = jnp.where(lane == k, column, found)
    return found


def as_columns(lines):
    return jnp.concatenate([lines, jnp.zeros((LANES - lines.shape[0], lines.shape[1]), WIDE)]).T


def combine_of(masked):
    weight = jnp.exp(masked - jnp.max(masked, axis=0, keepdims=True))
    return weight / jnp.sum(weight, axis=0, keepdims=True)


def slot_rows(
    images, seq, parts, token_src, back_src, router_src, sent, scores, spread, tokens, cotangent, router, arrivals
):
    copies_in = [
        pltpu.make_async_copy(source, target, arrivals.at[k])
        for k, (source, target) in enumerate(
            ((router_src, router), (token_src, tokens), (back_src, cotangent))
        )
    ]
    for copy in copies_in:
        copy.start()
    copies_in[0].wait()
    slots, width = router.shape
    rows, count, block = slots * images, images * seq, width // parts
    copies = (iota((rows, slots), 0) // images == iota((rows, slots), 1)).astype(NARROW)
    spread[...] = dot(copies, router[...]).astype(NARROW)
    own = iota((rows, count), 0) % images == iota((rows, count), 1) // seq
    copies_in[1].wait()
    masked = jnp.where(own, dot(spread[...], tokens[...], 1, 1), FAR)
    scores[...] = masked
    high, low = pieces(jnp.max(masked, axis=1, keepdims=True), 2)
    weight = jnp.exp(masked - (high + low))
    total = jnp.sum(weight, axis=1, keepdims=True)
    stats = as_lanes([high, low, *pieces(total, 2)], rows)
    lines = stats.T[:EXTRA].astype(NARROW)
    first, second = (piece.astype(NARROW) for piece in pieces(weight, 2))
    part_in = dot(first, tokens[...]) + dot(second, tokens[...])
    copies_in[2].wait()
    part_back = dot(combine_of(masked).astype(NARROW), cotangent[...])
    for t in range(parts):
        sent[t, :rows, :block] = part_in[:, t * block : (t + 1) * block].astype(NARROW)
        sent[t, :rows, block:] = part_back[:, t * block : (t + 1) * block].astype(NARROW)
        sent[t, rows:, :] = lines


def joined_rows(arrived, both, exact, stats):
    parts, rows, block = arrived.shape[0], both.shape[0], exact.shape[1]
    seen = [arrived[t, rows:, :].astype(WIDE) for t in range(parts)]
    tops = [line[0:1] + line[1:2] for line in seen]
    top = functools.reduce(jnp.maximum, tops)
    factors = [jnp.exp(own - top) for own in tops]
    total = sum(f * (line[2:3] + line[3:4]) for f, line in zip(factors, seen))
    scale = as_columns(jnp.concatenate([f / total for f in factors]))
    zeros = [jnp.zeros_like(top)] * (EXTRA - 2)
    stats[...] = as_columns(jnp.concatenate([top, total, *zeros]))
    slot_part = jnp.zeros((rows, block), WIDE)
    back_part = jnp.zeros((rows, block), WIDE)
    for t in range(parts):
        slot_part += arrived[t, :rows, :block].astype(WIDE) * scale[:, t : t + 1]
        back_part += arrived[t, :rows, block:].astype(WIDE)
    exact[...] = slot_part
    both[:, :block] = slot_part.astype(NARROW)
    both[:, block:] = back_part.astype(NARROW)


def by_expert(own, images, rows):
    row, column = iota((rows, rows), 0), iota((rows, rows), 1)
    each = rows // own
    source = (row % each) // images * (own * images) + row // each * images + row % images
    return (column == source).astype(NARROW)


def by_group(own, images, rows):
    row, column = iota((rows, rows), 0), iota((rows, rows), 1)
    each = rows // own
    target = (column % each) // images * (own * images) + column // each * images + column % images
    return (row == target).astype(NARROW)


def sorted_copies(own, images, arrived, sent):
    rows = arrived.shape[0]
    ordered = dot(by_expert(own, images, rows), arrived[...]).astype(NARROW)
    for t in range(sent.shape[0]):
        sent[t] = ordered


def halves(arrived, first, last):
    parts, block = arrived.shape[0], arrived.shape[2] // 2
    return tuple(
        jnp.concatenate([arrived[t, first:last, k * block : (k + 1) * block] for t in range(parts)], axis=1)
        for k in range(2)
    )


def experts(arrived, w_in, w_out, sent, acts):
    parts, rows, block = arrived.shape[0], arrived.shape[1], arrived.shape[2] // 2
    own, hidden_width = w_in.shape[0], w_in.shape[2]
    each = rows // own
    root = (2.0 / jnp.pi) ** 0.5
    for e in range(own):
        mine = slice(e * each, (e + 1) * each)
        slot_in, back = halves(arrived, e * each, (e + 1) * each)
        v = dot(slot_in, w_in[e])
        grad_hidden = dot(back, w_out[e], 1, 1)
        t = jnp.tanh(root * (v + 0.044715 * (v * v * v)))
        half = 0.5 * (1.0 + t)
        low = (v * half).astype(NARROW)
        slope = half + 0.5 * v * (1.0 - t * t) * (root * (1.0 + 3 * 0.044715 * (v * v)))
        grad_low = (slope * grad_hidden).astype(NARROW)
        acts[mine, :hidden_width] = low
        acts[mine, hidden_width:] = grad_low
        slot_out = dot(low, w_out[e])
        grad_in = dot(grad_low, w_in[e], 1, 1)
        for p in range(parts):
            sent[p, mine, :block] = slot_out[:, p * block : (p + 1) * block].astype(NARROW)
            sent[p, mine, block:] = grad_in[:, p * block : (p + 1) * block].astype(NARROW)


def weight_grads(arrived, acts, grad_in, grad_out):
    own, hidden_width = grad_in.shape[0], grad_in.shape[2]
    each = arrived.shape[1] // own
    for e in range(own):
        mine = slice(e * each, (e + 1) * each)
        slot_in, back = halves(arrived, e * each, (e + 1) * each)
        grad_in[e] = dot(slot_in, acts[mine, hidden_width:], 0, 0).astype(NARROW)
        grad_out[e] = dot(acts[mine, :hidden_width], back, 0, 0).astype(NARROW)


def joined_results(own, images, arrived, both):
    rows = both.shape[0]
    total = arrived[0].astype(WIDE)
    for t in range(1, arrived.shape[0]):
        total += arrived[t].astype(WIDE)
    both[...] = dot(by_group(own, images, rows), total.astype(NARROW)).astype(NARROW)


def dotted_copies(arrived, exact, sent):
    rows, block = exact.shape
    column = jnp.sum(exact[...] * arrived[:, block:].astype(WIDE), axis=1, keepdims=True)
    lines = as_lanes(pieces(column, 3), rows).T[:EXTRA].astype(NARROW)
    for t in range(sent.shape[0]):
        sent[t, :rows, :] = arrived[...]
        sent[t, rows:, :] = lines


def softmax_grads(
    images, arrived, tokens, cotangent, scores, stats, left, router
):
    parts, rows = arrived.shape[0], scores.shape[0]
    slots = rows // images
    slot_out, grad_in = halves(arrived, 0, rows)
    lines = arrived[0, rows:, :].astype(WIDE)
    for t in range(1, parts):
        lines += arrived[t, rows:, :].astype(WIDE)
    column_dot = jnp.sum(as_columns(lines)[:, :EXTRA], axis=1, keepdims=True)
    masked = scores[...]
    dispatch = jnp.exp(masked - stats[:, 0:1]) / stats[:, 1:2]
    combine = combine_of(masked)
    grad_combine = dot(slot_out, cotangent[...], 1, 1)
    grad_dispatch = dot(grad_in, tokens[...], 1, 1)
    row_dot = jnp.sum(grad_combine * combine, axis=0, keepdims=True)
    grad_logits = (
        combine * (grad_combine - row_dot) + dispatch * (grad_dispatch - column_dot)
    ).astype(NARROW)
    merge = (iota((slots, rows), 1) // images == iota((slots, rows), 0)).astype(NARROW)
    by_slot = dot(dot(merge, grad_logits).astype(NARROW), tokens[...])
    count, high, wide = router.shape
    across = by_slot.shape[1] // wide
    for k in range(count):
        down, right = k // across * high, k % across * wide
        router[k] = by_slot[down : down + high, right : right + wide].astype(router.dtype)
    left[:rows, :] = dispatch.astype(NARROW)
    left[rows:, :] = grad_logits


def token_grads(arrived, left, spread, grad_tokens):
    _, grad_in = halves(arrived, 0, spread.shape[0])
    right = jnp.concatenate([grad_in, spread[...]])
    grad_tokens[...] = dot(left[...], right, 0, 0).astype(NARROW)


def summed_copies(arrived, sent):
    total = arrived[0].astype(WIDE)
    for t in range(1, arrived.shape[0]):
        total += arrived[t].astype(WIDE)
    for t in range(sent.shape[0]):
        sent[t] = total.astype(sent.dtype)


def placed(arrived, router):
    count, high, wide = arrived.shape
    across = router.shape[1] // wide
    for k in range(count):
        down, right = k // across * high, k % across * wide
        router[down : down + high, right : right + wide] = arrived[k].astype(router.dtype)


def local(body, outs, flops, *args, limit=12, space=pltpu.VMEM, scratch=()):
    held = pl.BlockSpec(memory_space=pltpu.VMEM)
    moved = sum(a.size * a.dtype.itemsize for a in (*args, *outs))
    return pl.pallas_call(
        body,
        out_shape=outs,
        in_specs=[pl.BlockSpec(memory_space=space)] * len(args),
        scratch_shapes=scratch,
        out_specs=tuple([held] * len(outs)),
        cost_estimate=pl.CostEstimate(flops=flops, bytes_accessed=moved, transcendentals=0),
        compiler_params=pltpu.CompilerParams(vmem_limit_bytes=limit << 20),
    )(*args)


def shaped(shape, dtype=NARROW):
    return jax.ShapeDtypeStruct(shape, dtype)


def exchanged(blocks, axis):
    return lax.all_to_all(blocks, axis, split_axis=0, concat_axis=0, tiled=True)


def on_device(tokens, cotangent, dispatch_weight, w_in, w_out):
    images, seq, width = tokens.shape
    slots = dispatch_weight.shape[1]
    parts, groups = lax.axis_size("tensor"), lax.axis_size(DP)
    own, hidden_width = slots // groups, w_in.shape[2]
    rows, block, count = slots * images, width // parts, images * seq
    tokens, cotangent = tokens.reshape(count, width), cotangent.reshape(count, width)
    pair = 2 * block

    sent, scores, spread = local(
        functools.partial(slot_rows, images, seq, parts),
        (
            shaped((parts, rows + EXTRA, pair)),
            shaped((rows, count), WIDE),
            shaped((rows, width)),
        ),
        6 * rows * count * width,
        tokens,
        cotangent,
        dispatch_weight.T,
        limit=56,
        space=pltpu.HBM,
        scratch=(
            pltpu.VMEM(tokens.shape, NARROW),
            pltpu.VMEM(tokens.shape, NARROW),
            pltpu.VMEM((slots, width), NARROW),
            pltpu.SemaphoreType.DMA((3,)),
        ),
    )
    arrived = exchanged(sent, "tensor")
    both, exact, stats = local(
        joined_rows,
        (shaped((rows, pair)), shaped((rows, block), WIDE), shaped((rows, LANES), WIDE)),
        4 * rows * width,
        arrived,
    )
    arrived = exchanged(both.reshape(groups, own * images, pair), DP).reshape(rows, pair)
    (sent,) = local(
        functools.partial(sorted_copies, own, images),
        (shaped((parts, rows, pair)),),
        2 * rows * rows * pair,
        arrived,
    )
    arrived = exchanged(sent, "tensor")
    sent, acts = local(
        experts,
        (
            shaped((parts, rows, pair)),
            shaped((rows, 2 * hidden_width)),
        ),
        8 * rows * width * hidden_width,
        arrived,
        w_in,
        w_out,
    )
    back = exchanged(sent, "tensor")
    grad_w_in, grad_w_out = local(
        weight_grads,
        (shaped(w_in.shape), shaped(w_out.shape)),
        4 * rows * width * hidden_width,
        arrived,
        acts,
    )
    back, grad_w_in, grad_w_out = lax.optimization_barrier((back, grad_w_in, grad_w_out))
    (both,) = local(
        functools.partial(joined_results, own, images),
        (shaped((rows, pair)),),
        2 * rows * rows * pair,
        back,
    )
    arrived = exchanged(both.reshape(groups, own * images, pair), DP).reshape(rows, pair)
    (sent,) = local(
        dotted_copies, (shaped((parts, rows + EXTRA, pair)),), 4 * rows * width, arrived, exact
    )
    arrived = exchanged(sent, "tensor")
    plane = lax.axis_size(PLANE)
    across = width // LANES
    high = slots * across // plane
    left, router = local(
        functools.partial(softmax_grads, images),
        (shaped((2 * rows, count)), shaped((plane, high, LANES), MIDDLE)),
        4 * rows * count * width,
        arrived,
        tokens,
        cotangent,
        scores,
        stats,
    )
    (grad_tokens,) = local(
        token_grads,
        (shaped((count, width)),),
        4 * rows * count * width,
        arrived,
        left,
        spread,
    )
    column = lax.axis_size(COLUMN)
    (router,) = local(
        summed_copies,
        (shaped((column, high, LANES), MIDDLE),),
        slots * width,
        exchanged(router, PLANE),
    )
    (router,) = local(
        summed_copies,
        (shaped((plane, high, LANES), WIDE),),
        slots * width,
        exchanged(router, COLUMN),
    )
    (router,) = local(
        placed, (shaped((slots, width), WIDE),), slots * width, exchanged(router, PLANE)
    )
    grad_router = router.T
    return (grad_tokens.reshape(images, seq, width), grad_router, grad_w_in, grad_w_out)


def solution(mesh):
    depth = mesh.devices.shape[0] // 4
    fine = Mesh(
        mesh.devices.reshape(depth, 2, 2, mesh.devices.shape[1]), ("z", "y_hi", "core", "tensor")
    )
    return jax.shard_map(
        on_device,
        mesh=fine,
        in_specs=(
            P(DP, "tensor", None),
            P(DP, "tensor", None),
            P(),
            P(DP, None, "tensor"),
            P(DP, "tensor", None),
        ),
        out_specs=(P(DP, "tensor", None), P(), P(DP, None, "tensor"), P(DP, "tensor", None)),
        check_vma=False,
    )
```

time: 206 us -> 162 us (0.79)
  matrix products: 24.8 us -> 0 us
  blocking collectives: 94.9 us -> 119 us
  local copies, waits for them, and re-layouts: 22.9 us -> 0.03 us
  waiting for transfers between devices: 38.7 us -> 18.9 us
  Pallas kernels: 0 us -> 15.3 us
  starting transfers between devices: 17.1 us -> 7.09 us
  other arithmetic: 5.92 us -> 0 us
    dot_general x14 -> x0, matrix products: 24.8 us -> none  [the longest x1 3.18 us: on_device(): jnp.einsum('eid,eif->edf', slot_inputs, grad_pre, preferred_element_type=...]
    all_to_all x5 -> x7, blocking collectives: 94.9 us -> 119 us  [exchanged(): return lax.all_to_all(blocks, axis, split_axis=0, concat_axis=0, tiled=True)]
    all_to_all x3 -> x2, waiting for transfers between devices: 38.7 us -> 18.9 us  [exchanged(): return lax.all_to_all(blocks, axis, split_axis=0, concat_axis=0, tiled=True)]
    pallas_call x0 -> x12, Pallas kernels: none -> 15.3 us  [local(): pl.pallas_call(body, out_shape=outs, in_specs=[pl.BlockSpec(memory_space=...]
    all_to_all x3 -> x2, starting transfers between devices: 17.1 us -> 7.09 us  [exchanged(): return lax.all_to_all(blocks, axis, split_axis=0, concat_axis=0, tiled=True)]
    transpose x10 -> x0, local copies, waits for them, and re-layouts: 9.14 us -> none  [the longest x6 8.2 us: joined_features(): return jnp.moveaxis(blocks, 0, 1).reshape(rows, count * width)]
    another operation x12 -> x0, local copies, waits for them, and re-layouts: 6.62 us -> none  [the longest x1 2.03 us: on_device(): joined_features(arrived[:, :rows, :block]).reshape(slots, images, width)]
    reshape x5 -> x0, local copies, waits for them, and re-layouts: 4 us -> none  [the longest x1 1.92 us: on_device(): local_router.reshape(ranks, piece // 128, 128)]
  transfers between devices with their start and end apart: 3 -> 2, of which waited for: 3 -> 2; matrix products, arithmetic and copies ran while one was open for 5% -> 0% of each run, Pallas kernels for 0% -> 3%
where the time goes in v2:
time: 162 us; the launch traced here: 161 us
  blocking collectives  119 us (73%)
  waiting for transfers between devices  18.9 us (12%)
  Pallas kernels  15.3 us (9%)
  starting transfers between devices  7.09 us (4%)
    all_to_all x7, blocking collectives, exchanged(): return lax.all_to_all(blocks, axis, split_axis=0, concat_axis=0, tiled=True)  119 us
    all_to_all x2, waiting for transfers between devices, exchanged(): return lax.all_to_all(blocks, axis, split_axis=0, concat_axis=0, tiled=True)  18.9 us
    pallas_call x12, Pallas kernels, local(): pl.pallas_call(body, out_shape=outs, in_specs=[pl.BlockSpec(memory_space=...  15.3 us
    all_to_all x2, starting transfers between devices, exchanged(): return lax.all_to_all(blocks, axis, split_axis=0, concat_axis=0, tiled=True)  7.09 us
  transfers between devices with their start and end apart: 2, of which 2 were waited for; matrix products, arithmetic and copies ran while one was open for 0% of the time, Pallas kernels for 3%

profile of v2, /device:TPU:1, one launch (start us, length us, event | category | flops | bytes accessed | tf_op | source)
XLA Modules:
  0.0 161.5 jit_solution(3462541778329381824)
XLA Ops:
  0.6 3.9 %shard_map.84 = (bf16[8,264,256]{2,1,0:T(8,128)(2,1)}, f32[256,288]{1,0:T(8,128)}, bf16[256,1024]{1,0:T(8,128)(2,1)}) custom-call(bf16[288,1024]{1,0:T(8,128)(2,1)} %bitcast.9, bf16[288,1024]{1,0:T(8,128)(2,1)} %bitcast.11, bf16[64,1024]{1,0:T(8,128)(2,1)} %bitcast.19), custom_call_target="tpu_custom_call" | custom-call | flops 452984832 | bytes 3211264 | tf_op jit(solution)/shard_map/pallas_call | solution.py:246
  4.5 21.2 %all_to_all.45.arrived = bf16[8,264,256]{2,1,0:T(8,128)(2,1)S(1)} all-to-all(bf16[8,264,256]{2,1,0:T(8,128)(2,1)} %get-tuple-element.19), channel_id=1, replica_groups=mesh['z'=8,'y_hi'=2,'core'=2,'tensor'=8] {'tensor'}, dimensions={0} | all-to-all | bytes 2162688 | tf_op jit(solution)/shard_map/all_to_all | solution.py:262
  25.7 0.0 copy-start
  25.7 0.0 copy-start.1
  25.7 0.6 shard_map.85
  26.3 23.6 %all_to_all.46 = bf16[32,8,256]{2,1,0:T(8,128)(2,1)S(1)} all-to-all(bf16[32,8,256]{2,1,0:T(8,128)(2,1)S(1)} %bitcast.16), channel_id=1, replica_groups=mesh['z'=8,'y_hi'=2,'core'=2,'tensor'=8] {'z','y_hi','core'}, dimensions={0} | all-to-all | bytes 262144 | tf_op jit(solution)/shard_map/all_to_all | solution.py:262
  49.9 0.2 shard_map.86
  50.1 17.5 %all_to_all.47.arrived = bf16[8,256,256]{2,1,0:T(8,128)(2,1)S(1)} all-to-all(bf16[8,256,256]{2,1,0:T(8,128)(2,1)S(1)} %shard_map.86), channel_id=1, replica_groups=mesh['z'=8,'y_hi'=2,'core'=2,'tensor'=8] {'tensor'}, dimensions={0} | all-to-all | bytes 2097152 | tf_op jit(solution)/shard_map/all_to_all | solution.py:262
  67.6 0.0 copy-done
  67.6 0.0 copy-done.1
  67.6 3.2 %shard_map.87 = (bf16[8,256,256]{2,1,0:T(8,128)(2,1)}, bf16[256,1024]{1,0:T(8,128)(2,1)S(1)}) custom-call(bf16[8,256,256]{2,1,0:T(8,128)(2,1)S(1)} %all_to_all.47.arrived, bf16[2,1024,512]{2,1,0:T(8,128)(2,1)S(1)} %copy-done, bf16[2,512,1024]{2,1,0:T(8,128)(2,1)S(1)} %copy-done.1), custom_call_target="tpu_custom_call" | custom-call | flops 1073741824 | bytes 6815744 | tf_op jit(solution)/shard_map/pallas_call | solution.py:246
  70.8 3.6 %all-to-all-start.3 = ((bf16[8,256,256]{2,1,0:T(8,128)(2,1)}), bf16[8,256,256]{2,1,0:T(8,128)(2,1)S(1)}, u32[]{:S(2)}, u32[]{:S(2)}) async-start(bf16[8,256,256]{2,1,0:T(8,128)(2,1)} %get-tuple-element.21), calls=%async_computation.3 | async-start | bytes 2097152 | tf_op jit(solution)/shard_map/all_to_all | solution.py:262
  74.4 3.0 %shard_map.88 = (bf16[2,1024,512]{2,1,0:T(8,128)(2,1)}, bf16[2,512,1024]{2,1,0:T(8,128)(2,1)}) custom-call(bf16[8,256,256]{2,1,0:T(8,128)(2,1)S(1)} %all_to_all.47.arrived, bf16[256,1024]{1,0:T(8,128)(2,1)S(1)} %get-tuple-element.22.acts), custom_call_target="tpu_custom_call" | custom-call | flops 536870912 | bytes 5767168 | tf_op jit(solution)/shard_map/pallas_call | solution.py:246
  77.4 11.9 %all-to-all-done.3.arrived = bf16[8,256,256]{2,1,0:T(8,128)(2,1)S(1)} async-done(((bf16[8,256,256]{2,1,0:T(8,128)(2,1)}), bf16[8,256,256]{2,1,0:T(8,128)(2,1)S(1)}, u32[]{:S(2)}, u32[]{:S(2)}) %all-to-all-start.3) | async-done | bytes 1048608 | tf_op jit(solution)/shard_map/all_to_all | solution.py:262
  89.3 0.3 shard_map.89
  89.6 0.0 copy-start.2
  89.6 0.0 copy-start.3
  89.6 0.0 copy-start.5
  89.6 15.4 %all_to_all.48 = bf16[32,8,256]{2,1,0:T(8,128)(2,1)S(1)} all-to-all(bf16[32,8,256]{2,1,0:T(8,128)(2,1)S(1)} %bitcast.14), channel_id=1, replica_groups=mesh['z'=8,'y_hi'=2,'core'=2,'tensor'=8] {'z','y_hi','core'}, dimensions={0} | all-to-all | bytes 262144 | tf_op jit(solution)/shard_map/all_to_all | solution.py:262
  105.0 0.2 shard_map.90
  105.1 18.0 %all_to_all.49.arrived = bf16[8,264,256]{2,1,0:T(8,128)(2,1)S(1)} all-to-all(bf16[8,264,256]{2,1,0:T(8,128)(2,1)S(1)} %shard_map.90), channel_id=1, replica_groups=mesh['z'=8,'y_hi'=2,'core'=2,'tensor'=8] {'tensor'}, dimensions={0} | all-to-all | bytes 2162688 | tf_op jit(solution)/shard_map/all_to_all | solution.py:262
  123.2 0.0 copy-done.2
  123.2 0.0 copy-done.3
  123.2 0.0 copy-done.5
  123.2 0.0 copy-start.4
  123.2 1.2 shard_map.91
  124.4 9.3 %all_to_all.50.arrived = bf16[16,32,128]{2,1,0:T(8,128)(2,1)S(1)} all-to-all(bf16[16,32,128]{2,1,0:T(8,128)(2,1)S(1)} %get-tuple-element.31), channel_id=1, replica_groups=mesh['z'=8,'y_hi'=2,'core'=2,'tensor'=8] {'y_hi','tensor'}, dimensions={0} | all-to-all | bytes 262144 | tf_op jit(solution)/shard_map/all_to_all | solution.py:262
  133.7 14.4 %all_to_all.51.arrived = bf16[16,32,128]{2,1,0:T(8,128)(2,1)S(1)} all-to-all(bf16[16,32,128]{2,1,0:T(8,128)(2,1)S(1)} %shard_map.93), channel_id=1, replica_groups=mesh['z'=8,'y_hi'=2,'core'=2,'tensor'=8] {'z','core'}, dimensions={0} | all-to-all | bytes 262144 | tf_op jit(solution)/shard_map/all_to_all | solution.py:262
  148.1 0.7 shard_map.94
  148.9 3.5 %all-to-all-start.8 = ((f32[16,32,128]{2,1,0:T(8,128)}), f32[16,32,128]{2,1,0:T(8,128)S(1)}, u32[]{:S(2)}, u32[]{:S(2)}) async-start(f32[16,32,128]{2,1,0:T(8,128)} %shard_map.94), calls=%async_computation.8 | async-start | bytes 524288 | tf_op jit(solution)/shard_map/all_to_all | solution.py:262
  152.4 0.0 copy-done.4
  152.4 1.3 shard_map.92
  153.8 7.0 %all-to-all-done.8.arrived = f32[16,32,128]{2,1,0:T(8,128)S(1)} async-done(((f32[16,32,128]{2,1,0:T(8,128)}), f32[16,32,128]{2,1,0:T(8,128)S(1)}, u32[]{:S(2)}, u32[]{:S(2)}) %all-to-all-start.8) | async-done | bytes 262176 | tf_op jit(solution)/shard_map/all_to_all | solution.py:262
  160.7 0.7 shard_map.95
  (1 shorter events, 0.0 us)
Async XLA Ops:
  25.7 41.9 %copy-start = (bf16[2,1024,512]{2,1,0:T(8,128)(2,1)S(1)}, bf16[2,1024,512]{2,1,0:T(8,128)(2,1)}, u32[]{:S(2)}) copy-start(bf16[2,1024,512]{2,1,0:T(8,128)(2,1)} %w_in.1) | copy-start | bytes 6291460
  25.7 41.9 %copy-start.1 = (bf16[2,512,1024]{2,1,0:T(8,128)(2,1)S(1)}, bf16[2,512,1024]{2,1,0:T(8,128)(2,1)}, u32[]{:S(2)}) copy-start(bf16[2,512,1024]{2,1,0:T(8,128)(2,1)} %w_out.1) | copy-start | bytes 6291460
  70.8 18.5 %all-to-all-start.3 = ((bf16[8,256,256]{2,1,0:T(8,128)(2,1)}), bf16[8,256,256]{2,1,0:T(8,128)(2,1)S(1)}, u32[]{:S(2)}, u32[]{:S(2)}) async-start(bf16[8,256,256]{2,1,0:T(8,128)(2,1)} %get-tuple-element.21), calls=%async_computation.3 | async-start | bytes 2097152 | tf_op jit(solution)/shard_map/all_to_all | solution.py:262
  89.6 33.6 %copy-start.2 = (bf16[4,72,1024]{2,1,0:T(8,128)(2,1)S(1)}, bf16[4,72,1024]{2,1,0:T(8,128)(2,1)}, u32[]{:S(2)}) copy-start(bf16[4,72,1024]{2,1,0:T(8,128)(2,1)} %param.5) | copy-start | bytes 1769476
  89.6 33.6 %copy-start.3 = (bf16[4,72,1024]{2,1,0:T(8,128)(2,1)S(1)}, bf16[4,72,1024]{2,1,0:T(8,128)(2,1)}, u32[]{:S(2)}) copy-start(bf16[4,72,1024]{2,1,0:T(8,128)(2,1)} %param.6) | copy-start | bytes 1769476
  89.6 33.6 %copy-start.5 = (f32[256,288]{1,0:T(8,128)S(1)}, f32[256,288]{1,0:T(8,128)}, u32[]{:S(2)}) copy-start(f32[256,288]{1,0:T(8,128)} %get-tuple-element.27.scores) | copy-start | bytes 884740
  123.2 29.2 %copy-start.4 = (bf16[256,1024]{1,0:T(8,128)(2,1)S(1)}, bf16[256,1024]{1,0:T(8,128)(2,1)}, u32[]{:S(2)}) copy-start(bf16[256,1024]{1,0:T(8,128)(2,1)} %get-tuple-element.30.spread) | copy-start | bytes 1572868
  148.9 11.8 %all-to-all-start.8 = ((f32[16,32,128]{2,1,0:T(8,128)}), f32[16,32,128]{2,1,0:T(8,128)S(1)}, u32[]{:S(2)}, u32[]{:S(2)}) async-start(f32[16,32,128]{2,1,0:T(8,128)} %shard_map.94), calls=%async_computation.8 | async-start | bytes 524288 | tf_op jit(solution)/shard_map/all_to_all | solution.py:262

commit v3 on v2

v3 whole, which is shorter than its diff:
```python
import functools

import jax
import jax.numpy as jnp
from jax import lax
from jax.experimental import pallas as pl
from jax.experimental.pallas import tpu as pltpu
from jax.sharding import Mesh
from jax.sharding import PartitionSpec as P

NARROW = jnp.bfloat16
WIDE = jnp.float32
LANES = 128
EXTRA = 8
DP = ("z", "y_hi", "core")
TENSOR = ("x", "y_lo")
PLANE = ("y_hi", "x", "y_lo")
COLUMN = ("z", "core")


def dot(a, b, over_a=1, over_b=0):
    return lax.dot_general(a, b, (((over_a,), (over_b,)), ((), ())), preferred_element_type=WIDE)


def iota(shape, dim):
    return lax.broadcasted_iota(jnp.int32, shape, dim)


def pieces(x, count):
    found = []
    for _ in range(count):
        piece = x.astype(NARROW).astype(WIDE)
        found.append(piece)
        x = x - piece
    return found


def as_lanes(columns):
    rows = columns[0].shape[0]
    lane = iota((rows, LANES), 1)
    found = jnp.zeros((rows, LANES), WIDE)
    for k, column in enumerate(columns):
        found = jnp.where(lane == k, column, found)
    return found


def as_lines(columns, width):
    square = as_lanes(columns)
    square = jnp.concatenate([square, jnp.zeros((LANES - square.shape[0], LANES), WIDE)])
    lines = square.T[:EXTRA]
    return jnp.concatenate([lines, jnp.zeros((EXTRA, width - LANES), WIDE)], axis=1)


def as_columns(lines, rows):
    lines = lines[:, :LANES]
    return jnp.concatenate([lines, jnp.zeros((LANES - EXTRA, LANES), WIDE)]).T[:rows]


def selection(size, source):
    return (iota((size, size), 1) == source(iota((size, size), 0))).astype(NARROW)


def turned(size, outer, inner, unit):
    def source(row):
        a = row // unit % outer
        b = row // (unit * outer) % inner
        rest = row // (unit * outer * inner)
        return ((rest * outer + a) * inner + b) * unit + row % unit

    return selection(size, source)


def combine_of(scores):
    weight = jnp.exp(scores - jnp.max(scores, axis=0, keepdims=True))
    return weight / jnp.sum(weight, axis=0, keepdims=True)


def image_tokens(gathered):
    seq = gathered.shape[1] // 2
    return tuple(
        jnp.concatenate([gathered[k, f * seq : (f + 1) * seq, :] for k in range(gathered.shape[0])])
        for f in range(2)
    )


def slot_rows(planes, cores, own, gathered, router, sent, kept, scores, stats, ordered):
    slots, width = router.shape
    half = width // 2
    tokens, cotangent = image_tokens(gathered)
    ordered[...] = dot(turned(slots, planes, cores, own), router[...]).astype(NARROW)
    logits = dot(ordered[...], tokens, 1, 1)
    scores[...] = logits
    high, low = pieces(jnp.max(logits, axis=1, keepdims=True), 2)
    weight = jnp.exp(logits - (high + low))
    total = jnp.sum(weight, axis=1, keepdims=True)
    stats[...] = as_lanes([high + low, total])
    first, second = (piece.astype(NARROW) for piece in pieces(weight, 2))
    part_in = dot(first, tokens) + dot(second, tokens)
    part_back = dot(combine_of(logits).astype(NARROW), cotangent)
    lower = lax.axis_index("y_lo") == 0
    for k, part in enumerate((part_in, part_back)):
        mine = slice(k * slots, (k + 1) * slots)
        kept[mine, :] = jnp.where(lower, part[:, :half], part[:, half:])
        sent[mine, :] = jnp.where(lower, part[:, half:], part[:, :half]).astype(NARROW)
    sent[2 * slots :, :] = as_lines([high, low, *pieces(total, 2)], half).astype(NARROW)


def joined_rows(planes, own, arrived, kept, local_stats, both, exact, stats):
    slots = exact.shape[0]
    there = as_columns(arrived[2 * slots :, :].astype(WIDE), slots)
    top_here, total_here = local_stats[:, 0:1], local_stats[:, 1:2]
    top_there, total_there = there[:, 0:1] + there[:, 1:2], there[:, 2:3] + there[:, 3:4]
    top = jnp.maximum(top_here, top_there)
    here, there = jnp.exp(top_here - top), jnp.exp(top_there - top)
    total = here * total_here + there * total_there
    stats[...] = as_lanes([top, total])
    slot_part = kept[:slots, :] * (here / total) + arrived[:slots, :].astype(WIDE) * (there / total)
    back_part = kept[slots:, :] + arrived[slots : 2 * slots, :].astype(WIDE)
    exact[...] = slot_part
    narrow = jnp.concatenate([slot_part, back_part]).astype(NARROW)
    unit = planes * own
    both[...] = dot(turned(2 * slots, 2, slots // unit, unit), narrow).astype(NARROW)


def sorted_copies(planes, own, arrived, sent):
    rows = arrived.shape[0]
    unit = 2 * planes * own
    ordered = dot(turned(rows, rows // unit, unit, 1), arrived[...]).astype(NARROW)
    ordered = jnp.concatenate([ordered[: rows // 2], ordered[rows // 2 :]], axis=1)
    high = sent.shape[1]
    for k in range(sent.shape[0]):
        first = k // (sent.shape[0] // planes) * high
        sent[k] = ordered[first : first + high]


def expert_rows(arrived, own, e):
    each = arrived.shape[1] // own
    half = arrived.shape[2] // 2
    return tuple(
        jnp.concatenate(
            [
                jnp.concatenate(
                    [
                        arrived[j + h, e * each : (e + 1) * each, k * half : (k + 1) * half]
                        for h in range(2)
                    ],
                    axis=1,
                )
                for j in range(0, arrived.shape[0], 2)
            ]
        )
        for k in range(2)
    )


def experts(arrived, w_in, w_out, sent, acts):
    own, hidden_width = w_in.shape[0], w_in.shape[2]
    each, high, half = acts.shape[0] // own, arrived.shape[1] // own, arrived.shape[2] // 2
    root = (2.0 / jnp.pi) ** 0.5
    for e in range(own):
        mine = slice(e * each, (e + 1) * each)
        there = slice(e * high, (e + 1) * high)
        slot_in, back = expert_rows(arrived, own, e)
        v = dot(slot_in, w_in[e])
        grad_hidden = dot(back, w_out[e], 1, 1)
        t = jnp.tanh(root * (v + 0.044715 * (v * v * v)))
        upper = 0.5 * (1.0 + t)
        low = (v * upper).astype(NARROW)
        slope = upper + 0.5 * v * (1.0 - t * t) * (root * (1.0 + 3 * 0.044715 * (v * v)))
        grad_low = (slope * grad_hidden).astype(NARROW)
        acts[mine, :hidden_width] = low
        acts[mine, hidden_width:] = grad_low
        slot_out = dot(low, w_out[e]).astype(NARROW)
        grad_in = dot(grad_low, w_in[e], 1, 1).astype(NARROW)
        for k in range(sent.shape[0]):
            y, p = k // 2 * high, k % 2 * half
            sent[k, there, :half] = slot_out[y : y + high, p : p + half]
            sent[k, there, half:] = grad_in[y : y + high, p : p + half]


def weight_grads(arrived, acts, grad_in, grad_out):
    own, hidden_width = grad_in.shape[0], grad_in.shape[2]
    each = acts.shape[0] // own
    for e in range(own):
        mine = slice(e * each, (e + 1) * each)
        slot_in, back = expert_rows(arrived, own, e)
        grad_in[e] = dot(slot_in, acts[mine, hidden_width:], 0, 0).astype(NARROW)
        grad_out[e] = dot(acts[mine, :hidden_width], back, 0, 0).astype(NARROW)


def joined_results(planes, own, arrived, both):
    parts, half = arrived.shape[0] // planes, arrived.shape[2] // 2
    found = []
    for y in range(planes):
        total = arrived[y * parts].astype(WIDE)
        for t in range(1, parts):
            total += arrived[y * parts + t].astype(WIDE)
        found.append(total.astype(NARROW))
    found = jnp.concatenate(found)
    found = jnp.concatenate([found[:, :half], found[:, half:]])
    rows = found.shape[0]
    unit = 2 * planes * own
    both[...] = dot(turned(rows, unit, rows // unit, 1), found).astype(NARROW)


def dotted_rows(planes, own, arrived, exact, sent, column):
    slots, half = exact.shape
    unit = planes * own
    home = dot(turned(2 * slots, slots // unit, 2, unit), arrived[...])
    part = jnp.sum(exact[...] * home[slots:], axis=1, keepdims=True)
    column[...] = as_lanes([part])
    sent[: 2 * slots, :] = home.astype(NARROW)
    sent[2 * slots :, :] = as_lines(pieces(part, 3), half).astype(NARROW)


def softmax_grads(
    planes, cores, own, here, column, there, gathered, scores, stats, ordered, left, right, router
):
    slots = scores.shape[0]
    tokens, cotangent = image_tokens(gathered)
    lower = lax.axis_index("y_lo") == 0
    mine, other = here[: 2 * slots, :], there[: 2 * slots, :]
    joined = jnp.concatenate(
        [jnp.where(lower, mine, other), jnp.where(lower, other, mine)], axis=1
    )
    slot_out, grad_in = joined[:slots], joined[slots:]
    rest = as_columns(there[2 * slots :, :].astype(WIDE), slots)
    column_dot = column[:, 0:1] + (rest[:, 0:1] + rest[:, 1:2] + rest[:, 2:3])
    logits = scores[...]
    dispatch = jnp.exp(logits - stats[:, 0:1]) / stats[:, 1:2]
    combine = combine_of(logits)
    grad_combine = dot(slot_out, cotangent, 1, 1)
    grad_dispatch = dot(grad_in, tokens, 1, 1)
    row_dot = jnp.sum(grad_combine * combine, axis=0, keepdims=True)
    grad_logits = (
        combine * (grad_combine - row_dot) + dispatch * (grad_dispatch - column_dot)
    ).astype(NARROW)
    by_slot = dot(turned(slots, cores, planes, own), grad_logits).astype(NARROW)
    by_slot = dot(by_slot, tokens)
    count, high, wide = router.shape
    across = by_slot.shape[1] // wide
    for k in range(count):
        down, over = k // across * high, k % across * wide
        router[k] = by_slot[down : down + high, over : over + wide].astype(NARROW)
    left[:slots, :] = dispatch.astype(NARROW)
    left[slots:, :] = grad_logits
    right[:slots, :] = grad_in
    right[slots:, :] = ordered[...]


def token_grads(left, right, *refs):
    sent, found = refs[:-1], refs[-1]
    count, seq = found.shape[0], found.shape[1]
    grads = dot(left[...], right[...], 0, 0)
    for k in range(count):
        found[k] = grads[k * seq : (k + 1) * seq]
    here = lax.axis_index("x")
    for k in range(count):
        sent[k][...] = found[jnp.bitwise_xor(here, k)].astype(NARROW)


def placed_tokens(*refs):
    arrived, grad_tokens = refs[:-1], refs[-1]
    here = lax.axis_index("x")
    for k, block in enumerate(arrived):
        grad_tokens[jnp.bitwise_xor(here, k)] = block[...]


def summed_copies(arrived, sent):
    total = arrived[0].astype(WIDE)
    for t in range(1, arrived.shape[0]):
        total += arrived[t].astype(WIDE)
    for t in range(sent.shape[0]):
        sent[t] = total.astype(sent.dtype)


def placed(arrived, router):
    count, high, wide = arrived.shape
    across = router.shape[1] // wide
    for k in range(count):
        down, right = k // across * high, k % across * wide
        router[down : down + high, right : right + wide] = arrived[k].astype(router.dtype)


def local(body, outs, flops, *args, limit=12, scratch=()):
    moved = sum(a.size * a.dtype.itemsize for a in (*args, *outs))
    return pl.pallas_call(
        body,
        out_shape=outs,
        in_specs=[pl.BlockSpec(memory_space=pltpu.VMEM)] * len(args),
        out_specs=tuple([pl.BlockSpec(memory_space=pltpu.VMEM)] * len(outs)),
        scratch_shapes=scratch,
        cost_estimate=pl.CostEstimate(flops=flops, bytes_accessed=moved, transcendentals=0),
        compiler_params=pltpu.CompilerParams(vmem_limit_bytes=limit << 20),
    )(*args)


def shaped(shape, dtype=NARROW):
    return jax.ShapeDtypeStruct(shape, dtype)


def exchanged(blocks, axis):
    return lax.all_to_all(blocks, axis, split_axis=0, concat_axis=0, tiled=True)


def from_partner(block, axis, k):
    return lax.ppermute(block, axis, [(i, i ^ k) for i in range(lax.axis_size(axis))])


def on_device(tokens, cotangent, dispatch_weight, w_in, w_out):
    images, seq, width = tokens.shape
    slots = dispatch_weight.shape[1]
    own, hidden_width = w_in.shape[0], w_in.shape[2]
    planes, cores = lax.axis_size("y_hi"), lax.axis_size("core")
    plane, column = lax.axis_size(PLANE), lax.axis_size(COLUMN)
    half, count = width // 2, images * seq
    unit = planes * own
    rows = own * images * lax.axis_size(DP)

    both = jnp.concatenate([tokens, cotangent], axis=1)
    gathered = exchanged(both, "x")
    sent, kept, scores, stats, ordered = local(
        functools.partial(slot_rows, planes, cores, own),
        (
            shaped((2 * slots + EXTRA, half)),
            shaped((2 * slots, half), WIDE),
            shaped((slots, count), WIDE),
            shaped((slots, LANES), WIDE),
            shaped((slots, width)),
        ),
        8 * slots * count * width,
        gathered,
        dispatch_weight.T,
    )
    both, exact, stats = local(
        functools.partial(joined_rows, planes, own),
        (shaped((2 * slots, half)), shaped((slots, half), WIDE), shaped((slots, LANES), WIDE)),
        4 * slots * slots * width,
        from_partner(sent, "y_lo", 1),
        kept,
        stats,
    )
    arrived = exchanged(both.reshape(column, 2 * unit, half), COLUMN).reshape(2 * slots, half)
    high = own * column
    (sent,) = local(
        functools.partial(sorted_copies, planes, own),
        (shaped((plane, high, width)),),
        4 * slots * slots * width,
        arrived,
    )
    arrived = exchanged(sent, PLANE)
    sent, acts = local(
        experts,
        (shaped((plane, high, width)), shaped((rows, 2 * hidden_width))),
        8 * rows * width * hidden_width,
        arrived,
        w_in,
        w_out,
    )
    back = exchanged(sent, PLANE)
    grad_w_in, grad_w_out = local(
        weight_grads,
        (shaped(w_in.shape), shaped(w_out.shape)),
        4 * rows * width * hidden_width,
        arrived,
        acts,
    )
    (both,) = local(
        functools.partial(joined_results, planes, own),
        (shaped((2 * slots, half)),),
        4 * slots * slots * width,
        back,
    )
    arrived = exchanged(both.reshape(column, 2 * unit, half), COLUMN).reshape(2 * slots, half)
    sent, part = local(
        functools.partial(dotted_rows, planes, own),
        (shaped((2 * slots + EXTRA, half)), shaped((slots, LANES), WIDE)),
        4 * slots * slots * width,
        arrived,
        exact,
    )
    across = width // LANES
    tall = slots * across // plane
    left, right, router = local(
        functools.partial(softmax_grads, planes, cores, own),
        (
            shaped((2 * slots, count)),
            shaped((2 * slots, width)),
            shaped((plane, tall, LANES)),
        ),
        6 * slots * count * width,
        sent,
        part,
        from_partner(sent, "y_lo", 1),
        gathered,
        scores,
        stats,
        ordered,
    )
    blocks = local(
        token_grads,
        tuple([shaped((seq, width))] * images),
        4 * slots * count * width,
        left,
        right,
        scratch=(pltpu.VMEM((images, seq, width), WIDE),),
    )
    blocks = [blocks[0]] + [from_partner(blocks[k], "x", k) for k in range(1, images)]
    (grad_tokens,) = local(
        placed_tokens, (shaped((images, seq, width)),), count * width, *blocks
    )
    (router,) = local(
        summed_copies,
        (shaped((column, tall, LANES)),),
        slots * width,
        exchanged(router, PLANE),
    )
    (router,) = local(
        summed_copies,
        (shaped((plane, tall, LANES)),),
        slots * width,
        exchanged(router, COLUMN),
    )
    (router,) = local(
        placed, (shaped((slots, width), WIDE),), slots * width, exchanged(router, PLANE)
    )
    return (grad_tokens, router.T, grad_w_in, grad_w_out)


def solution(mesh):
    groups, parts = mesh.devices.shape
    fine = Mesh(
        mesh.devices.reshape(groups // 4, 2, 2, parts // 2, 2),
        ("z", "y_hi", "core", "x", "y_lo"),
    )
    return jax.shard_map(
        on_device,
        mesh=fine,
        in_specs=(
            P(DP, TENSOR, None),
            P(DP, TENSOR, None),
            P(),
            P(DP, None, TENSOR),
            P(DP, TENSOR, None),
        ),
        out_specs=(P(DP, TENSOR, None), P(), P(DP, None, TENSOR), P(DP, TENSOR, None)),
        check_vma=False,
    )
```

time: 162 us -> 149 us (0.920)
  blocking collectives: 119 us -> 104 us
  starting transfers between devices: 7.09 us -> 14.4 us
  Pallas kernels: 15.3 us -> 11.9 us
  waiting for transfers between devices: 18.9 us -> 15.9 us
    all_to_all x7 -> x6, blocking collectives: 119 us -> 104 us  [exchanged(): return lax.all_to_all(blocks, axis, split_axis=0, concat_axis=0, tiled=True)]
    all_to_all x2, waiting for transfers between devices: 18.9 us -> 8 us  [exchanged(): return lax.all_to_all(blocks, axis, split_axis=0, concat_axis=0, tiled=True)]
    ppermute x0 -> x5, waiting for transfers between devices: none -> 7.87 us  [from_partner(): lax.ppermute(block, axis, [(i, i ^ k) for i in range(lax.axis_size(axis))])]
    ppermute x0 -> x5, starting transfers between devices: none -> 5.69 us  [from_partner(): lax.ppermute(block, axis, [(i, i ^ k) for i in range(lax.axis_size(axis))])]
    pallas_call x12 -> x13, Pallas kernels: 15.3 us -> 11.9 us  [local(): pl.pallas_call(body, out_shape=outs, in_specs=[pl.BlockSpec(memory_space=...]
    all_to_all x2, starting transfers between devices: 7.09 us -> 8.71 us  [exchanged(): return lax.all_to_all(blocks, axis, split_axis=0, concat_axis=0, tiled=True)]
  transfers between devices with their start and end apart: 2 -> 7, of which waited for: 2 -> 4; matrix products, arithmetic and copies ran while one was open for 0% -> 0% of each run, Pallas kernels for 3% -> 3%
where the time goes in v3:
time: 149 us; the launch traced here: 148 us
  blocking collectives  104 us (70%)
  waiting for transfers between devices  15.9 us (11%)
  starting transfers between devices  14.4 us (10%)
  Pallas kernels  11.9 us (8%)
    all_to_all x6, blocking collectives, exchanged(): return lax.all_to_all(blocks, axis, split_axis=0, concat_axis=0, tiled=True)  104 us
    pallas_call x13, Pallas kernels, local(): pl.pallas_call(body, out_shape=outs, in_specs=[pl.BlockSpec(memory_space=...  11.9 us
    all_to_all x2, starting transfers between devices, exchanged(): return lax.all_to_all(blocks, axis, split_axis=0, concat_axis=0, tiled=True)  8.71 us
    all_to_all x2, waiting for transfers between devices, exchanged(): return lax.all_to_all(blocks, axis, split_axis=0, concat_axis=0, tiled=True)  8 us
    ppermute x5, waiting for transfers between devices, from_partner(): lax.ppermute(block, axis, [(i, i ^ k) for i in range(lax.axis_size(axis))])  7.87 us
    ppermute x5, starting transfers between devices, from_partner(): lax.ppermute(block, axis, [(i, i ^ k) for i in range(lax.axis_size(axis))])  5.69 us
  transfers between devices with their start and end apart: 7, of which 4 were waited for; matrix products, arithmetic and copies ran while one was open for 0% of the time, Pallas kernels for 3%

profile of v3, /device:TPU:1, one launch (start us, length us, event | category | flops | bytes accessed | tf_op | source)
XLA Modules:
  0.0 148.5 jit_solution(16817206009204096660)
XLA Ops:
  0.6 0.0 copy-start.2
  0.6 1.4 pad_maximum_fusion
  2.0 20.2 %all_to_all.40.gathered = bf16[4,144,1024]{2,1,0:T(8,128)(2,1)S(1)} all-to-all(bf16[4,144,1024]{2,1,0:T(8,128)(2,1)S(1)} %pad_maximum_fusion), channel_id=1, replica_groups=mesh['z'=8,'y_hi'=2,'core'=2,'x'=4,'y_lo'=2] {'x'}, dimensions={0} | all-to-all | bytes 2359296 | tf_op jit(solution)/shard_map/all_to_all | solution.py:303
  22.2 0.0 copy-done.2
  22.3 0.0 copy-start.1
  22.3 1.1 shard_map.84
  23.4 0.0 copy-start
  23.4 1.4 collective-permute-start
  24.8 2.6 %collective-permute-done.arrived = bf16[136,512]{1,0:T(8,128)(2,1)S(1)} collective-permute-done((bf16[136,512]{1,0:T(8,128)(2,1)S(1)}, bf16[136,512]{1,0:T(8,128)(2,1)S(1)}, u32[]{:S(2)}, u32[]{:S(2)}) %collective-permute-start) | collective-permute-done | bytes 139296 | tf_op jit(solution)/shard_map/ppermute | solution.py:307
  27.4 0.5 shard_map.85
  27.9 20.2 %all_to_all.41 = bf16[16,8,512]{2,1,0:T(8,128)(2,1)S(1)} all-to-all(bf16[16,8,512]{2,1,0:T(8,128)(2,1)S(1)} %bitcast.10), channel_id=1, replica_groups=mesh['z'=8,'y_hi'=2,'core'=2,'x'=4,'y_lo'=2] {'z','core'}, dimensions={0} | all-to-all | bytes 262144 | tf_op jit(solution)/shard_map/all_to_all | solution.py:303
  48.0 0.2 shard_map.86
  48.3 21.5 %all_to_all.42.arrived = bf16[16,32,1024]{2,1,0:T(8,128)(2,1)S(1)} all-to-all(bf16[16,32,1024]{2,1,0:T(8,128)(2,1)S(1)} %shard_map.86), channel_id=1, replica_groups=mesh['z'=8,'y_hi'=2,'core'=2,'x'=4,'y_lo'=2] {'y_hi','x','y_lo'}, dimensions={0} | all-to-all | bytes 2097152 | tf_op jit(solution)/shard_map/all_to_all | solution.py:303
  69.8 0.0 copy-done.1
  69.8 0.0 copy-done
  69.8 2.3 %shard_map.87 = (bf16[16,32,1024]{2,1,0:T(8,128)(2,1)S(1)}, bf16[256,1024]{1,0:T(8,128)(2,1)S(1)}) custom-call(bf16[16,32,1024]{2,1,0:T(8,128)(2,1)S(1)} %all_to_all.42.arrived, bf16[2,1024,512]{2,1,0:T(8,128)(2,1)S(1)} %copy-done, bf16[2,512,1024]{2,1,0:T(8,128)(2,1)S(1)} %copy-done.1), custom_call_target="tpu_custom_call" | custom-call | flops 1073741824 | bytes 6815744 | tf_op jit(solution)/shard_map/pallas_call | solution.py:287
  72.0 18.8 %all_to_all.43.arrived = bf16[16,32,1024]{2,1,0:T(8,128)(2,1)S(1)} all-to-all(bf16[16,32,1024]{2,1,0:T(8,128)(2,1)S(1)} %get-tuple-element.29), channel_id=1, replica_groups=mesh['z'=8,'y_hi'=2,'core'=2,'x'=4,'y_lo'=2] {'y_hi','x','y_lo'}, dimensions={0} | all-to-all | bytes 2097152 | tf_op jit(solution)/shard_map/all_to_all | solution.py:303
  90.9 0.3 shard_map.88
  91.2 13.8 %all_to_all.44 = bf16[16,8,512]{2,1,0:T(8,128)(2,1)S(1)} all-to-all(bf16[16,8,512]{2,1,0:T(8,128)(2,1)S(1)} %bitcast.7), channel_id=1, replica_groups=mesh['z'=8,'y_hi'=2,'core'=2,'x'=4,'y_lo'=2] {'z','core'}, dimensions={0} | all-to-all | bytes 262144 | tf_op jit(solution)/shard_map/all_to_all | solution.py:303
  104.9 0.3 shard_map.89
  105.2 0.3 collective-permute-start.1
  105.6 5.3 %collective-permute-done.1.there = bf16[136,512]{1,0:T(8,128)(2,1)S(1)} collective-permute-done((bf16[136,512]{1,0:T(8,128)(2,1)S(1)}, bf16[136,512]{1,0:T(8,128)(2,1)S(1)}, u32[]{:S(2)}, u32[]{:S(2)}) %collective-permute-start.1) | collective-permute-done | bytes 139296 | tf_op jit(solution)/shard_map/ppermute | solution.py:307
  110.9 0.9 shard_map.90
  111.7 9.7 %all_to_all.45.arrived = bf16[16,32,128]{2,1,0:T(8,128)(2,1)S(1)} all-to-all(bf16[16,32,128]{2,1,0:T(8,128)(2,1)S(1)} %get-tuple-element.42), channel_id=1, replica_groups=mesh['z'=8,'y_hi'=2,'core'=2,'x'=4,'y_lo'=2] {'y_hi','x','y_lo'}, dimensions={0} | all-to-all | bytes 262144 | tf_op jit(solution)/shard_map/all_to_all | solution.py:303
  121.4 0.7 shard_map.93
  122.1 5.2 %all-to-all-start.6 = ((bf16[16,32,128]{2,1,0:T(8,128)(2,1)}), bf16[16,32,128]{2,1,0:T(8,128)(2,1)S(1)}, u32[]{:S(2)}, u32[]{:S(2)}) async-start(bf16[16,32,128]{2,1,0:T(8,128)(2,1)} %shard_map.93), calls=%async_computation.6 | async-start | bytes 262144 | tf_op jit(solution)/shard_map/all_to_all | solution.py:303
  127.3 0.4 shard_map.91
  127.7 0.3 collective-permute-start.2
  128.0 2.0 %collective-permute-start.3 = (bf16[72,1024]{1,0:T(8,128)(2,1)S(1)}, bf16[72,1024]{1,0:T(8,128)(2,1)S(1)}, u32[]{:S(2)}, u32[]{:S(2)}) collective-permute-start(bf16[72,1024]{1,0:T(8,128)(2,1)S(1)} %get-tuple-element.40), channel_id=1, source_target_pairs={{0,4},{2,6},{4,0},{6,2},{1,5},{3,7},{5,1},{7,3},{8,12},{10,14},{12... | collective-permute-start | bytes 442376 | tf_op jit(solution)/shard_map/ppermute | solution.py:307
  130.0 1.7 %collective-permute-start.4 = (bf16[72,1024]{1,0:T(8,128)(2,1)S(1)}, bf16[72,1024]{1,0:T(8,128)(2,1)S(1)}, u32[]{:S(2)}, u32[]{:S(2)}) collective-permute-start(bf16[72,1024]{1,0:T(8,128)(2,1)S(1)} %get-tuple-element.41), channel_id=1, source_target_pairs={{0,6},{2,4},{4,2},{6,0},{1,7},{3,5},{5,3},{7,1},{8,14},{10,12},{12... | collective-permute-start | bytes 442376 | tf_op jit(solution)/shard_map/ppermute | solution.py:307
  131.6 4.8 %all-to-all-done.6.arrived = bf16[16,32,128]{2,1,0:T(8,128)(2,1)S(1)} async-done(((bf16[16,32,128]{2,1,0:T(8,128)(2,1)}), bf16[16,32,128]{2,1,0:T(8,128)(2,1)S(1)}, u32[]{:S(2)}, u32[]{:S(2)}) %all-to-all-start.6) | async-done | bytes 131104 | tf_op jit(solution)/shard_map/all_to_all | solution.py:303
  136.5 0.7 shard_map.94
  137.2 3.5 %all-to-all-start.7 = ((bf16[16,32,128]{2,1,0:T(8,128)(2,1)}), bf16[16,32,128]{2,1,0:T(8,128)(2,1)S(1)}, u32[]{:S(2)}, u32[]{:S(2)}) async-start(bf16[16,32,128]{2,1,0:T(8,128)(2,1)} %shard_map.94), calls=%async_computation.7 | async-start | bytes 262144 | tf_op jit(solution)/shard_map/all_to_all | solution.py:303
  140.7 3.0 %shard_map.96 = (bf16[2,1024,512]{2,1,0:T(8,128)(2,1)}, bf16[2,512,1024]{2,1,0:T(8,128)(2,1)}) custom-call(bf16[16,32,1024]{2,1,0:T(8,128)(2,1)S(1)} %all_to_all.42.arrived, bf16[256,1024]{1,0:T(8,128)(2,1)S(1)} %get-tuple-element.43.acts), custom_call_target="tpu_custom_call" | custom-call | flops 536870912 | bytes 5767168 | tf_op jit(solution)/shard_map/pallas_call | solution.py:287
  143.7 0.0 collective-permute-done.2.refs_1_
  143.7 0.0 collective-permute-done.3.refs_2_
  143.7 0.0 collective-permute-done.4.refs_3_
  143.7 0.9 shard_map.92
  144.6 3.2 %all-to-all-done.7.arrived = bf16[16,32,128]{2,1,0:T(8,128)(2,1)S(1)} async-done(((bf16[16,32,128]{2,1,0:T(8,128)(2,1)}), bf16[16,32,128]{2,1,0:T(8,128)(2,1)S(1)}, u32[]{:S(2)}, u32[]{:S(2)}) %all-to-all-start.7) | async-done | bytes 131104 | tf_op jit(solution)/shard_map/all_to_all | solution.py:303
  147.7 0.7 shard_map.95
Async XLA Ops:
  0.6 21.6 %copy-start.2 = (bf16[1024,64]{0,1:T(8,128)(2,1)S(1)}, bf16[1024,64]{0,1:T(8,128)(2,1)}, u32[]{:S(2)}) copy-start(bf16[1024,64]{0,1:T(8,128)(2,1)} %param.7) | copy-start | bytes 393220
  22.3 47.5 %copy-start.1 = (bf16[2,512,1024]{2,1,0:T(8,128)(2,1)S(1)}, bf16[2,512,1024]{2,1,0:T(8,128)(2,1)}, u32[]{:S(2)}) copy-start(bf16[2,512,1024]{2,1,0:T(8,128)(2,1)} %w_out.1) | copy-start | bytes 6291460
  23.4 46.4 %copy-start = (bf16[2,1024,512]{2,1,0:T(8,128)(2,1)S(1)}, bf16[2,1024,512]{2,1,0:T(8,128)(2,1)}, u32[]{:S(2)}) copy-start(bf16[2,1024,512]{2,1,0:T(8,128)(2,1)} %w_in.1) | copy-start | bytes 6291460
  23.4 4.0 %collective-permute-start = (bf16[136,512]{1,0:T(8,128)(2,1)S(1)}, bf16[136,512]{1,0:T(8,128)(2,1)S(1)}, u32[]{:S(2)}, u32[]{:S(2)}) collective-permute-start(bf16[136,512]{1,0:T(8,128)(2,1)S(1)} %get-tuple-element.25), channel_id=1, source_target_pairs={{0,1},{1,0},{2,3},{3,2},{4,5},{5,4},{6,7},{7,6},{8,9},{9,8},{10,11... | collective-permute-start | bytes 417800 | tf_op jit(solution)/shard_map/ppermute | solution.py:307
  105.2 5.6 %collective-permute-start.1 = (bf16[136,512]{1,0:T(8,128)(2,1)S(1)}, bf16[136,512]{1,0:T(8,128)(2,1)S(1)}, u32[]{:S(2)}, u32[]{:S(2)}) collective-permute-start(bf16[136,512]{1,0:T(8,128)(2,1)S(1)} %get-tuple-element.31.here), channel_id=1, source_target_pairs={{0,1},{1,0},{2,3},{3,2},{4,5},{5,4},{6,7},{7,6},{8,9},{9,8},{10,11... | collective-permute-start | bytes 417800 | tf_op jit(solution)/shard_map/ppermute | solution.py:307
  122.1 14.4 %all-to-all-start.6 = ((bf16[16,32,128]{2,1,0:T(8,128)(2,1)}), bf16[16,32,128]{2,1,0:T(8,128)(2,1)S(1)}, u32[]{:S(2)}, u32[]{:S(2)}) async-start(bf16[16,32,128]{2,1,0:T(8,128)(2,1)} %shard_map.93), calls=%async_computation.6 | async-start | bytes 262144 | tf_op jit(solution)/shard_map/all_to_all | solution.py:303
  127.7 16.0 %collective-permute-start.2 = (bf16[72,1024]{1,0:T(8,128)(2,1)S(1)}, bf16[72,1024]{1,0:T(8,128)(2,1)S(1)}, u32[]{:S(2)}, u32[]{:S(2)}) collective-permute-start(bf16[72,1024]{1,0:T(8,128)(2,1)S(1)} %get-tuple-element.39), channel_id=1, source_target_pairs={{0,2},{2,0},{4,6},{6,4},{1,3},{3,1},{5,7},{7,5},{8,10},{10,8},{12,... | collective-permute-start | bytes 442376 | tf_op jit(solution)/shard_map/ppermute | solution.py:307
  128.0 15.7 %collective-permute-start.3 = (bf16[72,1024]{1,0:T(8,128)(2,1)S(1)}, bf16[72,1024]{1,0:T(8,128)(2,1)S(1)}, u32[]{:S(2)}, u32[]{:S(2)}) collective-permute-start(bf16[72,1024]{1,0:T(8,128)(2,1)S(1)} %get-tuple-element.40), channel_id=1, source_target_pairs={{0,4},{2,6},{4,0},{6,2},{1,5},{3,7},{5,1},{7,3},{8,12},{10,14},{12... | collective-permute-start | bytes 442376 | tf_op jit(solution)/shard_map/ppermute | solution.py:307
  130.0 13.7 %collective-permute-start.4 = (bf16[72,1024]{1,0:T(8,128)(2,1)S(1)}, bf16[72,1024]{1,0:T(8,128)(2,1)S(1)}, u32[]{:S(2)}, u32[]{:S(2)}) collective-permute-start(bf16[72,1024]{1,0:T(8,128)(2,1)S(1)} %get-tuple-element.41), channel_id=1, source_target_pairs={{0,6},{2,4},{4,2},{6,0},{1,7},{3,5},{5,3},{7,1},{8,14},{10,12},{12... | collective-permute-start | bytes 442376 | tf_op jit(solution)/shard_map/ppermute | solution.py:307
  137.2 10.6 %all-to-all-start.7 = ((bf16[16,32,128]{2,1,0:T(8,128)(2,1)}), bf16[16,32,128]{2,1,0:T(8,128)(2,1)S(1)}, u32[]{:S(2)}, u32[]{:S(2)}) async-start(bf16[16,32,128]{2,1,0:T(8,128)(2,1)} %shard_map.94), calls=%async_computation.7 | async-start | bytes 262144 | tf_op jit(solution)/shard_map/all_to_all | solution.py:303

commit v4 on v3

--- a/solution.py
+++ b/solution.py
@@ -75,15 +75,22 @@
     return weight / jnp.sum(weight, axis=0, keepdims=True)
 
 
-def image_tokens(gathered):
-    seq = gathered.shape[1] // 2
+def sorted_blocks(both, *sent):
+    here = lax.axis_index("x")
+    for k, block in enumerate(sent):
+        block[...] = both[jnp.bitwise_xor(here, k)]
+
+
+def image_tokens(blocks):
+    seq = blocks[0].shape[0] // 2
     return tuple(
-        jnp.concatenate([gathered[k, f * seq : (f + 1) * seq, :] for k in range(gathered.shape[0])])
-        for f in range(2)
-    )
-
-
-def slot_rows(planes, cores, own, gathered, router, sent, kept, scores, stats, ordered):
+        jnp.concatenate([block[f * seq : (f + 1) * seq, :] for block in blocks]) for f in range(2)
+    )
+
+
+def slot_rows(planes, cores, own, *refs):
+    router, sent, kept, scores, stats, ordered = refs[-6:]
+    gathered = refs[:-6]
     slots, width = router.shape
     half = width // 2
     tokens, cotangent = image_tokens(gathered)
@@ -97,7 +104,7 @@
     first, second = (piece.astype(NARROW) for piece in pieces(weight, 2))
     part_in = dot(first, tokens) + dot(second, tokens)
     part_back = dot(combine_of(logits).astype(NARROW), cotangent)
-    lower = lax.axis_index("y_lo") == 0
+    lower = lax.axis_index("core") == 0
     for k, part in enumerate((part_in, part_back)):
         mine = slice(k * slots, (k + 1) * slots)
         kept[mine, :] = jnp.where(lower, part[:, :half], part[:, half:])
@@ -122,12 +129,14 @@
     both[...] = dot(turned(2 * slots, 2, slots // unit, unit), narrow).astype(NARROW)
 
 
-def sorted_copies(planes, own, arrived, sent):
+def sorted_copies(planes, arrived, sent):
     rows = arrived.shape[0]
-    unit = 2 * planes * own
-    ordered = dot(turned(rows, rows // unit, unit, 1), arrived[...]).astype(NARROW)
-    ordered = jnp.concatenate([ordered[: rows // 2], ordered[rows // 2 :]], axis=1)
     high = sent.shape[1]
+    ordered = dot(turned(rows, rows // 16, 16, 1), arrived[...]).astype(NARROW)
+    part = planes * high
+    ordered = jnp.concatenate(
+        [ordered[j * part : (j + 1) * part] for j in (0, 2, 1, 3)], axis=1
+    )
     for k in range(sent.shape[0]):
         first = k // (sent.shape[0] // planes) * high
         sent[k] = ordered[first : first + high]
@@ -135,18 +144,12 @@
 
 def expert_rows(arrived, own, e):
     each = arrived.shape[1] // own
-    half = arrived.shape[2] // 2
+    width = arrived.shape[2] // 2
     return tuple(
         jnp.concatenate(
             [
-                jnp.concatenate(
-                    [
-                        arrived[j + h, e * each : (e + 1) * each, k * half : (k + 1) * half]
-                        for h in range(2)
-                    ],
-                    axis=1,
-                )
-                for j in range(0, arrived.shape[0], 2)
+                arrived[j, e * each : (e + 1) * each, k * width : (k + 1) * width]
+                for j in range(arrived.shape[0])
             ]
         )
         for k in range(2)
@@ -155,7 +158,7 @@
 
 def experts(arrived, w_in, w_out, sent, acts):
     own, hidden_width = w_in.shape[0], w_in.shape[2]
-    each, high, half = acts.shape[0] // own, arrived.shape[1] // own, arrived.shape[2] // 2
+    each, high, width = acts.shape[0] // own, arrived.shape[1] // own, arrived.shape[2] // 2
     root = (2.0 / jnp.pi) ** 0.5
     for e in range(own):
         mine = slice(e * each, (e + 1) * each)
@@ -173,9 +176,8 @@
         slot_out = dot(low, w_out[e]).astype(NARROW)
         grad_in = dot(grad_low, w_in[e], 1, 1).astype(NARROW)
         for k in range(sent.shape[0]):
-            y, p = k // 2 * high, k % 2 * half
-            sent[k, there, :half] = slot_out[y : y + high, p : p + half]
-            sent[k, there, half:] = grad_in[y : y + high, p : p + half]
+            sent[k, there, :width] = slot_out[k * high : (k + 1) * high]
+            sent[k, there, width:] = grad_in[k * high : (k + 1) * high]
 
 
 def weight_grads(arrived, acts, grad_in, grad_out):
@@ -188,8 +190,8 @@
         grad_out[e] = dot(acts[mine, :hidden_width], back, 0, 0).astype(NARROW)
 
 
-def joined_results(planes, own, arrived, both):
-    parts, half = arrived.shape[0] // planes, arrived.shape[2] // 2
+def joined_results(planes, arrived, both):
+    parts, half = arrived.shape[0] // planes, both.shape[1]
     found = []
     for y in range(planes):
         total = arrived[y * parts].astype(WIDE)
@@ -197,10 +199,9 @@
             total += arrived[y * parts + t].astype(WIDE)
         found.append(total.astype(NARROW))
     found = jnp.concatenate(found)
-    found = jnp.concatenate([found[:, :half], found[:, half:]])
+    found = jnp.concatenate([found[:, j * half : (j + 1) * half] for j in (0, 2, 1, 3)])
     rows = found.shape[0]
-    unit = 2 * planes * own
-    both[...] = dot(turned(rows, unit, rows // unit, 1), found).astype(NARROW)
+    both[...] = dot(turned(rows, 16, rows // 16, 1), found).astype(NARROW)
 
 
 def dotted_rows(planes, own, arrived, exact, sent, column):
@@ -213,12 +214,12 @@
     sent[2 * slots :, :] = as_lines(pieces(part, 3), half).astype(NARROW)
 
 
-def softmax_grads(
-    planes, cores, own, here, column, there, gathered, scores, stats, ordered, left, right, router
-):
+def softmax_grads(planes, cores, own, *refs):
+    here, column, there, scores, stats, ordered, left, right, router = refs[-9:]
+    gathered = refs[:-9]
     slots = scores.shape[0]
     tokens, cotangent = image_tokens(gathered)
-    lower = lax.axis_index("y_lo") == 0
+    lower = lax.axis_index("core") == 0
     mine, other = here[: 2 * slots, :], there[: 2 * slots, :]
     joined = jnp.concatenate(
         [jnp.where(lower, mine, other), jnp.where(lower, other, mine)], axis=1
@@ -248,15 +249,11 @@
     right[slots:, :] = ordered[...]
 
 
-def token_grads(left, right, *refs):
-    sent, found = refs[:-1], refs[-1]
-    count, seq = found.shape[0], found.shape[1]
+def token_grads(left, right, *sent):
+    seq = sent[0].shape[0]
     grads = dot(left[...], right[...], 0, 0)
-    for k in range(count):
-        found[k] = grads[k * seq : (k + 1) * seq]
-    here = lax.axis_index("x")
-    for k in range(count):
-        sent[k][...] = found[jnp.bitwise_xor(here, k)].astype(NARROW)
+    for k, block in enumerate(sent):
+        block[...] = grads[k * seq : (k + 1) * seq].astype(NARROW)
 
 
 def placed_tokens(*refs):
@@ -282,14 +279,13 @@
         router[down : down + high, right : right + wide] = arrived[k].astype(router.dtype)
 
 
-def local(body, outs, flops, *args, limit=12, scratch=()):
+def local(body, outs, flops, *args, limit=12):
     moved = sum(a.size * a.dtype.itemsize for a in (*args, *outs))
     return pl.pallas_call(
         body,
         out_shape=outs,
         in_specs=[pl.BlockSpec(memory_space=pltpu.VMEM)] * len(args),
         out_specs=tuple([pl.BlockSpec(memory_space=pltpu.VMEM)] * len(outs)),
-        scratch_shapes=scratch,
         cost_estimate=pl.CostEstimate(flops=flops, bytes_accessed=moved, transcendentals=0),
         compiler_params=pltpu.CompilerParams(vmem_limit_bytes=limit << 20),
     )(*args)
@@ -303,8 +299,20 @@
     return lax.all_to_all(blocks, axis, split_axis=0, concat_axis=0, tiled=True)
 
 
-def from_partner(block, axis, k):
-    return lax.ppermute(block, axis, [(i, i ^ k) for i in range(lax.axis_size(axis))])
+def from_partner(block):
+    return lax.ppermute(block, "core", [(0, 1), (1, 0)])
+
+
+def moved(block, k):
+    axes = ("core", "x", "y_lo")
+    across = lax.axis_size("x")
+    pairs = []
+    for core in range(2):
+        for x in range(across):
+            for low in range(2):
+                source = (core * across + x) * 2 + low
+                pairs.append((source, (low * across + (x ^ k)) * 2 + core))
+    return lax.ppermute(block, axes, pairs)
 
 
 def on_device(tokens, cotangent, dispatch_weight, w_in, w_out):
@@ -318,7 +326,10 @@
     rows = own * images * lax.axis_size(DP)
 
     both = jnp.concatenate([tokens, cotangent], axis=1)
-    gathered = exchanged(both, "x")
+    blocks = local(
+        sorted_blocks, tuple([shaped((2 * seq, width))] * images), count * width, both
+    )
+    gathered = [moved(block, k) for k, block in enumerate(blocks)]
     sent, kept, scores, stats, ordered = local(
         functools.partial(slot_rows, planes, cores, own),
         (
@@ -329,29 +340,29 @@
             shaped((slots, width)),
         ),
         8 * slots * count * width,
-        gathered,
+        *gathered,
         dispatch_weight.T,
     )
     both, exact, stats = local(
         functools.partial(joined_rows, planes, own),
         (shaped((2 * slots, half)), shaped((slots, half), WIDE), shaped((slots, LANES), WIDE)),
         4 * slots * slots * width,
-        from_partner(sent, "y_lo", 1),
+        from_partner(sent),
         kept,
         stats,
     )
     arrived = exchanged(both.reshape(column, 2 * unit, half), COLUMN).reshape(2 * slots, half)
-    high = own * column
+    high = own * lax.axis_size("z")
     (sent,) = local(
-        functools.partial(sorted_copies, planes, own),
-        (shaped((plane, high, width)),),
+        functools.partial(sorted_copies, planes),
+        (shaped((plane, high, 2 * width)),),
         4 * slots * slots * width,
         arrived,
     )
     arrived = exchanged(sent, PLANE)
     sent, acts = local(
         experts,
-        (shaped((plane, high, width)), shaped((rows, 2 * hidden_width))),
+        (shaped((plane, high, 2 * width)), shaped((rows, 2 * hidden_width))),
         8 * rows * width * hidden_width,
         arrived,
         w_in,
@@ -366,7 +377,7 @@
         acts,
     )
     (both,) = local(
-        functools.partial(joined_results, planes, own),
+        functools.partial(joined_results, planes),
         (shaped((2 * slots, half)),),
         4 * slots * slots * width,
         back,
@@ -389,10 +400,10 @@
             shaped((plane, tall, LANES)),
         ),
         6 * slots * count * width,
+        *gathered,
         sent,
         part,
-        from_partner(sent, "y_lo", 1),
-        gathered,
+        from_partner(sent),
         scores,
         stats,
         ordered,
@@ -403,9 +414,8 @@
         4 * slots * count * width,
         left,
         right,
-        scratch=(pltpu.VMEM((images, seq, width), WIDE),),
-    )
-    blocks = [blocks[0]] + [from_partner(blocks[k], "x", k) for k in range(1, images)]
+    )
+    blocks = [moved(block, k) for k, block in enumerate(blocks)]
     (grad_tokens,) = local(
         placed_tokens, (shaped((images, seq, width)),), count * width, *blocks
     )

time: 149 us -> 142 us (0.953)
  blocking collectives: 104 us -> 81.7 us
  starting transfers between devices: 14.4 us -> 26.6 us
  waiting for transfers between devices: 15.9 us -> 19.2 us
    all_to_all x6 -> x5, blocking collectives: 104 us -> 81.7 us  [exchanged(): return lax.all_to_all(blocks, axis, split_axis=0, concat_axis=0, tiled=True)]
    ppermute x5 -> x10, starting transfers between devices: 5.69 us -> 18.2 us  [the longest x8 18 us: moved(): return lax.ppermute(block, axes, pairs)]
    ppermute x5 -> x10, waiting for transfers between devices: 7.87 us -> 15.7 us  [the longest x8 13 us: moved(): return lax.ppermute(block, axes, pairs)]
    all_to_all x2, waiting for transfers between devices: 8 us -> 3.54 us  [exchanged(): return lax.all_to_all(blocks, axis, split_axis=0, concat_axis=0, tiled=True)]
    pallas_call x13 -> x14, Pallas kernels: 11.9 us -> 11.9 us  [local(): pl.pallas_call(body, out_shape=outs, in_specs=[pl.BlockSpec(memory_space=...]
  transfers between devices with their start and end apart: 7 -> 12, of which waited for: 4 -> 8; matrix products, arithmetic and copies ran while one was open for 0% -> 0% of each run, Pallas kernels for 3% -> 3%
where the time goes in v4:
time: 142 us
  blocking collectives  81.7 us (58%)
  starting transfers between devices  26.6 us (19%)
  waiting for transfers between devices  19.2 us (14%)
  Pallas kernels  11.9 us (8%)
    all_to_all x5, blocking collectives, exchanged(): return lax.all_to_all(blocks, axis, split_axis=0, concat_axis=0, tiled=True)  81.7 us
    ppermute x8, starting transfers between devices, moved(): return lax.ppermute(block, axes, pairs)  18 us
    ppermute x8, waiting for transfers between devices, moved(): return lax.ppermute(block, axes, pairs)  13 us
    pallas_call x14, Pallas kernels, local(): pl.pallas_call(body, out_shape=outs, in_specs=[pl.BlockSpec(memory_space=...  11.9 us
    all_to_all x2, starting transfers between devices, exchanged(): return lax.all_to_all(blocks, axis, split_axis=0, concat_axis=0, tiled=True)  8.38 us
    all_to_all x2, waiting for transfers between devices, exchanged(): return lax.all_to_all(blocks, axis, split_axis=0, concat_axis=0, tiled=True)  3.54 us
  transfers between devices with their start and end apart: 12, of which 8 were waited for; matrix products, arithmetic and copies ran while one was open for 0% of the time, Pallas kernels for 3%

profile of v4, /device:TPU:1, one launch (start us, length us, event | category | flops | bytes accessed | tf_op | source)
XLA Modules:
  0.0 141.6 jit_solution(10811942913331588923)
XLA Ops:
  0.6 0.0 copy-start.2
  0.6 1.4 pad_maximum_fusion.both
  2.0 0.1 shard_map.84
  2.1 4.6 %collective-permute-start = (bf16[144,1024]{1,0:T(8,128)(2,1)S(1)}, bf16[144,1024]{1,0:T(8,128)(2,1)S(1)}, u32[]{:S(2)}, u32[]{:S(2)}) collective-permute-start(bf16[144,1024]{1,0:T(8,128)(2,1)S(1)} %get-tuple-element.29), channel_id=1, source_target_pairs={{0,0},{1,8},{2,2},{3,10},{4,4},{5,12},{6,6},{7,14},{8,1},{9,9},{10... | collective-permute-start | bytes 884744 | tf_op jit(solution)/shard_map/ppermute | solution.py:315
  6.7 1.0 collective-permute-start.1
  7.7 3.9 %collective-permute-start.2 = (bf16[144,1024]{1,0:T(8,128)(2,1)S(1)}, bf16[144,1024]{1,0:T(8,128)(2,1)S(1)}, u32[]{:S(2)}, u32[]{:S(2)}) collective-permute-start(bf16[144,1024]{1,0:T(8,128)(2,1)S(1)} %get-tuple-element.31), channel_id=1, source_target_pairs={{0,4},{1,12},{2,6},{3,14},{4,0},{5,8},{6,2},{7,10},{8,5},{9,13},{1... | collective-permute-start | bytes 884744 | tf_op jit(solution)/shard_map/ppermute | solution.py:315
  11.7 0.0 collective-permute-start.3
  11.7 0.7 collective-permute-done.refs_0_
  12.3 4.6 %collective-permute-done.1.refs_1_ = bf16[144,1024]{1,0:T(8,128)(2,1)S(1)} collective-permute-done((bf16[144,1024]{1,0:T(8,128)(2,1)S(1)}, bf16[144,1024]{1,0:T(8,128)(2,1)S(1)}, u32[]{:S(2)}, u32[]{:S(2)}) %collective-permute-start.1) | collective-permute-done | bytes 294944 | tf_op jit(solution)/shard_map/ppermute | solution.py:315
  16.9 5.1 %collective-permute-done.2.refs_2_ = bf16[144,1024]{1,0:T(8,128)(2,1)S(1)} collective-permute-done((bf16[144,1024]{1,0:T(8,128)(2,1)S(1)}, bf16[144,1024]{1,0:T(8,128)(2,1)S(1)}, u32[]{:S(2)}, u32[]{:S(2)}) %collective-permute-start.2) | collective-permute-done | bytes 294944 | tf_op jit(solution)/shard_map/ppermute | solution.py:315
  22.0 2.7 %collective-permute-done.3.refs_3_ = bf16[144,1024]{1,0:T(8,128)(2,1)S(1)} collective-permute-done((bf16[144,1024]{1,0:T(8,128)(2,1)S(1)}, bf16[144,1024]{1,0:T(8,128)(2,1)S(1)}, u32[]{:S(2)}, u32[]{:S(2)}) %collective-permute-start.3) | collective-permute-done | bytes 294944 | tf_op jit(solution)/shard_map/ppermute | solution.py:315
  24.7 0.0 copy-done.2
  24.7 1.1 shard_map.85
  25.8 0.0 copy-start
  25.8 0.1 collective-permute-start.4
  25.9 1.3 collective-permute-done.4.arrived
  27.3 0.5 shard_map.86
  27.7 17.3 %all_to_all.35 = bf16[16,8,512]{2,1,0:T(8,128)(2,1)S(1)} all-to-all(bf16[16,8,512]{2,1,0:T(8,128)(2,1)S(1)} %bitcast.10), channel_id=1, replica_groups=mesh['z'=8,'y_hi'=2,'core'=2,'x'=4,'y_lo'=2] {'z','core'}, dimensions={0} | all-to-all | bytes 262144 | tf_op jit(solution)/shard_map/all_to_all | solution.py:299
  45.1 0.2 shard_map.87
  45.3 22.1 %all_to_all.36.arrived = bf16[16,16,2048]{2,1,0:T(8,128)(2,1)S(1)} all-to-all(bf16[16,16,2048]{2,1,0:T(8,128)(2,1)S(1)} %shard_map.87), channel_id=1, replica_groups=mesh['z'=8,'y_hi'=2,'core'=2,'x'=4,'y_lo'=2] {'y_hi','x','y_lo'}, dimensions={0} | all-to-all | bytes 2097152 | tf_op jit(solution)/shard_map/all_to_all | solution.py:299
  67.4 0.0 copy-done.1
  67.4 2.2 %shard_map.88 = (bf16[16,16,2048]{2,1,0:T(8,128)(2,1)S(1)}, bf16[256,1024]{1,0:T(8,128)(2,1)S(1)}) custom-call(bf16[16,16,2048]{2,1,0:T(8,128)(2,1)S(1)} %all_to_all.36.arrived, bf16[2,1024,512]{2,1,0:T(8,128)(2,1)S(1)} %copy-done, bf16[2,512,1024]{2,1,0:T(8,128)(2,1)S(1)} %copy-done.1), custom_call_target="tpu_custom_call" | custom-call | flops 1073741824 | bytes 6815744 | tf_op jit(solution)/shard_map/pallas_call | solution.py:284
  69.7 18.8 %all_to_all.37.arrived = bf16[16,16,2048]{2,1,0:T(8,128)(2,1)S(1)} all-to-all(bf16[16,16,2048]{2,1,0:T(8,128)(2,1)S(1)} %get-tuple-element.37), channel_id=1, replica_groups=mesh['z'=8,'y_hi'=2,'core'=2,'x'=4,'y_lo'=2] {'y_hi','x','y_lo'}, dimensions={0} | all-to-all | bytes 2097152 | tf_op jit(solution)/shard_map/all_to_all | solution.py:299
  88.5 0.3 shard_map.89
  88.8 13.8 %all_to_all.38 = bf16[16,8,512]{2,1,0:T(8,128)(2,1)S(1)} all-to-all(bf16[16,8,512]{2,1,0:T(8,128)(2,1)S(1)} %bitcast.7), channel_id=1, replica_groups=mesh['z'=8,'y_hi'=2,'core'=2,'x'=4,'y_lo'=2] {'z','core'}, dimensions={0} | all-to-all | bytes 262144 | tf_op jit(solution)/shard_map/all_to_all | solution.py:299
  102.6 0.3 shard_map.90
  102.9 0.0 collective-permute-start.5
  102.9 1.3 collective-permute-done.5.refs_6_
  104.3 0.9 shard_map.91
  105.1 9.7 %all_to_all.39.arrived = bf16[16,32,128]{2,1,0:T(8,128)(2,1)S(1)} all-to-all(bf16[16,32,128]{2,1,0:T(8,128)(2,1)S(1)} %get-tuple-element.50), channel_id=1, replica_groups=mesh['z'=8,'y_hi'=2,'core'=2,'x'=4,'y_lo'=2] {'y_hi','x','y_lo'}, dimensions={0} | all-to-all | bytes 262144 | tf_op jit(solution)/shard_map/all_to_all | solution.py:299
  114.8 0.7 shard_map.94
  115.5 4.9 %all-to-all-start.5 = ((bf16[16,32,128]{2,1,0:T(8,128)(2,1)}), bf16[16,32,128]{2,1,0:T(8,128)(2,1)S(1)}, u32[]{:S(2)}, u32[]{:S(2)}) async-start(bf16[16,32,128]{2,1,0:T(8,128)(2,1)} %shard_map.94), calls=%async_computation.5 | async-start | bytes 262144 | tf_op jit(solution)/shard_map/all_to_all | solution.py:299
  120.4 0.3 shard_map.92
  120.7 2.2 %collective-permute-start.6 = (bf16[72,1024]{1,0:T(8,128)(2,1)S(1)}, bf16[72,1024]{1,0:T(8,128)(2,1)S(1)}, u32[]{:S(2)}, u32[]{:S(2)}) collective-permute-start(bf16[72,1024]{1,0:T(8,128)(2,1)S(1)} %get-tuple-element.46), channel_id=1, source_target_pairs={{0,0},{1,8},{2,2},{3,10},{4,4},{5,12},{6,6},{7,14},{8,1},{9,9},{10... | collective-permute-start | bytes 442376 | tf_op jit(solution)/shard_map/ppermute | solution.py:315
  122.9 1.4 %collective-permute-start.7 = (bf16[72,1024]{1,0:T(8,128)(2,1)S(1)}, bf16[72,1024]{1,0:T(8,128)(2,1)S(1)}, u32[]{:S(2)}, u32[]{:S(2)}) collective-permute-start(bf16[72,1024]{1,0:T(8,128)(2,1)S(1)} %get-tuple-element.47), channel_id=1, source_target_pairs={{0,2},{1,10},{2,0},{3,8},{4,6},{5,14},{6,4},{7,12},{8,3},{9,11},{1... | collective-permute-start | bytes 442376 | tf_op jit(solution)/shard_map/ppermute | solution.py:315
  124.4 2.0 %collective-permute-start.8 = (bf16[72,1024]{1,0:T(8,128)(2,1)S(1)}, bf16[72,1024]{1,0:T(8,128)(2,1)S(1)}, u32[]{:S(2)}, u32[]{:S(2)}) collective-permute-start(bf16[72,1024]{1,0:T(8,128)(2,1)S(1)} %get-tuple-element.48), channel_id=1, source_target_pairs={{0,4},{1,12},{2,6},{3,14},{4,0},{5,8},{6,2},{7,10},{8,5},{9,13},{1... | collective-permute-start | bytes 442376 | tf_op jit(solution)/shard_map/ppermute | solution.py:315
  126.3 2.9 %collective-permute-start.9 = (bf16[72,1024]{1,0:T(8,128)(2,1)S(1)}, bf16[72,1024]{1,0:T(8,128)(2,1)S(1)}, u32[]{:S(2)}, u32[]{:S(2)}) collective-permute-start(bf16[72,1024]{1,0:T(8,128)(2,1)S(1)} %get-tuple-element.49), channel_id=1, source_target_pairs={{0,6},{1,14},{2,4},{3,12},{4,2},{5,10},{6,0},{7,8},{8,7},{9,15},{1... | collective-permute-start | bytes 442376 | tf_op jit(solution)/shard_map/ppermute | solution.py:315
  129.2 0.3 all-to-all-done.5.arrived
  129.5 0.7 shard_map.95
  130.2 3.5 %all-to-all-start.6 = ((bf16[16,32,128]{2,1,0:T(8,128)(2,1)}), bf16[16,32,128]{2,1,0:T(8,128)(2,1)S(1)}, u32[]{:S(2)}, u32[]{:S(2)}) async-start(bf16[16,32,128]{2,1,0:T(8,128)(2,1)} %shard_map.95), calls=%async_computation.6 | async-start | bytes 262144 | tf_op jit(solution)/shard_map/all_to_all | solution.py:299
  133.7 3.0 %shard_map.97 = (bf16[2,1024,512]{2,1,0:T(8,128)(2,1)}, bf16[2,512,1024]{2,1,0:T(8,128)(2,1)}) custom-call(bf16[16,16,2048]{2,1,0:T(8,128)(2,1)S(1)} %all_to_all.36.arrived, bf16[256,1024]{1,0:T(8,128)(2,1)S(1)} %get-tuple-element.51.acts), custom_call_target="tpu_custom_call" | custom-call | flops 536870912 | bytes 5767168 | tf_op jit(solution)/shard_map/pallas_call | solution.py:284
  136.8 0.0 collective-permute-done.6.refs_0_
  136.8 0.0 collective-permute-done.7.refs_1_
  136.8 0.0 collective-permute-done.8.refs_2_
  136.8 0.0 collective-permute-done.9.refs_3_
  136.8 0.9 shard_map.93
  137.7 3.2 %all-to-all-done.6.arrived = bf16[16,32,128]{2,1,0:T(8,128)(2,1)S(1)} async-done(((bf16[16,32,128]{2,1,0:T(8,128)(2,1)}), bf16[16,32,128]{2,1,0:T(8,128)(2,1)S(1)}, u32[]{:S(2)}, u32[]{:S(2)}) %all-to-all-start.6) | async-done | bytes 131104 | tf_op jit(solution)/shard_map/all_to_all | solution.py:299
  140.9 0.7 shard_map.96
  (2 shorter events, 0.0 us)
Async XLA Ops:
  0.6 24.0 %copy-start.2 = (bf16[1024,64]{0,1:T(8,128)(2,1)S(1)}, bf16[1024,64]{0,1:T(8,128)(2,1)}, u32[]{:S(2)}) copy-start(bf16[1024,64]{0,1:T(8,128)(2,1)} %param.7) | copy-start | bytes 393220
  2.1 10.2 %collective-permute-start = (bf16[144,1024]{1,0:T(8,128)(2,1)S(1)}, bf16[144,1024]{1,0:T(8,128)(2,1)S(1)}, u32[]{:S(2)}, u32[]{:S(2)}) collective-permute-start(bf16[144,1024]{1,0:T(8,128)(2,1)S(1)} %get-tuple-element.29), channel_id=1, source_target_pairs={{0,0},{1,8},{2,2},{3,10},{4,4},{5,12},{6,6},{7,14},{8,1},{9,9},{10... | collective-permute-start | bytes 884744 | tf_op jit(solution)/shard_map/ppermute | solution.py:315
  6.7 10.2 %collective-permute-start.1 = (bf16[144,1024]{1,0:T(8,128)(2,1)S(1)}, bf16[144,1024]{1,0:T(8,128)(2,1)S(1)}, u32[]{:S(2)}, u32[]{:S(2)}) collective-permute-start(bf16[144,1024]{1,0:T(8,128)(2,1)S(1)} %get-tuple-element.30), channel_id=1, source_target_pairs={{0,2},{1,10},{2,0},{3,8},{4,6},{5,14},{6,4},{7,12},{8,3},{9,11},{1... | collective-permute-start | bytes 884744 | tf_op jit(solution)/shard_map/ppermute | solution.py:315
  7.7 14.2 %collective-permute-start.2 = (bf16[144,1024]{1,0:T(8,128)(2,1)S(1)}, bf16[144,1024]{1,0:T(8,128)(2,1)S(1)}, u32[]{:S(2)}, u32[]{:S(2)}) collective-permute-start(bf16[144,1024]{1,0:T(8,128)(2,1)S(1)} %get-tuple-element.31), channel_id=1, source_target_pairs={{0,4},{1,12},{2,6},{3,14},{4,0},{5,8},{6,2},{7,10},{8,5},{9,13},{1... | collective-permute-start | bytes 884744 | tf_op jit(solution)/shard_map/ppermute | solution.py:315
  11.7 13.0 %collective-permute-start.3 = (bf16[144,1024]{1,0:T(8,128)(2,1)S(1)}, bf16[144,1024]{1,0:T(8,128)(2,1)S(1)}, u32[]{:S(2)}, u32[]{:S(2)}) collective-permute-start(bf16[144,1024]{1,0:T(8,128)(2,1)S(1)} %get-tuple-element.32), channel_id=1, source_target_pairs={{0,6},{1,14},{2,4},{3,12},{4,2},{5,10},{6,0},{7,8},{8,7},{9,15},{1... | collective-permute-start | bytes 884744 | tf_op jit(solution)/shard_map/ppermute | solution.py:315
  24.7 42.7 %copy-start.1 = (bf16[2,512,1024]{2,1,0:T(8,128)(2,1)S(1)}, bf16[2,512,1024]{2,1,0:T(8,128)(2,1)}, u32[]{:S(2)}) copy-start(bf16[2,512,1024]{2,1,0:T(8,128)(2,1)} %w_out.1) | copy-start | bytes 6291460
  25.8 41.6 %copy-start = (bf16[2,1024,512]{2,1,0:T(8,128)(2,1)S(1)}, bf16[2,1024,512]{2,1,0:T(8,128)(2,1)}, u32[]{:S(2)}) copy-start(bf16[2,1024,512]{2,1,0:T(8,128)(2,1)} %w_in.1) | copy-start | bytes 6291460
  25.8 1.4 %collective-permute-start.4 = (bf16[136,512]{1,0:T(8,128)(2,1)S(1)}, bf16[136,512]{1,0:T(8,128)(2,1)S(1)}, u32[]{:S(2)}, u32[]{:S(2)}) collective-permute-start(bf16[136,512]{1,0:T(8,128)(2,1)S(1)} %get-tuple-element.33), channel_id=1, source_target_pairs={{0,8},{8,0},{1,9},{9,1},{2,10},{10,2},{3,11},{11,3},{4,12},{12,4},... | collective-permute-start | bytes 417800 | tf_op jit(solution)/shard_map/ppermute | solution.py:303
  102.9 1.4 collective-permute-start.5
  115.5 14.1 %all-to-all-start.5 = ((bf16[16,32,128]{2,1,0:T(8,128)(2,1)}), bf16[16,32,128]{2,1,0:T(8,128)(2,1)S(1)}, u32[]{:S(2)}, u32[]{:S(2)}) async-start(bf16[16,32,128]{2,1,0:T(8,128)(2,1)} %shard_map.94), calls=%async_computation.5 | async-start | bytes 262144 | tf_op jit(solution)/shard_map/all_to_all | solution.py:299
  120.7 16.1 %collective-permute-start.6 = (bf16[72,1024]{1,0:T(8,128)(2,1)S(1)}, bf16[72,1024]{1,0:T(8,128)(2,1)S(1)}, u32[]{:S(2)}, u32[]{:S(2)}) collective-permute-start(bf16[72,1024]{1,0:T(8,128)(2,1)S(1)} %get-tuple-element.46), channel_id=1, source_target_pairs={{0,0},{1,8},{2,2},{3,10},{4,4},{5,12},{6,6},{7,14},{8,1},{9,9},{10... | collective-permute-start | bytes 442376 | tf_op jit(solution)/shard_map/ppermute | solution.py:315
  122.9 13.9 %collective-permute-start.7 = (bf16[72,1024]{1,0:T(8,128)(2,1)S(1)}, bf16[72,1024]{1,0:T(8,128)(2,1)S(1)}, u32[]{:S(2)}, u32[]{:S(2)}) collective-permute-start(bf16[72,1024]{1,0:T(8,128)(2,1)S(1)} %get-tuple-element.47), channel_id=1, source_target_pairs={{0,2},{1,10},{2,0},{3,8},{4,6},{5,14},{6,4},{7,12},{8,3},{9,11},{1... | collective-permute-start | bytes 442376 | tf_op jit(solution)/shard_map/ppermute | solution.py:315
  124.4 12.4 %collective-permute-start.8 = (bf16[72,1024]{1,0:T(8,128)(2,1)S(1)}, bf16[72,1024]{1,0:T(8,128)(2,1)S(1)}, u32[]{:S(2)}, u32[]{:S(2)}) collective-permute-start(bf16[72,1024]{1,0:T(8,128)(2,1)S(1)} %get-tuple-element.48), channel_id=1, source_target_pairs={{0,4},{1,12},{2,6},{3,14},{4,0},{5,8},{6,2},{7,10},{8,5},{9,13},{1... | collective-permute-start | bytes 442376 | tf_op jit(solution)/shard_map/ppermute | solution.py:315
  126.3 10.4 %collective-permute-start.9 = (bf16[72,1024]{1,0:T(8,128)(2,1)S(1)}, bf16[72,1024]{1,0:T(8,128)(2,1)S(1)}, u32[]{:S(2)}, u32[]{:S(2)}) collective-permute-start(bf16[72,1024]{1,0:T(8,128)(2,1)S(1)} %get-tuple-element.49), channel_id=1, source_target_pairs={{0,6},{1,14},{2,4},{3,12},{4,2},{5,10},{6,0},{7,8},{8,7},{9,15},{1... | collective-permute-start | bytes 442376 | tf_op jit(solution)/shard_map/ppermute | solution.py:315
  130.2 10.6 %all-to-all-start.6 = ((bf16[16,32,128]{2,1,0:T(8,128)(2,1)}), bf16[16,32,128]{2,1,0:T(8,128)(2,1)S(1)}, u32[]{:S(2)}, u32[]{:S(2)}) async-start(bf16[16,32,128]{2,1,0:T(8,128)(2,1)} %shard_map.95), calls=%async_computation.6 | async-start | bytes 262144 | tf_op jit(solution)/shard_map/all_to_all | solution.py:299

commit v5 on v4

--- a/solution.py
+++ b/solution.py
@@ -88,13 +88,25 @@
     )
 
 
-def slot_rows(planes, cores, own, *refs):
+def own_first(mine, other):
+    lower = lax.axis_index("core") == 0
+    return jnp.concatenate([jnp.where(lower, mine, other), jnp.where(lower, other, mine)])
+
+
+def cores_rows(rows):
+    lower = lax.axis_index("core") == 0
+    first, second = rows[: rows.shape[0] // 2], rows[rows.shape[0] // 2 :]
+    return jnp.where(lower, first, second), jnp.where(lower, second, first)
+
+
+def slot_rows(cores, own, *refs):
     router, sent, kept, scores, stats, ordered = refs[-6:]
     gathered = refs[:-6]
     slots, width = router.shape
-    half = width // 2
+    half = slots // 2
     tokens, cotangent = image_tokens(gathered)
-    ordered[...] = dot(turned(slots, planes, cores, own), router[...]).astype(NARROW)
+    order = turned(slots, slots // (cores * own), cores, own)
+    ordered[...] = dot(order, router[...]).astype(NARROW)
     logits = dot(ordered[...], tokens, 1, 1)
     scores[...] = logits
     high, low = pieces(jnp.max(logits, axis=1, keepdims=True), 2)
@@ -104,39 +116,37 @@
     first, second = (piece.astype(NARROW) for piece in pieces(weight, 2))
     part_in = dot(first, tokens) + dot(second, tokens)
     part_back = dot(combine_of(logits).astype(NARROW), cotangent)
-    lower = lax.axis_index("core") == 0
     for k, part in enumerate((part_in, part_back)):
-        mine = slice(k * slots, (k + 1) * slots)
-        kept[mine, :] = jnp.where(lower, part[:, :half], part[:, half:])
-        sent[mine, :] = jnp.where(lower, part[:, half:], part[:, :half]).astype(NARROW)
-    sent[2 * slots :, :] = as_lines([high, low, *pieces(total, 2)], half).astype(NARROW)
-
-
-def joined_rows(planes, own, arrived, kept, local_stats, both, exact, stats):
-    slots = exact.shape[0]
-    there = as_columns(arrived[2 * slots :, :].astype(WIDE), slots)
+        place = slice(k * half, (k + 1) * half)
+        mine, other = cores_rows(part)
+        kept[place, :] = mine
+        sent[place, :] = other.astype(NARROW)
+    sent[slots:, :] = as_lines([high, low, *pieces(total, 2)], width).astype(NARROW)
+
+
+def joined_rows(unit, arrived, kept, local_stats, both, exact, stats):
+    half = exact.shape[0]
+    slots = 2 * half
+    there = as_columns(arrived[slots:, :].astype(WIDE), slots)
     top_here, total_here = local_stats[:, 0:1], local_stats[:, 1:2]
     top_there, total_there = there[:, 0:1] + there[:, 1:2], there[:, 2:3] + there[:, 3:4]
     top = jnp.maximum(top_here, top_there)
     here, there = jnp.exp(top_here - top), jnp.exp(top_there - top)
     total = here * total_here + there * total_there
     stats[...] = as_lanes([top, total])
-    slot_part = kept[:slots, :] * (here / total) + arrived[:slots, :].astype(WIDE) * (there / total)
-    back_part = kept[slots:, :] + arrived[slots : 2 * slots, :].astype(WIDE)
+    scale_here, _ = cores_rows(here / total)
+    scale_there, _ = cores_rows(there / total)
+    slot_part = kept[:half, :] * scale_here + arrived[:half, :].astype(WIDE) * scale_there
+    back_part = kept[half:, :] + arrived[half:slots, :].astype(WIDE)
     exact[...] = slot_part
     narrow = jnp.concatenate([slot_part, back_part]).astype(NARROW)
-    unit = planes * own
-    both[...] = dot(turned(2 * slots, 2, slots // unit, unit), narrow).astype(NARROW)
-
-
-def sorted_copies(planes, arrived, sent):
-    rows = arrived.shape[0]
-    high = sent.shape[1]
-    ordered = dot(turned(rows, rows // 16, 16, 1), arrived[...]).astype(NARROW)
-    part = planes * high
-    ordered = jnp.concatenate(
-        [ordered[j * part : (j + 1) * part] for j in (0, 2, 1, 3)], axis=1
-    )
+    both[...] = dot(turned(slots, 2, half // unit, unit), narrow).astype(NARROW)
+
+
+def sorted_copies(planes, unit, arrived, sent):
+    rows, high = arrived.shape[0], sent.shape[1]
+    ordered = dot(turned(rows, rows // (2 * unit), 2 * unit, 1), arrived[...]).astype(NARROW)
+    ordered = jnp.concatenate([ordered[: rows // 2], ordered[rows // 2 :]], axis=1)
     for k in range(sent.shape[0]):
         first = k // (sent.shape[0] // planes) * high
         sent[k] = ordered[first : first + high]
@@ -190,8 +200,8 @@
         grad_out[e] = dot(acts[mine, :hidden_width], back, 0, 0).astype(NARROW)
 
 
-def joined_results(planes, arrived, both):
-    parts, half = arrived.shape[0] // planes, both.shape[1]
+def joined_results(planes, unit, arrived, both):
+    parts, width = arrived.shape[0] // planes, both.shape[1]
     found = []
     for y in range(planes):
         total = arrived[y * parts].astype(WIDE)
@@ -199,34 +209,30 @@
             total += arrived[y * parts + t].astype(WIDE)
         found.append(total.astype(NARROW))
     found = jnp.concatenate(found)
-    found = jnp.concatenate([found[:, j * half : (j + 1) * half] for j in (0, 2, 1, 3)])
+    found = jnp.concatenate([found[:, :width], found[:, width:]])
     rows = found.shape[0]
-    both[...] = dot(turned(rows, 16, rows // 16, 1), found).astype(NARROW)
-
-
-def dotted_rows(planes, own, arrived, exact, sent, column):
-    slots, half = exact.shape
-    unit = planes * own
-    home = dot(turned(2 * slots, slots // unit, 2, unit), arrived[...])
-    part = jnp.sum(exact[...] * home[slots:], axis=1, keepdims=True)
+    both[...] = dot(turned(rows, 2 * unit, rows // (2 * unit), 1), found).astype(NARROW)
+
+
+def dotted_rows(unit, arrived, exact, sent, column):
+    half, width = exact.shape
+    home = dot(turned(2 * half, half // unit, 2, unit), arrived[...])
+    part = jnp.sum(exact[...] * home[half:], axis=1, keepdims=True)
     column[...] = as_lanes([part])
-    sent[: 2 * slots, :] = home.astype(NARROW)
-    sent[2 * slots :, :] = as_lines(pieces(part, 3), half).astype(NARROW)
-
-
-def softmax_grads(planes, cores, own, *refs):
+    sent[: 2 * half, :] = home.astype(NARROW)
+    sent[2 * half :, :] = as_lines(pieces(part, 3), width).astype(NARROW)
+
+
+def softmax_grads(cores, own, *refs):
     here, column, there, scores, stats, ordered, left, right, router = refs[-9:]
     gathered = refs[:-9]
     slots = scores.shape[0]
+    half = slots // 2
     tokens, cotangent = image_tokens(gathered)
-    lower = lax.axis_index("core") == 0
-    mine, other = here[: 2 * slots, :], there[: 2 * slots, :]
-    joined = jnp.concatenate(
-        [jnp.where(lower, mine, other), jnp.where(lower, other, mine)], axis=1
-    )
-    slot_out, grad_in = joined[:slots], joined[slots:]
-    rest = as_columns(there[2 * slots :, :].astype(WIDE), slots)
-    column_dot = column[:, 0:1] + (rest[:, 0:1] + rest[:, 1:2] + rest[:, 2:3])
+    slot_out = own_first(here[:half, :], there[:half, :])
+    grad_in = own_first(here[half:slots, :], there[half:slots, :])
+    rest = as_columns(there[slots:, :].astype(WIDE), half)
+    column_dot = own_first(column[:, 0:1], rest[:, 0:1] + rest[:, 1:2] + rest[:, 2:3])
     logits = scores[...]
     dispatch = jnp.exp(logits - stats[:, 0:1]) / stats[:, 1:2]
     combine = combine_of(logits)
@@ -236,8 +242,8 @@
     grad_logits = (
         combine * (grad_combine - row_dot) + dispatch * (grad_dispatch - column_dot)
     ).astype(NARROW)
-    by_slot = dot(turned(slots, cores, planes, own), grad_logits).astype(NARROW)
-    by_slot = dot(by_slot, tokens)
+    order = turned(slots, cores, slots // (cores * own), own)
+    by_slot = dot(dot(order, grad_logits).astype(NARROW), tokens)
     count, high, wide = router.shape
     across = by_slot.shape[1] // wide
     for k in range(count):
@@ -321,7 +327,7 @@
     own, hidden_width = w_in.shape[0], w_in.shape[2]
     planes, cores = lax.axis_size("y_hi"), lax.axis_size("core")
     plane, column = lax.axis_size(PLANE), lax.axis_size(COLUMN)
-    half, count = width // 2, images * seq
+    half, count, depth = slots // 2, images * seq, lax.axis_size("z")
     unit = planes * own
     rows = own * images * lax.axis_size(DP)
 
@@ -331,10 +337,10 @@
     )
     gathered = [moved(block, k) for k, block in enumerate(blocks)]
     sent, kept, scores, stats, ordered = local(
-        functools.partial(slot_rows, planes, cores, own),
+        functools.partial(slot_rows, cores, own),
         (
-            shaped((2 * slots + EXTRA, half)),
-            shaped((2 * slots, half), WIDE),
+            shaped((slots + EXTRA, width)),
+            shaped((slots, width), WIDE),
             shaped((slots, count), WIDE),
             shaped((slots, LANES), WIDE),
             shaped((slots, width)),
@@ -344,17 +350,17 @@
         dispatch_weight.T,
     )
     both, exact, stats = local(
-        functools.partial(joined_rows, planes, own),
-        (shaped((2 * slots, half)), shaped((slots, half), WIDE), shaped((slots, LANES), WIDE)),
+        functools.partial(joined_rows, unit),
+        (shaped((slots, width)), shaped((half, width), WIDE), shaped((slots, LANES), WIDE)),
         4 * slots * slots * width,
         from_partner(sent),
         kept,
         stats,
     )
-    arrived = exchanged(both.reshape(column, 2 * unit, half), COLUMN).reshape(2 * slots, half)
-    high = own * lax.axis_size("z")
+    arrived = exchanged(both.reshape(depth, 2 * unit, width), "z").reshape(slots, width)
+    high = own * depth
     (sent,) = local(
-        functools.partial(sorted_copies, planes),
+        functools.partial(sorted_copies, planes, unit),
         (shaped((plane, high, 2 * width)),),
         4 * slots * slots * width,
         arrived,
@@ -377,15 +383,15 @@
         acts,
     )
     (both,) = local(
-        functools.partial(joined_results, planes),
-        (shaped((2 * slots, half)),),
+        functools.partial(joined_results, planes, unit),
+        (shaped((slots, width)),),
         4 * slots * slots * width,
         back,
     )
-    arrived = exchanged(both.reshape(column, 2 * unit, half), COLUMN).reshape(2 * slots, half)
+    arrived = exchanged(both.reshape(depth, 2 * unit, width), "z").reshape(slots, width)
     sent, part = local(
-        functools.partial(dotted_rows, planes, own),
-        (shaped((2 * slots + EXTRA, half)), shaped((slots, LANES), WIDE)),
+        functools.partial(dotted_rows, unit),
+        (shaped((slots + EXTRA, width)), shaped((half, LANES), WIDE)),
         4 * slots * slots * width,
         arrived,
         exact,
@@ -393,7 +399,7 @@
     across = width // LANES
     tall = slots * across // plane
     left, right, router = local(
-        functools.partial(softmax_grads, planes, cores, own),
+        functools.partial(softmax_grads, cores, own),
         (
             shaped((2 * slots, count)),
             shaped((2 * slots, width)),

time: 142 us -> 139 us (0.979)
  blocking collectives: 81.7 us -> 75.1 us
  starting transfers between devices: 26.6 us -> 30.9 us
    all_to_all x5, blocking collectives: 81.7 us -> 75.1 us  [exchanged(): return lax.all_to_all(blocks, axis, split_axis=0, concat_axis=0, tiled=True)]
    ppermute x2, starting transfers between devices: 0.14 us -> 4.21 us  [from_partner(): return lax.ppermute(block, 'core', [(0, 1), (1, 0)])]
  transfers between devices with their start and end apart: 12 -> 12, of which waited for: 8 -> 8; matrix products, arithmetic and copies ran while one was open for 0% -> 0% of each run, Pallas kernels for 3% -> 4%
where the time goes in v5:
time: 139 us
  blocking collectives  75.1 us (54%)
  starting transfers between devices  30.9 us (22%)
  waiting for transfers between devices  18.9 us (14%)
  Pallas kernels  11.8 us (8%)
    all_to_all x5, blocking collectives, exchanged(): return lax.all_to_all(blocks, axis, split_axis=0, concat_axis=0, tiled=True)  75.1 us
    ppermute x8, starting transfers between devices, moved(): return lax.ppermute(block, axes, pairs)  18 us
    ppermute x8, waiting for transfers between devices, moved(): return lax.ppermute(block, axes, pairs)  13 us
    pallas_call x14, Pallas kernels, local(): pl.pallas_call(body, out_shape=outs, in_specs=[pl.BlockSpec(memory_space=...  11.8 us
    all_to_all x2, starting transfers between devices, exchanged(): return lax.all_to_all(blocks, axis, split_axis=0, concat_axis=0, tiled=True)  8.61 us
    ppermute x2, starting transfers between devices, from_partner(): return lax.ppermute(block, 'core', [(0, 1), (1, 0)])  4.21 us
    all_to_all x2, waiting for transfers between devices, exchanged(): return lax.all_to_all(blocks, axis, split_axis=0, concat_axis=0, tiled=True)  3.51 us
  transfers between devices with their start and end apart: 12, of which 8 were waited for; matrix products, arithmetic and copies ran while one was open for 0% of the time, Pallas kernels for 4%

profile of v5, /device:TPU:1, one launch (start us, length us, event | category | flops | bytes accessed | tf_op | source)
XLA Modules:
  0.0 138.8 jit_solution(12179954233130129870)
XLA Ops:
  0.6 0.0 copy-start.2
  0.6 1.4 pad_maximum_fusion.both
  2.0 0.1 shard_map.84
  2.1 4.6 %collective-permute-start = (bf16[144,1024]{1,0:T(8,128)(2,1)S(1)}, bf16[144,1024]{1,0:T(8,128)(2,1)S(1)}, u32[]{:S(2)}, u32[]{:S(2)}) collective-permute-start(bf16[144,1024]{1,0:T(8,128)(2,1)S(1)} %get-tuple-element.29), channel_id=1, source_target_pairs={{0,0},{1,8},{2,2},{3,10},{4,4},{5,12},{6,6},{7,14},{8,1},{9,9},{10... | collective-permute-start | bytes 884744 | tf_op jit(solution)/shard_map/ppermute | solution.py:321
  6.7 1.0 collective-permute-start.1
  7.7 3.9 %collective-permute-start.2 = (bf16[144,1024]{1,0:T(8,128)(2,1)S(1)}, bf16[144,1024]{1,0:T(8,128)(2,1)S(1)}, u32[]{:S(2)}, u32[]{:S(2)}) collective-permute-start(bf16[144,1024]{1,0:T(8,128)(2,1)S(1)} %get-tuple-element.31), channel_id=1, source_target_pairs={{0,4},{1,12},{2,6},{3,14},{4,0},{5,8},{6,2},{7,10},{8,5},{9,13},{1... | collective-permute-start | bytes 884744 | tf_op jit(solution)/shard_map/ppermute | solution.py:321
  11.7 0.0 collective-permute-start.3
  11.7 0.7 collective-permute-done.refs_0_
  12.3 4.6 %collective-permute-done.1.refs_1_ = bf16[144,1024]{1,0:T(8,128)(2,1)S(1)} collective-permute-done((bf16[144,1024]{1,0:T(8,128)(2,1)S(1)}, bf16[144,1024]{1,0:T(8,128)(2,1)S(1)}, u32[]{:S(2)}, u32[]{:S(2)}) %collective-permute-start.1) | collective-permute-done | bytes 294944 | tf_op jit(solution)/shard_map/ppermute | solution.py:321
  16.9 5.1 %collective-permute-done.2.refs_2_ = bf16[144,1024]{1,0:T(8,128)(2,1)S(1)} collective-permute-done((bf16[144,1024]{1,0:T(8,128)(2,1)S(1)}, bf16[144,1024]{1,0:T(8,128)(2,1)S(1)}, u32[]{:S(2)}, u32[]{:S(2)}) %collective-permute-start.2) | collective-permute-done | bytes 294944 | tf_op jit(solution)/shard_map/ppermute | solution.py:321
  22.0 2.7 %collective-permute-done.3.refs_3_ = bf16[144,1024]{1,0:T(8,128)(2,1)S(1)} collective-permute-done((bf16[144,1024]{1,0:T(8,128)(2,1)S(1)}, bf16[144,1024]{1,0:T(8,128)(2,1)S(1)}, u32[]{:S(2)}, u32[]{:S(2)}) %collective-permute-start.3) | collective-permute-done | bytes 294944 | tf_op jit(solution)/shard_map/ppermute | solution.py:321
  24.7 0.0 copy-done.2
  24.7 1.1 shard_map.85
  25.8 0.0 copy-start
  25.8 0.1 collective-permute-start.4
  25.9 1.4 collective-permute-done.4.arrived
  27.3 0.5 shard_map.86
  27.7 16.4 %all_to_all.35 = bf16[8,8,1024]{2,1,0:T(8,128)(2,1)S(1)} all-to-all(bf16[8,8,1024]{2,1,0:T(8,128)(2,1)S(1)} %bitcast.10), channel_id=1, replica_groups=mesh['z'=8,'y_hi'=2,'core'=2,'x'=4,'y_lo'=2] {'z'}, dimensions={0} | all-to-all | bytes 262144 | tf_op jit(solution)/shard_map/all_to_all | solution.py:305
  44.1 0.2 shard_map.87
  44.3 20.1 %all_to_all.36.arrived = bf16[16,16,2048]{2,1,0:T(8,128)(2,1)S(1)} all-to-all(bf16[16,16,2048]{2,1,0:T(8,128)(2,1)S(1)} %shard_map.87), channel_id=1, replica_groups=mesh['z'=8,'y_hi'=2,'core'=2,'x'=4,'y_lo'=2] {'y_hi','x','y_lo'}, dimensions={0} | all-to-all | bytes 2097152 | tf_op jit(solution)/shard_map/all_to_all | solution.py:305
  64.4 0.0 copy-done
  64.5 2.2 %shard_map.88 = (bf16[16,16,2048]{2,1,0:T(8,128)(2,1)S(1)}, bf16[256,1024]{1,0:T(8,128)(2,1)S(1)}) custom-call(bf16[16,16,2048]{2,1,0:T(8,128)(2,1)S(1)} %all_to_all.36.arrived, bf16[2,1024,512]{2,1,0:T(8,128)(2,1)S(1)} %copy-done, bf16[2,512,1024]{2,1,0:T(8,128)(2,1)S(1)} %copy-done.1), custom_call_target="tpu_custom_call" | custom-call | flops 1073741824 | bytes 6815744 | tf_op jit(solution)/shard_map/pallas_call | solution.py:290
  66.6 16.3 %all_to_all.37.arrived = bf16[16,16,2048]{2,1,0:T(8,128)(2,1)S(1)} all-to-all(bf16[16,16,2048]{2,1,0:T(8,128)(2,1)S(1)} %get-tuple-element.37), channel_id=1, replica_groups=mesh['z'=8,'y_hi'=2,'core'=2,'x'=4,'y_lo'=2] {'y_hi','x','y_lo'}, dimensions={0} | all-to-all | bytes 2097152 | tf_op jit(solution)/shard_map/all_to_all | solution.py:305
  83.0 0.3 shard_map.89
  83.3 12.6 %all_to_all.38 = bf16[8,8,1024]{2,1,0:T(8,128)(2,1)S(1)} all-to-all(bf16[8,8,1024]{2,1,0:T(8,128)(2,1)S(1)} %bitcast.7), channel_id=1, replica_groups=mesh['z'=8,'y_hi'=2,'core'=2,'x'=4,'y_lo'=2] {'z'}, dimensions={0} | all-to-all | bytes 262144 | tf_op jit(solution)/shard_map/all_to_all | solution.py:305
  95.9 0.3 shard_map.90
  96.2 4.1 %collective-permute-start.5 = (bf16[72,1024]{1,0:T(8,128)(2,1)S(1)}, bf16[72,1024]{1,0:T(8,128)(2,1)S(1)}, u32[]{:S(2)}, u32[]{:S(2)}) collective-permute-start(bf16[72,1024]{1,0:T(8,128)(2,1)S(1)} %get-tuple-element.39.refs_4_), channel_id=1, source_target_pairs={{0,8},{8,0},{1,9},{9,1},{2,10},{10,2},{3,11},{11,3},{4,12},{12,4},... | collective-permute-start | bytes 442376 | tf_op jit(solution)/shard_map/ppermute | solution.py:309
  100.3 1.0 collective-permute-done.5.refs_6_
  101.3 0.8 shard_map.91
  102.2 9.6 %all_to_all.39.arrived = bf16[16,32,128]{2,1,0:T(8,128)(2,1)S(1)} all-to-all(bf16[16,32,128]{2,1,0:T(8,128)(2,1)S(1)} %get-tuple-element.50), channel_id=1, replica_groups=mesh['z'=8,'y_hi'=2,'core'=2,'x'=4,'y_lo'=2] {'y_hi','x','y_lo'}, dimensions={0} | all-to-all | bytes 262144 | tf_op jit(solution)/shard_map/all_to_all | solution.py:305
  111.8 0.7 shard_map.94
  112.5 5.1 %all-to-all-start.5 = ((bf16[16,32,128]{2,1,0:T(8,128)(2,1)}), bf16[16,32,128]{2,1,0:T(8,128)(2,1)S(1)}, u32[]{:S(2)}, u32[]{:S(2)}) async-start(bf16[16,32,128]{2,1,0:T(8,128)(2,1)} %shard_map.94), calls=%async_computation.5 | async-start | bytes 262144 | tf_op jit(solution)/shard_map/all_to_all | solution.py:305
  117.6 0.3 shard_map.92
  117.9 2.2 %collective-permute-start.6 = (bf16[72,1024]{1,0:T(8,128)(2,1)S(1)}, bf16[72,1024]{1,0:T(8,128)(2,1)S(1)}, u32[]{:S(2)}, u32[]{:S(2)}) collective-permute-start(bf16[72,1024]{1,0:T(8,128)(2,1)S(1)} %get-tuple-element.46), channel_id=1, source_target_pairs={{0,0},{1,8},{2,2},{3,10},{4,4},{5,12},{6,6},{7,14},{8,1},{9,9},{10... | collective-permute-start | bytes 442376 | tf_op jit(solution)/shard_map/ppermute | solution.py:321
  120.2 1.5 %collective-permute-start.7 = (bf16[72,1024]{1,0:T(8,128)(2,1)S(1)}, bf16[72,1024]{1,0:T(8,128)(2,1)S(1)}, u32[]{:S(2)}, u32[]{:S(2)}) collective-permute-start(bf16[72,1024]{1,0:T(8,128)(2,1)S(1)} %get-tuple-element.47), channel_id=1, source_target_pairs={{0,2},{1,10},{2,0},{3,8},{4,6},{5,14},{6,4},{7,12},{8,3},{9,11},{1... | collective-permute-start | bytes 442376 | tf_op jit(solution)/shard_map/ppermute | solution.py:321
  121.6 2.0 %collective-permute-start.8 = (bf16[72,1024]{1,0:T(8,128)(2,1)S(1)}, bf16[72,1024]{1,0:T(8,128)(2,1)S(1)}, u32[]{:S(2)}, u32[]{:S(2)}) collective-permute-start(bf16[72,1024]{1,0:T(8,128)(2,1)S(1)} %get-tuple-element.48), channel_id=1, source_target_pairs={{0,4},{1,12},{2,6},{3,14},{4,0},{5,8},{6,2},{7,10},{8,5},{9,13},{1... | collective-permute-start | bytes 442376 | tf_op jit(solution)/shard_map/ppermute | solution.py:321
  123.6 2.8 %collective-permute-start.9 = (bf16[72,1024]{1,0:T(8,128)(2,1)S(1)}, bf16[72,1024]{1,0:T(8,128)(2,1)S(1)}, u32[]{:S(2)}, u32[]{:S(2)}) collective-permute-start(bf16[72,1024]{1,0:T(8,128)(2,1)S(1)} %get-tuple-element.49), channel_id=1, source_target_pairs={{0,6},{1,14},{2,4},{3,12},{4,2},{5,10},{6,0},{7,8},{8,7},{9,15},{1... | collective-permute-start | bytes 442376 | tf_op jit(solution)/shard_map/ppermute | solution.py:321
  126.5 0.3 all-to-all-done.5.arrived
  126.8 0.7 shard_map.95
  127.5 3.5 %all-to-all-start.6 = ((bf16[16,32,128]{2,1,0:T(8,128)(2,1)}), bf16[16,32,128]{2,1,0:T(8,128)(2,1)S(1)}, u32[]{:S(2)}, u32[]{:S(2)}) async-start(bf16[16,32,128]{2,1,0:T(8,128)(2,1)} %shard_map.95), calls=%async_computation.6 | async-start | bytes 262144 | tf_op jit(solution)/shard_map/all_to_all | solution.py:305
  131.0 3.0 %shard_map.97 = (bf16[2,1024,512]{2,1,0:T(8,128)(2,1)}, bf16[2,512,1024]{2,1,0:T(8,128)(2,1)}) custom-call(bf16[16,16,2048]{2,1,0:T(8,128)(2,1)S(1)} %all_to_all.36.arrived, bf16[256,1024]{1,0:T(8,128)(2,1)S(1)} %get-tuple-element.51.acts), custom_call_target="tpu_custom_call" | custom-call | flops 536870912 | bytes 5767168 | tf_op jit(solution)/shard_map/pallas_call | solution.py:290
  134.0 0.0 collective-permute-done.6.refs_0_
  134.0 0.0 collective-permute-done.7.refs_1_
  134.0 0.0 collective-permute-done.8.refs_2_
  134.0 0.0 collective-permute-done.9.refs_3_
  134.0 0.9 shard_map.93
  134.9 3.2 %all-to-all-done.6.arrived = bf16[16,32,128]{2,1,0:T(8,128)(2,1)S(1)} async-done(((bf16[16,32,128]{2,1,0:T(8,128)(2,1)}), bf16[16,32,128]{2,1,0:T(8,128)(2,1)S(1)}, u32[]{:S(2)}, u32[]{:S(2)}) %all-to-all-start.6) | async-done | bytes 131104 | tf_op jit(solution)/shard_map/all_to_all | solution.py:305
  138.1 0.7 shard_map.96
  (2 shorter events, 0.0 us)
Async XLA Ops:
  0.6 24.0 %copy-start.2 = (bf16[1024,64]{0,1:T(8,128)(2,1)S(1)}, bf16[1024,64]{0,1:T(8,128)(2,1)}, u32[]{:S(2)}) copy-start(bf16[1024,64]{0,1:T(8,128)(2,1)} %param.7) | copy-start | bytes 393220
  2.1 10.2 %collective-permute-start = (bf16[144,1024]{1,0:T(8,128)(2,1)S(1)}, bf16[144,1024]{1,0:T(8,128)(2,1)S(1)}, u32[]{:S(2)}, u32[]{:S(2)}) collective-permute-start(bf16[144,1024]{1,0:T(8,128)(2,1)S(1)} %get-tuple-element.29), channel_id=1, source_target_pairs={{0,0},{1,8},{2,2},{3,10},{4,4},{5,12},{6,6},{7,14},{8,1},{9,9},{10... | collective-permute-start | bytes 884744 | tf_op jit(solution)/shard_map/ppermute | solution.py:321
  6.7 10.2 %collective-permute-start.1 = (bf16[144,1024]{1,0:T(8,128)(2,1)S(1)}, bf16[144,1024]{1,0:T(8,128)(2,1)S(1)}, u32[]{:S(2)}, u32[]{:S(2)}) collective-permute-start(bf16[144,1024]{1,0:T(8,128)(2,1)S(1)} %get-tuple-element.30), channel_id=1, source_target_pairs={{0,2},{1,10},{2,0},{3,8},{4,6},{5,14},{6,4},{7,12},{8,3},{9,11},{1... | collective-permute-start | bytes 884744 | tf_op jit(solution)/shard_map/ppermute | solution.py:321
  7.7 14.2 %collective-permute-start.2 = (bf16[144,1024]{1,0:T(8,128)(2,1)S(1)}, bf16[144,1024]{1,0:T(8,128)(2,1)S(1)}, u32[]{:S(2)}, u32[]{:S(2)}) collective-permute-start(bf16[144,1024]{1,0:T(8,128)(2,1)S(1)} %get-tuple-element.31), channel_id=1, source_target_pairs={{0,4},{1,12},{2,6},{3,14},{4,0},{5,8},{6,2},{7,10},{8,5},{9,13},{1... | collective-permute-start | bytes 884744 | tf_op jit(solution)/shard_map/ppermute | solution.py:321
  11.7 13.0 %collective-permute-start.3 = (bf16[144,1024]{1,0:T(8,128)(2,1)S(1)}, bf16[144,1024]{1,0:T(8,128)(2,1)S(1)}, u32[]{:S(2)}, u32[]{:S(2)}) collective-permute-start(bf16[144,1024]{1,0:T(8,128)(2,1)S(1)} %get-tuple-element.32), channel_id=1, source_target_pairs={{0,6},{1,14},{2,4},{3,12},{4,2},{5,10},{6,0},{7,8},{8,7},{9,15},{1... | collective-permute-start | bytes 884744 | tf_op jit(solution)/shard_map/ppermute | solution.py:321
  24.7 39.8 %copy-start.1 = (bf16[2,512,1024]{2,1,0:T(8,128)(2,1)S(1)}, bf16[2,512,1024]{2,1,0:T(8,128)(2,1)}, u32[]{:S(2)}) copy-start(bf16[2,512,1024]{2,1,0:T(8,128)(2,1)} %w_out.1) | copy-start | bytes 6291460
  25.8 38.7 %copy-start = (bf16[2,1024,512]{2,1,0:T(8,128)(2,1)S(1)}, bf16[2,1024,512]{2,1,0:T(8,128)(2,1)}, u32[]{:S(2)}) copy-start(bf16[2,1024,512]{2,1,0:T(8,128)(2,1)} %w_in.1) | copy-start | bytes 6291460
  25.8 1.5 %collective-permute-start.4 = (bf16[72,1024]{1,0:T(8,128)(2,1)S(1)}, bf16[72,1024]{1,0:T(8,128)(2,1)S(1)}, u32[]{:S(2)}, u32[]{:S(2)}) collective-permute-start(bf16[72,1024]{1,0:T(8,128)(2,1)S(1)} %get-tuple-element.33), channel_id=1, source_target_pairs={{0,8},{8,0},{1,9},{9,1},{2,10},{10,2},{3,11},{11,3},{4,12},{12,4},... | collective-permute-start | bytes 442376 | tf_op jit(solution)/shard_map/ppermute | solution.py:309
  96.2 5.1 %collective-permute-start.5 = (bf16[72,1024]{1,0:T(8,128)(2,1)S(1)}, bf16[72,1024]{1,0:T(8,128)(2,1)S(1)}, u32[]{:S(2)}, u32[]{:S(2)}) collective-permute-start(bf16[72,1024]{1,0:T(8,128)(2,1)S(1)} %get-tuple-element.39.refs_4_), channel_id=1, source_target_pairs={{0,8},{8,0},{1,9},{9,1},{2,10},{10,2},{3,11},{11,3},{4,12},{12,4},... | collective-permute-start | bytes 442376 | tf_op jit(solution)/shard_map/ppermute | solution.py:309
  112.5 14.3 %all-to-all-start.5 = ((bf16[16,32,128]{2,1,0:T(8,128)(2,1)}), bf16[16,32,128]{2,1,0:T(8,128)(2,1)S(1)}, u32[]{:S(2)}, u32[]{:S(2)}) async-start(bf16[16,32,128]{2,1,0:T(8,128)(2,1)} %shard_map.94), calls=%async_computation.5 | async-start | bytes 262144 | tf_op jit(solution)/shard_map/all_to_all | solution.py:305
  117.9 16.1 %collective-permute-start.6 = (bf16[72,1024]{1,0:T(8,128)(2,1)S(1)}, bf16[72,1024]{1,0:T(8,128)(2,1)S(1)}, u32[]{:S(2)}, u32[]{:S(2)}) collective-permute-start(bf16[72,1024]{1,0:T(8,128)(2,1)S(1)} %get-tuple-element.46), channel_id=1, source_target_pairs={{0,0},{1,8},{2,2},{3,10},{4,4},{5,12},{6,6},{7,14},{8,1},{9,9},{10... | collective-permute-start | bytes 442376 | tf_op jit(solution)/shard_map/ppermute | solution.py:321
  120.2 13.9 %collective-permute-start.7 = (bf16[72,1024]{1,0:T(8,128)(2,1)S(1)}, bf16[72,1024]{1,0:T(8,128)(2,1)S(1)}, u32[]{:S(2)}, u32[]{:S(2)}) collective-permute-start(bf16[72,1024]{1,0:T(8,128)(2,1)S(1)} %get-tuple-element.47), channel_id=1, source_target_pairs={{0,2},{1,10},{2,0},{3,8},{4,6},{5,14},{6,4},{7,12},{8,3},{9,11},{1... | collective-permute-start | bytes 442376 | tf_op jit(solution)/shard_map/ppermute | solution.py:321
  121.6 12.4 %collective-permute-start.8 = (bf16[72,1024]{1,0:T(8,128)(2,1)S(1)}, bf16[72,1024]{1,0:T(8,128)(2,1)S(1)}, u32[]{:S(2)}, u32[]{:S(2)}) collective-permute-start(bf16[72,1024]{1,0:T(8,128)(2,1)S(1)} %get-tuple-element.48), channel_id=1, source_target_pairs={{0,4},{1,12},{2,6},{3,14},{4,0},{5,8},{6,2},{7,10},{8,5},{9,13},{1... | collective-permute-start | bytes 442376 | tf_op jit(solution)/shard_map/ppermute | solution.py:321
  123.6 10.4 %collective-permute-start.9 = (bf16[72,1024]{1,0:T(8,128)(2,1)S(1)}, bf16[72,1024]{1,0:T(8,128)(2,1)S(1)}, u32[]{:S(2)}, u32[]{:S(2)}) collective-permute-start(bf16[72,1024]{1,0:T(8,128)(2,1)S(1)} %get-tuple-element.49), channel_id=1, source_target_pairs={{0,6},{1,14},{2,4},{3,12},{4,2},{5,10},{6,0},{7,8},{8,7},{9,15},{1... | collective-permute-start | bytes 442376 | tf_op jit(solution)/shard_map/ppermute | solution.py:321
  127.5 10.6 %all-to-all-start.6 = ((bf16[16,32,128]{2,1,0:T(8,128)(2,1)}), bf16[16,32,128]{2,1,0:T(8,128)(2,1)S(1)}, u32[]{:S(2)}, u32[]{:S(2)}) async-start(bf16[16,32,128]{2,1,0:T(8,128)(2,1)} %shard_map.95), calls=%async_computation.6 | async-start | bytes 262144 | tf_op jit(solution)/shard_map/all_to_all | solution.py:305

commit v6 on v5

--- a/solution.py
+++ b/solution.py
@@ -389,6 +389,7 @@
         back,
     )
     arrived = exchanged(both.reshape(depth, 2 * unit, width), "z").reshape(slots, width)
+    arrived, grad_w_in, grad_w_out = lax.optimization_barrier((arrived, grad_w_in, grad_w_out))
     sent, part = local(
         functools.partial(dotted_rows, unit),
         (shaped((slots + EXTRA, width)), shaped((half, LANES), WIDE)),

time: 139 us -> 140 us (level)
  blocking collectives: 75.1 us -> 62.5 us
  waiting for transfers between devices: 18.9 us -> 26.8 us
  starting transfers between devices: 30.9 us -> 35.8 us
    all_to_all x5 -> x4, blocking collectives: 75.1 us -> 62.5 us  [exchanged(): return lax.all_to_all(blocks, axis, split_axis=0, concat_axis=0, tiled=True)]
    all_to_all x2 -> x3, waiting for transfers between devices: 3.51 us -> 11.4 us  [exchanged(): return lax.all_to_all(blocks, axis, split_axis=0, concat_axis=0, tiled=True)]
    all_to_all x2 -> x3, starting transfers between devices: 8.61 us -> 13.5 us  [exchanged(): return lax.all_to_all(blocks, axis, split_axis=0, concat_axis=0, tiled=True)]
  transfers between devices with their start and end apart: 12 -> 13, of which waited for: 8 -> 9; matrix products, arithmetic and copies ran while one was open for 0% -> 0% of each run, Pallas kernels for 4% -> 4%
where the time goes in v6:
time: 140 us
  blocking collectives  62.5 us (45%)
  starting transfers between devices  35.8 us (26%)
  waiting for transfers between devices  26.8 us (19%)
  Pallas kernels  12.5 us (9%)
    all_to_all x4, blocking collectives, exchanged(): return lax.all_to_all(blocks, axis, split_axis=0, concat_axis=0, tiled=True)  62.5 us
    ppermute x8, starting transfers between devices, moved(): return lax.ppermute(block, axes, pairs)  18 us
    all_to_all x3, starting transfers between devices, exchanged(): return lax.all_to_all(blocks, axis, split_axis=0, concat_axis=0, tiled=True)  13.5 us
    ppermute x8, waiting for transfers between devices, moved(): return lax.ppermute(block, axes, pairs)  13 us
    pallas_call x14, Pallas kernels, local(): pl.pallas_call(body, out_shape=outs, in_specs=[pl.BlockSpec(memory_space=...  12.5 us
    all_to_all x3, waiting for transfers between devices, exchanged(): return lax.all_to_all(blocks, axis, split_axis=0, concat_axis=0, tiled=True)  11.4 us
    ppermute x2, starting transfers between devices, from_partner(): return lax.ppermute(block, 'core', [(0, 1), (1, 0)])  4.21 us
  transfers between devices with their start and end apart: 13, of which 9 were waited for; matrix products, arithmetic and copies ran while one was open for 0% of the time, Pallas kernels for 4%

profile of v6, /device:TPU:1, one launch (start us, length us, event | category | flops | bytes accessed | tf_op | source)
XLA Modules:
  0.0 139.7 jit_solution(923026241823186725)
XLA Ops:
  0.6 0.0 copy-start.2
  0.6 1.4 pad_maximum_fusion.both
  2.0 0.1 shard_map.84
  2.1 4.6 %collective-permute-start = (bf16[144,1024]{1,0:T(8,128)(2,1)S(1)}, bf16[144,1024]{1,0:T(8,128)(2,1)S(1)}, u32[]{:S(2)}, u32[]{:S(2)}) collective-permute-start(bf16[144,1024]{1,0:T(8,128)(2,1)S(1)} %get-tuple-element.32), channel_id=1, source_target_pairs={{0,0},{1,8},{2,2},{3,10},{4,4},{5,12},{6,6},{7,14},{8,1},{9,9},{10... | collective-permute-start | bytes 884744 | tf_op jit(solution)/shard_map/ppermute | solution.py:321
  6.7 1.0 collective-permute-start.1
  7.7 3.9 %collective-permute-start.2 = (bf16[144,1024]{1,0:T(8,128)(2,1)S(1)}, bf16[144,1024]{1,0:T(8,128)(2,1)S(1)}, u32[]{:S(2)}, u32[]{:S(2)}) collective-permute-start(bf16[144,1024]{1,0:T(8,128)(2,1)S(1)} %get-tuple-element.34), channel_id=1, source_target_pairs={{0,4},{1,12},{2,6},{3,14},{4,0},{5,8},{6,2},{7,10},{8,5},{9,13},{1... | collective-permute-start | bytes 884744 | tf_op jit(solution)/shard_map/ppermute | solution.py:321
  11.7 0.0 collective-permute-start.3
  11.7 0.7 collective-permute-done.refs_0_
  12.3 4.6 %collective-permute-done.1.refs_1_ = bf16[144,1024]{1,0:T(8,128)(2,1)S(1)} collective-permute-done((bf16[144,1024]{1,0:T(8,128)(2,1)S(1)}, bf16[144,1024]{1,0:T(8,128)(2,1)S(1)}, u32[]{:S(2)}, u32[]{:S(2)}) %collective-permute-start.1) | collective-permute-done | bytes 294944 | tf_op jit(solution)/shard_map/ppermute | solution.py:321
  16.9 5.1 %collective-permute-done.2.refs_2_ = bf16[144,1024]{1,0:T(8,128)(2,1)S(1)} collective-permute-done((bf16[144,1024]{1,0:T(8,128)(2,1)S(1)}, bf16[144,1024]{1,0:T(8,128)(2,1)S(1)}, u32[]{:S(2)}, u32[]{:S(2)}) %collective-permute-start.2) | collective-permute-done | bytes 294944 | tf_op jit(solution)/shard_map/ppermute | solution.py:321
  22.0 2.7 %collective-permute-done.3.refs_3_ = bf16[144,1024]{1,0:T(8,128)(2,1)S(1)} collective-permute-done((bf16[144,1024]{1,0:T(8,128)(2,1)S(1)}, bf16[144,1024]{1,0:T(8,128)(2,1)S(1)}, u32[]{:S(2)}, u32[]{:S(2)}) %collective-permute-start.3) | collective-permute-done | bytes 294944 | tf_op jit(solution)/shard_map/ppermute | solution.py:321
  24.7 1.1 shard_map.85
  25.8 0.0 copy-start
  25.8 0.1 collective-permute-start.4
  25.9 1.4 collective-permute-done.4.arrived
  27.3 0.5 shard_map.86
  27.7 16.4 %all_to_all.35 = bf16[8,8,1024]{2,1,0:T(8,128)(2,1)S(1)} all-to-all(bf16[8,8,1024]{2,1,0:T(8,128)(2,1)S(1)} %bitcast.9), channel_id=1, replica_groups=mesh['z'=8,'y_hi'=2,'core'=2,'x'=4,'y_lo'=2] {'z'}, dimensions={0} | all-to-all | bytes 262144 | tf_op jit(solution)/shard_map/all_to_all | solution.py:305
  44.1 0.2 shard_map.87
  44.3 20.1 %all_to_all.36.arrived = bf16[16,16,2048]{2,1,0:T(8,128)(2,1)S(1)} all-to-all(bf16[16,16,2048]{2,1,0:T(8,128)(2,1)S(1)} %shard_map.87), channel_id=1, replica_groups=mesh['z'=8,'y_hi'=2,'core'=2,'x'=4,'y_lo'=2] {'y_hi','x','y_lo'}, dimensions={0} | all-to-all | bytes 2097152 | tf_op jit(solution)/shard_map/all_to_all | solution.py:305
  64.4 0.0 copy-done
  64.5 2.2 %shard_map.88 = (bf16[16,16,2048]{2,1,0:T(8,128)(2,1)S(1)}, bf16[256,1024]{1,0:T(8,128)(2,1)S(1)}) custom-call(bf16[16,16,2048]{2,1,0:T(8,128)(2,1)S(1)} %all_to_all.36.arrived, bf16[2,1024,512]{2,1,0:T(8,128)(2,1)S(1)} %copy-done, bf16[2,512,1024]{2,1,0:T(8,128)(2,1)S(1)} %copy-done.1), custom_call_target="tpu_custom_call" | custom-call | flops 1073741824 | bytes 6815744 | tf_op jit(solution)/shard_map/pallas_call | solution.py:290
  66.6 16.3 %all_to_all.37.arrived = bf16[16,16,2048]{2,1,0:T(8,128)(2,1)S(1)} all-to-all(bf16[16,16,2048]{2,1,0:T(8,128)(2,1)S(1)} %get-tuple-element.40), channel_id=1, replica_groups=mesh['z'=8,'y_hi'=2,'core'=2,'x'=4,'y_lo'=2] {'y_hi','x','y_lo'}, dimensions={0} | all-to-all | bytes 2097152 | tf_op jit(solution)/shard_map/all_to_all | solution.py:305
  83.0 0.9 shard_map.89
  83.9 4.9 %all-to-all-start.3 = ((bf16[8,8,1024]{2,1,0:T(8,128)(2,1)}), bf16[8,8,1024]{2,1,0:T(8,128)(2,1)S(1)}, u32[]{:S(2)}, u32[]{:S(2)}) async-start(bf16[8,8,1024]{2,1,0:T(8,128)(2,1)} %bitcast.3), calls=%async_computation.3 | async-start | bytes 262144 | tf_op jit(solution)/shard_map/all_to_all | solution.py:305
  88.8 3.0 %shard_map.90 = (bf16[2,1024,512]{2,1,0:T(8,128)(2,1)}, bf16[2,512,1024]{2,1,0:T(8,128)(2,1)}) custom-call(bf16[16,16,2048]{2,1,0:T(8,128)(2,1)S(1)} %all_to_all.36.arrived, bf16[256,1024]{1,0:T(8,128)(2,1)S(1)} %get-tuple-element.41.acts), custom_call_target="tpu_custom_call" | custom-call | flops 536870912 | bytes 5767168 | tf_op jit(solution)/shard_map/pallas_call | solution.py:290
  91.8 4.9 %all-to-all-done.3 = bf16[8,8,1024]{2,1,0:T(8,128)(2,1)S(1)} async-done(((bf16[8,8,1024]{2,1,0:T(8,128)(2,1)}), bf16[8,8,1024]{2,1,0:T(8,128)(2,1)S(1)}, u32[]{:S(2)}, u32[]{:S(2)}) %all-to-all-start.3) | async-done | bytes 131104 | tf_op jit(solution)/shard_map/all_to_all | solution.py:305
  96.7 0.3 shard_map.91
  97.1 4.1 %collective-permute-start.5 = (bf16[72,1024]{1,0:T(8,128)(2,1)S(1)}, bf16[72,1024]{1,0:T(8,128)(2,1)S(1)}, u32[]{:S(2)}, u32[]{:S(2)}) collective-permute-start(bf16[72,1024]{1,0:T(8,128)(2,1)S(1)} %get-tuple-element.46.refs_4_), channel_id=1, source_target_pairs={{0,8},{8,0},{1,9},{9,1},{2,10},{10,2},{3,11},{11,3},{4,12},{12,4},... | collective-permute-start | bytes 442376 | tf_op jit(solution)/shard_map/ppermute | solution.py:309
  101.2 1.0 collective-permute-done.5.refs_6_
  102.2 0.8 shard_map.92
  103.1 9.6 %all_to_all.38.arrived = bf16[16,32,128]{2,1,0:T(8,128)(2,1)S(1)} all-to-all(bf16[16,32,128]{2,1,0:T(8,128)(2,1)S(1)} %get-tuple-element.57), channel_id=1, replica_groups=mesh['z'=8,'y_hi'=2,'core'=2,'x'=4,'y_lo'=2] {'y_hi','x','y_lo'}, dimensions={0} | all-to-all | bytes 262144 | tf_op jit(solution)/shard_map/all_to_all | solution.py:305
  112.7 0.7 shard_map.95
  113.4 5.1 %all-to-all-start.5 = ((bf16[16,32,128]{2,1,0:T(8,128)(2,1)}), bf16[16,32,128]{2,1,0:T(8,128)(2,1)S(1)}, u32[]{:S(2)}, u32[]{:S(2)}) async-start(bf16[16,32,128]{2,1,0:T(8,128)(2,1)} %shard_map.95), calls=%async_computation.5 | async-start | bytes 262144 | tf_op jit(solution)/shard_map/all_to_all | solution.py:305
  118.5 0.3 shard_map.93
  118.8 2.2 %collective-permute-start.6 = (bf16[72,1024]{1,0:T(8,128)(2,1)S(1)}, bf16[72,1024]{1,0:T(8,128)(2,1)S(1)}, u32[]{:S(2)}, u32[]{:S(2)}) collective-permute-start(bf16[72,1024]{1,0:T(8,128)(2,1)S(1)} %get-tuple-element.53), channel_id=1, source_target_pairs={{0,0},{1,8},{2,2},{3,10},{4,4},{5,12},{6,6},{7,14},{8,1},{9,9},{10... | collective-permute-start | bytes 442376 | tf_op jit(solution)/shard_map/ppermute | solution.py:321
  121.0 1.5 %collective-permute-start.7 = (bf16[72,1024]{1,0:T(8,128)(2,1)S(1)}, bf16[72,1024]{1,0:T(8,128)(2,1)S(1)}, u32[]{:S(2)}, u32[]{:S(2)}) collective-permute-start(bf16[72,1024]{1,0:T(8,128)(2,1)S(1)} %get-tuple-element.54), channel_id=1, source_target_pairs={{0,2},{1,10},{2,0},{3,8},{4,6},{5,14},{6,4},{7,12},{8,3},{9,11},{1... | collective-permute-start | bytes 442376 | tf_op jit(solution)/shard_map/ppermute | solution.py:321
  122.5 2.0 %collective-permute-start.8 = (bf16[72,1024]{1,0:T(8,128)(2,1)S(1)}, bf16[72,1024]{1,0:T(8,128)(2,1)S(1)}, u32[]{:S(2)}, u32[]{:S(2)}) collective-permute-start(bf16[72,1024]{1,0:T(8,128)(2,1)S(1)} %get-tuple-element.55), channel_id=1, source_target_pairs={{0,4},{1,12},{2,6},{3,14},{4,0},{5,8},{6,2},{7,10},{8,5},{9,13},{1... | collective-permute-start | bytes 442376 | tf_op jit(solution)/shard_map/ppermute | solution.py:321
  124.5 2.8 %collective-permute-start.9 = (bf16[72,1024]{1,0:T(8,128)(2,1)S(1)}, bf16[72,1024]{1,0:T(8,128)(2,1)S(1)}, u32[]{:S(2)}, u32[]{:S(2)}) collective-permute-start(bf16[72,1024]{1,0:T(8,128)(2,1)S(1)} %get-tuple-element.56), channel_id=1, source_target_pairs={{0,6},{1,14},{2,4},{3,12},{4,2},{5,10},{6,0},{7,8},{8,7},{9,15},{1... | collective-permute-start | bytes 442376 | tf_op jit(solution)/shard_map/ppermute | solution.py:321
  127.3 0.3 all-to-all-done.5.arrived
  127.7 0.7 shard_map.96
  128.3 3.5 %all-to-all-start.6 = ((bf16[16,32,128]{2,1,0:T(8,128)(2,1)}), bf16[16,32,128]{2,1,0:T(8,128)(2,1)S(1)}, u32[]{:S(2)}, u32[]{:S(2)}) async-start(bf16[16,32,128]{2,1,0:T(8,128)(2,1)} %shard_map.96), calls=%async_computation.6 | async-start | bytes 262144 | tf_op jit(solution)/shard_map/all_to_all | solution.py:305
  131.9 0.0 collective-permute-done.6.refs_0_
  131.9 0.0 collective-permute-done.7.refs_1_
  131.9 0.0 collective-permute-done.8.refs_2_
  131.9 0.0 collective-permute-done.9.refs_3_
  131.9 0.9 shard_map.94
  132.8 6.2 %all-to-all-done.6.arrived = bf16[16,32,128]{2,1,0:T(8,128)(2,1)S(1)} async-done(((bf16[16,32,128]{2,1,0:T(8,128)(2,1)}), bf16[16,32,128]{2,1,0:T(8,128)(2,1)S(1)}, u32[]{:S(2)}, u32[]{:S(2)}) %all-to-all-start.6) | async-done | bytes 131104 | tf_op jit(solution)/shard_map/all_to_all | solution.py:305
  138.9 0.7 shard_map.97
  (3 shorter events, 0.0 us)
Async XLA Ops:
  0.6 24.0 %copy-start.2 = (bf16[1024,64]{0,1:T(8,128)(2,1)S(1)}, bf16[1024,64]{0,1:T(8,128)(2,1)}, u32[]{:S(2)}) copy-start(bf16[1024,64]{0,1:T(8,128)(2,1)} %param.7) | copy-start | bytes 393220
  2.1 10.2 %collective-permute-start = (bf16[144,1024]{1,0:T(8,128)(2,1)S(1)}, bf16[144,1024]{1,0:T(8,128)(2,1)S(1)}, u32[]{:S(2)}, u32[]{:S(2)}) collective-permute-start(bf16[144,1024]{1,0:T(8,128)(2,1)S(1)} %get-tuple-element.32), channel_id=1, source_target_pairs={{0,0},{1,8},{2,2},{3,10},{4,4},{5,12},{6,6},{7,14},{8,1},{9,9},{10... | collective-permute-start | bytes 884744 | tf_op jit(solution)/shard_map/ppermute | solution.py:321
  6.7 10.2 %collective-permute-start.1 = (bf16[144,1024]{1,0:T(8,128)(2,1)S(1)}, bf16[144,1024]{1,0:T(8,128)(2,1)S(1)}, u32[]{:S(2)}, u32[]{:S(2)}) collective-permute-start(bf16[144,1024]{1,0:T(8,128)(2,1)S(1)} %get-tuple-element.33), channel_id=1, source_target_pairs={{0,2},{1,10},{2,0},{3,8},{4,6},{5,14},{6,4},{7,12},{8,3},{9,11},{1... | collective-permute-start | bytes 884744 | tf_op jit(solution)/shard_map/ppermute | solution.py:321
  7.7 14.2 %collective-permute-start.2 = (bf16[144,1024]{1,0:T(8,128)(2,1)S(1)}, bf16[144,1024]{1,0:T(8,128)(2,1)S(1)}, u32[]{:S(2)}, u32[]{:S(2)}) collective-permute-start(bf16[144,1024]{1,0:T(8,128)(2,1)S(1)} %get-tuple-element.34), channel_id=1, source_target_pairs={{0,4},{1,12},{2,6},{3,14},{4,0},{5,8},{6,2},{7,10},{8,5},{9,13},{1... | collective-permute-start | bytes 884744 | tf_op jit(solution)/shard_map/ppermute | solution.py:321
  11.7 13.0 %collective-permute-start.3 = (bf16[144,1024]{1,0:T(8,128)(2,1)S(1)}, bf16[144,1024]{1,0:T(8,128)(2,1)S(1)}, u32[]{:S(2)}, u32[]{:S(2)}) collective-permute-start(bf16[144,1024]{1,0:T(8,128)(2,1)S(1)} %get-tuple-element.35), channel_id=1, source_target_pairs={{0,6},{1,14},{2,4},{3,12},{4,2},{5,10},{6,0},{7,8},{8,7},{9,15},{1... | collective-permute-start | bytes 884744 | tf_op jit(solution)/shard_map/ppermute | solution.py:321
  24.7 39.8 %copy-start.1 = (bf16[2,512,1024]{2,1,0:T(8,128)(2,1)S(1)}, bf16[2,512,1024]{2,1,0:T(8,128)(2,1)}, u32[]{:S(2)}) copy-start(bf16[2,512,1024]{2,1,0:T(8,128)(2,1)} %w_out.1) | copy-start | bytes 6291460
  25.8 38.7 %copy-start = (bf16[2,1024,512]{2,1,0:T(8,128)(2,1)S(1)}, bf16[2,1024,512]{2,1,0:T(8,128)(2,1)}, u32[]{:S(2)}) copy-start(bf16[2,1024,512]{2,1,0:T(8,128)(2,1)} %w_in.1) | copy-start | bytes 6291460
  25.8 1.5 %collective-permute-start.4 = (bf16[72,1024]{1,0:T(8,128)(2,1)S(1)}, bf16[72,1024]{1,0:T(8,128)(2,1)S(1)}, u32[]{:S(2)}, u32[]{:S(2)}) collective-permute-start(bf16[72,1024]{1,0:T(8,128)(2,1)S(1)} %get-tuple-element.36), channel_id=1, source_target_pairs={{0,8},{8,0},{1,9},{9,1},{2,10},{10,2},{3,11},{11,3},{4,12},{12,4},... | collective-permute-start | bytes 442376 | tf_op jit(solution)/shard_map/ppermute | solution.py:309
  83.9 12.8 %all-to-all-start.3 = ((bf16[8,8,1024]{2,1,0:T(8,128)(2,1)}), bf16[8,8,1024]{2,1,0:T(8,128)(2,1)S(1)}, u32[]{:S(2)}, u32[]{:S(2)}) async-start(bf16[8,8,1024]{2,1,0:T(8,128)(2,1)} %bitcast.3), calls=%async_computation.3 | async-start | bytes 262144 | tf_op jit(solution)/shard_map/all_to_all | solution.py:305
  97.1 5.1 %collective-permute-start.5 = (bf16[72,1024]{1,0:T(8,128)(2,1)S(1)}, bf16[72,1024]{1,0:T(8,128)(2,1)S(1)}, u32[]{:S(2)}, u32[]{:S(2)}) collective-permute-start(bf16[72,1024]{1,0:T(8,128)(2,1)S(1)} %get-tuple-element.46.refs_4_), channel_id=1, source_target_pairs={{0,8},{8,0},{1,9},{9,1},{2,10},{10,2},{3,11},{11,3},{4,12},{12,4},... | collective-permute-start | bytes 442376 | tf_op jit(solution)/shard_map/ppermute | solution.py:309
  113.4 14.3 %all-to-all-start.5 = ((bf16[16,32,128]{2,1,0:T(8,128)(2,1)}), bf16[16,32,128]{2,1,0:T(8,128)(2,1)S(1)}, u32[]{:S(2)}, u32[]{:S(2)}) async-start(bf16[16,32,128]{2,1,0:T(8,128)(2,1)} %shard_map.95), calls=%async_computation.5 | async-start | bytes 262144 | tf_op jit(solution)/shard_map/all_to_all | solution.py:305
  118.8 13.1 %collective-permute-start.6 = (bf16[72,1024]{1,0:T(8,128)(2,1)S(1)}, bf16[72,1024]{1,0:T(8,128)(2,1)S(1)}, u32[]{:S(2)}, u32[]{:S(2)}) collective-permute-start(bf16[72,1024]{1,0:T(8,128)(2,1)S(1)} %get-tuple-element.53), channel_id=1, source_target_pairs={{0,0},{1,8},{2,2},{3,10},{4,4},{5,12},{6,6},{7,14},{8,1},{9,9},{10... | collective-permute-start | bytes 442376 | tf_op jit(solution)/shard_map/ppermute | solution.py:321
  121.0 10.8 %collective-permute-start.7 = (bf16[72,1024]{1,0:T(8,128)(2,1)S(1)}, bf16[72,1024]{1,0:T(8,128)(2,1)S(1)}, u32[]{:S(2)}, u32[]{:S(2)}) collective-permute-start(bf16[72,1024]{1,0:T(8,128)(2,1)S(1)} %get-tuple-element.54), channel_id=1, source_target_pairs={{0,2},{1,10},{2,0},{3,8},{4,6},{5,14},{6,4},{7,12},{8,3},{9,11},{1... | collective-permute-start | bytes 442376 | tf_op jit(solution)/shard_map/ppermute | solution.py:321
  122.5 9.4 %collective-permute-start.8 = (bf16[72,1024]{1,0:T(8,128)(2,1)S(1)}, bf16[72,1024]{1,0:T(8,128)(2,1)S(1)}, u32[]{:S(2)}, u32[]{:S(2)}) collective-permute-start(bf16[72,1024]{1,0:T(8,128)(2,1)S(1)} %get-tuple-element.55), channel_id=1, source_target_pairs={{0,4},{1,12},{2,6},{3,14},{4,0},{5,8},{6,2},{7,10},{8,5},{9,13},{1... | collective-permute-start | bytes 442376 | tf_op jit(solution)/shard_map/ppermute | solution.py:321
  124.5 7.4 %collective-permute-start.9 = (bf16[72,1024]{1,0:T(8,128)(2,1)S(1)}, bf16[72,1024]{1,0:T(8,128)(2,1)S(1)}, u32[]{:S(2)}, u32[]{:S(2)}) collective-permute-start(bf16[72,1024]{1,0:T(8,128)(2,1)S(1)} %get-tuple-element.56), channel_id=1, source_target_pairs={{0,6},{1,14},{2,4},{3,12},{4,2},{5,10},{6,0},{7,8},{8,7},{9,15},{1... | collective-permute-start | bytes 442376 | tf_op jit(solution)/shard_map/ppermute | solution.py:321
  128.3 10.6 %all-to-all-start.6 = ((bf16[16,32,128]{2,1,0:T(8,128)(2,1)}), bf16[16,32,128]{2,1,0:T(8,128)(2,1)S(1)}, u32[]{:S(2)}, u32[]{:S(2)}) async-start(bf16[16,32,128]{2,1,0:T(8,128)(2,1)} %shard_map.96), calls=%async_computation.6 | async-start | bytes 262144 | tf_op jit(solution)/shard_map/all_to_all | solution.py:305
